TPU v7x, 8 devices: a whole 2x2x1 slice. The times are simulated.
8 devices in a mesh: dp: 2 (over z, y), ep: 4 (over x, core).
Axes of the slice: x: 2, y: 2, z: 1, core: 2. Of those that a mesh axis runs over, the one named last changes fastest.
Arguments:
- x_tokens: bfloat16 [16, 1024, 1024], P(('dp', 'ep'))
- dy_tokens: bfloat16 [16, 1024, 1024], P(('dp', 'ep'))
- route_idx: int32 [16, 1024, 8], P(('dp', 'ep'))
- norm1_gain: bfloat16 [1024], replicated
- norm2_gain: bfloat16 [1024], replicated
- w_qkv: bfloat16 [1024, 3072], replicated
- w_attn_out: bfloat16 [1024, 1024], replicated
- w_router: bfloat16 [1024, 64], replicated
- w_gate: bfloat16 [64, 1024, 1024], P('ep')
- w_up: bfloat16 [64, 1024, 1024], P('ep')
- w_down: bfloat16 [64, 1024, 1024], P('ep')
Outputs:
- output 1: bfloat16 [16, 1024, 1024], P(('dp', 'ep'))
- output 2: float32 [1024], replicated
- output 3: float32 [1024], replicated
- output 4: float32 [1024, 3072], replicated
- output 5: float32 [1024, 1024], replicated
- output 6: float32 [1024, 64], replicated
- output 7: float32 [64, 1024, 1024], P('ep')
- output 8: float32 [64, 1024, 1024], P('ep')
- output 9: float32 [64, 1024, 1024], P('ep')
All inputs are finite; a program needn't handle non-finite values.
Results may differ from a plain program's by a relative error of at most 0.0178083.
Values are sent between devices in bfloat16 or wider.
A program may use at most 1.5 GiB of HBM per device.

v0:
```python
import jax
import jax.numpy as jnp
from jax import lax
from jax.sharding import PartitionSpec as P

EPS = 1e-6
HEAD_DIM = 128
ROPE_BASE = 10000.0


def capacity_rows(num_tokens, top_k, num_experts):
    return 8 * ((5 * num_tokens * top_k + 32 * num_experts - 1) // (32 * num_experts))


def rms_norm(x_rows, gain_vec):
    x_f32 = x_rows.astype(jnp.float32)
    inv_rms = lax.rsqrt(jnp.mean(x_f32 * x_f32, axis=-1, keepdims=True) + EPS)
    return (x_f32 * inv_rms * gain_vec.astype(jnp.float32)).astype(jnp.bfloat16)


def rms_norm_bwd(x_rows, gain_vec, d_out):
    x_f32 = x_rows.astype(jnp.float32)
    inv_rms = lax.rsqrt(jnp.mean(x_f32 * x_f32, axis=-1, keepdims=True) + EPS)
    d_gain = jnp.sum(d_out * x_f32 * inv_rms, axis=0)
    d_scaled = d_out * gain_vec.astype(jnp.float32)
    d_x = inv_rms * d_scaled - x_f32 * inv_rms ** 3 * jnp.mean(d_scaled * x_f32, axis=-1, keepdims=True)
    return d_x, d_gain


def rope_rotate(head_vals):
    seq_len = head_vals.shape[1]
    half_dim = head_vals.shape[-1] // 2
    inv_freq = ROPE_BASE ** (-jnp.arange(half_dim, dtype=jnp.float32) / half_dim)
    angles = jnp.arange(seq_len, dtype=jnp.float32)[:, None] * inv_freq[None, :]
    cos_b = jnp.cos(angles)[None, :, None, :]
    sin_b = jnp.sin(angles)[None, :, None, :]
    lower_half = head_vals[..., :half_dim]
    upper_half = head_vals[..., half_dim:]
    return jnp.concatenate([lower_half * cos_b - upper_half * sin_b, upper_half * cos_b + lower_half * sin_b], axis=-1)


def attention_core(qkv_rows, num_seqs):
    num_tokens = qkv_rows.shape[0]
    seq_len = num_tokens // num_seqs
    model_width = qkv_rows.shape[1] // 3
    qkv_heads = qkv_rows.reshape(num_seqs, seq_len, 3, model_width // HEAD_DIM, HEAD_DIM)
    query_rot = rope_rotate(qkv_heads[:, :, 0]).astype(jnp.bfloat16)
    key_rot = rope_rotate(qkv_heads[:, :, 1]).astype(jnp.bfloat16)
    value_h = qkv_heads[:, :, 2].astype(jnp.bfloat16)
    scores = jnp.einsum('bqhd,bkhd->bhqk', query_rot, key_rot, preferred_element_type=jnp.float32) * HEAD_DIM ** -0.5
    causal = jnp.arange(seq_len)[:, None] >= jnp.arange(seq_len)[None, :]
    attn_probs = jax.nn.softmax(jnp.where(causal, scores, -1e30), axis=-1).astype(jnp.bfloat16)
    context = jnp.einsum('bhqk,bkhd->bqhd', attn_probs, value_h, preferred_element_type=jnp.float32)
    return context.astype(jnp.bfloat16).reshape(num_tokens, model_width)


def gate_probs(logits, idx_rows):
    probs_all = jax.nn.softmax(logits, axis=-1)
    picked = jnp.take_along_axis(probs_all, idx_rows, axis=1)
    return picked / jnp.sum(picked, axis=1, keepdims=True)


def route_slots(idx_rows, num_experts, capacity):
    num_tokens, top_k = idx_rows.shape
    hit_count = jnp.sum((idx_rows[:, :, None] == jnp.arange(num_experts)[None, None, :]).astype(jnp.int32), axis=1)
    earlier = jnp.cumsum(hit_count, axis=0) - hit_count
    position = jnp.take_along_axis(earlier, idx_rows, axis=1)
    slot_ids = jnp.where(position < capacity, idx_rows * capacity + position, num_experts * capacity)
    source_ids = jnp.full((num_experts * capacity,), num_tokens * top_k, jnp.int32).at[slot_ids.reshape(-1)].set(jnp.arange(num_tokens * top_k, dtype=jnp.int32), mode='drop')
    return slot_ids, source_ids


def take_rows(table, row_ids):
    return jnp.take(table, row_ids, axis=0, mode='fill', fill_value=0)


def dense_forward(x_rows, idx_rows, num_seqs, norm1_gain, norm2_gain, w_qkv, w_attn_out, w_router):
    normed1 = rms_norm(x_rows, norm1_gain)
    qkv_rows = jnp.dot(normed1, w_qkv, preferred_element_type=jnp.float32)
    context, attn_pullback = jax.vjp(lambda qkv_in: attention_core(qkv_in, num_seqs), qkv_rows)
    h_rows = (x_rows.astype(jnp.float32) + jnp.dot(context, w_attn_out, preferred_element_type=jnp.float32)).astype(jnp.bfloat16)
    normed2 = rms_norm(h_rows, norm2_gain)
    logits = jnp.dot(normed2, w_router, preferred_element_type=jnp.float32)
    gate_vals, gate_pullback = jax.vjp(lambda logit_in: gate_probs(logit_in, idx_rows), logits)
    saved_state = (normed1, attn_pullback, context, h_rows, normed2, gate_pullback)
    return normed2, gate_vals, saved_state


def dense_backward(saved_state, x_rows, dy_rows, d_gates, d_normed2_moe, norm1_gain, norm2_gain, w_qkv, w_attn_out, w_router):
    normed1, attn_pullback, context, h_rows, normed2, gate_pullback = saved_state
    d_logits = gate_pullback(d_gates)[0].astype(jnp.bfloat16)
    d_w_router = jnp.einsum('td,te->de', normed2, d_logits, preferred_element_type=jnp.float32)
    d_normed2 = d_normed2_moe + jnp.einsum('te,de->td', d_logits, w_router, preferred_element_type=jnp.float32)
    d_h_part, d_norm2_gain = rms_norm_bwd(h_rows, norm2_gain, d_normed2)
    d_h = (dy_rows.astype(jnp.float32) + d_h_part).astype(jnp.bfloat16)
    d_w_attn_out = jnp.einsum('td,te->de', context, d_h, preferred_element_type=jnp.float32)
    d_context = jnp.einsum('te,de->td', d_h, w_attn_out, preferred_element_type=jnp.float32).astype(jnp.bfloat16)
    d_qkv = attn_pullback(d_context)[0].astype(jnp.bfloat16)
    d_w_qkv = jnp.einsum('td,te->de', normed1, d_qkv, preferred_element_type=jnp.float32)
    d_normed1 = jnp.einsum('te,de->td', d_qkv, w_qkv, preferred_element_type=jnp.float32)
    d_x_part, d_norm1_gain = rms_norm_bwd(x_rows, norm1_gain, d_normed1)
    d_x = (d_h.astype(jnp.float32) + d_x_part).astype(jnp.bfloat16)
    return d_x, (d_norm1_gain, d_norm2_gain, d_w_qkv, d_w_attn_out, d_w_router)


def expert_forward(slot_rows, w_gate, w_up, w_down):
    act_gate = jnp.einsum('slcd,ldf->slcf', slot_rows, w_gate, preferred_element_type=jnp.float32)
    act_up = jnp.einsum('slcd,ldf->slcf', slot_rows, w_up, preferred_element_type=jnp.float32)
    hidden = (jax.nn.silu(act_gate) * act_up).astype(jnp.bfloat16)
    expert_out = jnp.einsum('slcf,lfd->slcd', hidden, w_down, preferred_element_type=jnp.float32).astype(jnp.bfloat16)
    return act_gate, act_up, hidden, expert_out


def expert_backward(slot_rows, act_gate, act_up, hidden, d_expert_out, w_gate, w_up, w_down):
    d_hidden = jnp.einsum('slcd,lfd->slcf', d_expert_out, w_down, preferred_element_type=jnp.float32)
    d_w_down = jnp.einsum('slcf,slcd->lfd', hidden, d_expert_out, preferred_element_type=jnp.float32)
    sigmoid_g = jax.nn.sigmoid(act_gate)
    d_act_up = (d_hidden * act_gate * sigmoid_g).astype(jnp.bfloat16)
    d_act_gate = (d_hidden * act_up * sigmoid_g * (1.0 + act_gate * (1.0 - sigmoid_g))).astype(jnp.bfloat16)
    d_w_gate = jnp.einsum('slcd,slcf->ldf', slot_rows, d_act_gate, preferred_element_type=jnp.float32)
    d_w_up = jnp.einsum('slcd,slcf->ldf', slot_rows, d_act_up, preferred_element_type=jnp.float32)
    d_slot_rows = jnp.einsum('slcf,ldf->slcd', d_act_gate, w_gate, preferred_element_type=jnp.float32) + jnp.einsum('slcf,ldf->slcd', d_act_up, w_up, preferred_element_type=jnp.float32)
    return d_slot_rows.astype(jnp.bfloat16), d_w_gate, d_w_up, d_w_down


def solution(mesh):
    ep_size = mesh.shape['ep']
    tok_spec = P(('dp', 'ep'), None, None)
    rep_spec = P()
    exp_spec = P('ep', None, None)

    def local_step(x_tokens, dy_tokens, route_idx, norm1_gain, norm2_gain, w_qkv, w_attn_out, w_router, w_gate, w_up, w_down):
        num_seqs, seq_len, model_width = x_tokens.shape
        num_tokens = num_seqs * seq_len
        top_k = route_idx.shape[-1]
        local_experts = w_gate.shape[0]
        num_experts = local_experts * ep_size
        capacity = capacity_rows(num_tokens, top_k, num_experts)
        x_rows = x_tokens.reshape(num_tokens, model_width)
        dy_rows = dy_tokens.reshape(num_tokens, model_width)
        idx_rows = route_idx.reshape(num_tokens, top_k)
        normed2, gate_vals, saved_state = dense_forward(x_rows, idx_rows, num_seqs, norm1_gain, norm2_gain, w_qkv, w_attn_out, w_router)
        slot_ids, source_ids = route_slots(idx_rows, num_experts, capacity)
        slot_flat = slot_ids.reshape(-1)
        token_of_slot = source_ids // top_k
        send_rows = take_rows(normed2, token_of_slot).reshape(ep_size, local_experts, capacity, model_width)
        recv_rows = lax.all_to_all(send_rows, 'ep', 0, 0, tiled=True)
        act_gate, act_up, hidden, expert_out = expert_forward(recv_rows, w_gate, w_up, w_down)
        back_rows = lax.all_to_all(expert_out, 'ep', 0, 0, tiled=True).reshape(num_experts * capacity, model_width)
        choice_rows = take_rows(back_rows, slot_flat).reshape(num_tokens, top_k, model_width)
        d_gates = jnp.einsum('td,tkd->tk', dy_rows, choice_rows, preferred_element_type=jnp.float32)
        gate_of_slot = take_rows(gate_vals.reshape(-1), source_ids)
        d_slot_out = (take_rows(dy_rows, token_of_slot).astype(jnp.float32) * gate_of_slot[:, None]).astype(jnp.bfloat16)
        d_expert_out = lax.all_to_all(d_slot_out.reshape(ep_size, local_experts, capacity, model_width), 'ep', 0, 0, tiled=True)
        d_recv, d_w_gate, d_w_up, d_w_down = expert_backward(recv_rows, act_gate, act_up, hidden, d_expert_out, w_gate, w_up, w_down)
        d_back = lax.all_to_all(d_recv, 'ep', 0, 0, tiled=True).reshape(num_experts * capacity, model_width)
        d_normed2_moe = jnp.sum(take_rows(d_back, slot_flat).reshape(num_tokens, top_k, model_width).astype(jnp.float32), axis=1)
        d_x, dense_grads = dense_backward(saved_state, x_rows, dy_rows, d_gates, d_normed2_moe, norm1_gain, norm2_gain, w_qkv, w_attn_out, w_router)
        expert_grads = lax.psum((d_w_gate, d_w_up, d_w_down), 'dp')
        dense_grads = lax.psum(dense_grads, ('dp', 'ep'))
        return (d_x.reshape(x_tokens.shape),) + tuple(dense_grads) + tuple(expert_grads)

    return jax.shard_map(local_step, mesh=mesh,
                         in_specs=(tok_spec, tok_spec, tok_spec, rep_spec, rep_spec, rep_spec, rep_spec, rep_spec, exp_spec, exp_spec, exp_spec),
                         out_specs=(tok_spec, rep_spec, rep_spec, rep_spec, rep_spec, rep_spec, exp_spec, exp_spec, exp_spec),
                         check_vma=False)
```

profile of v0, /device:TPU:0, one launch (start us, length us, event | category | flops | bytes accessed | tf_op | source)
XLA Modules:
  0.0 8238.1 jit_solution(15348178965740361997)
XLA Ops:
  51.7 130.6 %gather_fusion.1 = s32[16384]{0:T(1024)S(1)} fusion(s32[2048,64]{0,1:T(8,128)S(1)} %fusion.105, s32[16384]{0:T(1024)S(1)} %reshape.431), kind=kCustom, calls=%fused_computation.5 | custom fusion | bytes 262144 | tf_op jit(solution)/shard_map/jit(take_along_axis)/gather | solution.py:67
  182.6 60.6 scatter_custom_fusion
  291.2 34.8 fusion.134
  326.0 32.8 divide_convert_fusion
  396.6 130.6 %gather_fusion.2 = f32[16384]{0:T(1024)S(1)} fusion(f32[2048,64]{0,1:T(8,128)S(1)} %fusion.108, s32[16384]{0:T(1024)S(1)} %copy-done.4), kind=kCustom, calls=%fused_computation.6 | custom fusion | bytes 262144 | tf_op jit(solution)/shard_map/jvp(jit(take_along_axis))/gather | solution.py:59
  533.9 113.0 %gather_fusion = f32[20480]{0:T(1024)S(1)} fusion(f32[16384]{0:T(1024)S(1)} %select_divide_fusion, s32[20480]{0:T(1024)S(1)} %copy-done.35), kind=kCustom, calls=%fused_computation.4 | custom fusion | bytes 245760 | tf_op jit(solution)/shard_map/jit(_take)/gather | solution.py:74
  647.0 102.3 %gather_fusion.3 = bf16[20480,1024]{1,0:T(8,128)(2,1)} fusion(bf16[2048,1024]{1,0:T(8,128)(2,1)} %bitcast.258, s32[20480]{0:T(1024)S(1)} %copy-done.31), kind=kCustom, calls=%fused_computation.clone | custom fusion | bytes 83968000 | tf_op jit(solution)/shard_map/jit(_take)/gather | solution.py:74
  788.8 102.3 %gather_fusion.4 = bf16[20480,1024]{1,0:T(8,128)(2,1)} fusion(bf16[2048,1024]{1,0:T(8,128)(2,1)} %copy-done.1, s32[20480]{0:T(1024)S(1)} %copy-done.31), kind=kCustom, calls=%fused_computation.2.clone | custom fusion | bytes 83968000 | tf_op jit(solution)/shard_map/jit(_take)/gather | solution.py:74
  919.3 322.7 %all-to-all-done = bf16[4,16,320,1024]{3,2,1,0:T(8,128)(2,1)} async-done(((bf16[4,16,320,1024]{3,2,1,0:T(8,128)(2,1)}), bf16[4,16,320,1024]{3,2,1,0:T(8,128)(2,1)}, u32[]{:S(2)}, u32[]{:S(2)}) %all-to-all-start) | async-done | bytes 41943072 | tf_op jit(solution)/shard_map/all_to_all | solution.py:154
  1253.4 65.0 fusion.30
  1318.4 387.4 %all-to-all-done.1 = bf16[4,16,320,1024]{3,2,1,0:T(8,128)(2,1)} async-done(((bf16[4,16,320,1024]{3,2,1,0:T(8,128)(2,1)}), bf16[4,16,320,1024]{3,2,1,0:T(8,128)(2,1)}, u32[]{:S(2)}, u32[]{:S(2)}) %all-to-all-start.1) | async-done | bytes 41943072 | tf_op jit(solution)/shard_map/all_to_all | solution.py:147
  1705.7 74.4 fusion.26
  1780.1 134.5 %fusion.10 = (bf16[4,16,320,1024]{3,2,0,1:T(8,128)(2,1)}, bf16[4,16,320,1024]{3,2,0,1:T(8,128)(2,1)}, bf16[4,16,320,1024]{3,2,0,1:T(8,128)(2,1)}) fusion(f32[16,4,320,1024]{3,2,1,0:T(8,128)} %fusion.26, f32[16,4,320,1024]{3,2,1,0:T(8,128)} %fusion.30, bf16[16,1024,1024]{2,1,0:T(8,128)(2,1)} %param.23, bf16[4,16,320,1024]{3,2,1,0:T(8,128)(2,1)} %all-to-all-done.1), kind=kOutput, calls=%fused_computation.25 | convolution fusion | flops 43285217280 | bytes 369098752 | tf_op jit(solution)/shard_map/slcd,ldf->slcf/dot_general | solution.py:107
  1914.7 57.5 convert_bitcast_fusion
  2011.6 75.6 fusion.32
  2087.1 75.8 fusion.19
  2191.1 272.8 %all-to-all-done.3 = bf16[4,16,320,1024]{3,2,1,0:T(8,128)(2,1)} async-done(((bf16[4,16,320,1024]{3,2,1,0:T(8,128)(2,1)}), bf16[4,16,320,1024]{3,2,1,0:T(8,128)(2,1)}, u32[]{:S(2)}, u32[]{:S(2)}) %all-to-all-start.3) | async-done | bytes 41943072 | tf_op jit(solution)/shard_map/all_to_all | solution.py:149
  2480.1 301.1 %gather_fusion.6 = bf16[16384,1024]{1,0:T(8,128)(2,1)} fusion(bf16[20480,1024]{1,0:T(8,128)(2,1)} %bitcast.36, s32[16384]{0:T(1024)S(1)} %broadcast_clamp_fusion.1), kind=kCustom, calls=%fused_computation.3.clone | custom fusion | bytes 67174400 | tf_op jit(solution)/shard_map/jit(_take)/gather | solution.py:74
  2812.6 86.6 %scatter_custom_fusion.1 = f32[131072]{0:T(1024)} fusion(s32[16384]{0:T(1024)S(1)} %reshape.451, f32[16384]{0:T(1024)S(1)} %reshape.453, f32[]{:T(128)} %constant.67.clone.1), kind=kCustom, calls=%fused_computation.160 | custom fusion | flops 16384 | bytes 524292
  2927.5 300.5 %gather_fusion.5 = bf16[16384,1024]{1,0:T(8,128)(2,1)} fusion(bf16[20480,1024]{1,0:T(8,128)(2,1)} %bitcast.32, s32[16384]{0:T(1024)S(1)} %broadcast_clamp_fusion.1), kind=kCustom, calls=%fused_computation.1.clone | custom fusion | bytes 67174400 | tf_op jit(solution)/shard_map/jit(_take)/gather | solution.py:74
  3308.2 37.2 fusion.17
  3345.4 37.9 convert_bitcast_fusion.1
  3383.3 37.1 convert_bitcast_fusion.2
  3507.3 59.9 fusion.54
  3567.4 60.0 fusion.48
  3627.4 60.2 fusion.51
  3742.3 1430.8 %all-reduce.18.cloned.1.call-done = f32[16,1024,1024]{2,1,0:T(8,128)} async-done(((f32[16,1024,1024]{2,1,0:T(8,128)}), f32[16,1024,1024]{2,1,0:T(8,128)}) %all-reduce.18.cloned.1.call-update) | async-done | bytes 67108880 | tf_op jit(solution)/shard_map/psum | solution.py:159
  5173.1 1456.7 %all-reduce.14.cloned.1.call-done = f32[16,1024,1024]{2,1,0:T(8,128)} async-done(((f32[16,1024,1024]{2,1,0:T(8,128)}), f32[16,1024,1024]{2,1,0:T(8,128)}) %all-reduce.14.cloned.1.call-update) | async-done | bytes 67108880 | tf_op jit(solution)/shard_map/psum | solution.py:159
  6629.8 1456.6 %all-reduce.16.cloned.1.call-done = f32[16,1024,1024]{2,1,0:T(8,128)} async-done(((f32[16,1024,1024]{2,1,0:T(8,128)}), f32[16,1024,1024]{2,1,0:T(8,128)}) %all-reduce.16.cloned.1.call-update) | async-done | bytes 67108880 | tf_op jit(solution)/shard_map/psum | solution.py:159
  8100.3 43.6 copy.235
  8143.9 43.6 copy.236
  8187.5 43.6 copy.237
  (240 shorter events, 595.0 us)
Async XLA Ops:
  7.2 375.8 %copy-start = (bf16[1024,1024]{1,0:T(8,128)(2,1)S(1)}, bf16[1024,1024]{1,0:T(8,128)(2,1)}, u32[]{:S(2)}) copy-start(bf16[1024,1024]{1,0:T(8,128)(2,1)} %param.21) | copy-start | bytes 6291460
  14.8 167.5 %copy-start.3 = (s32[16384]{0:T(1024)}, s32[16384]{0:T(1024)S(1)}, u32[]{:S(2)}) copy-start(s32[16384]{0:T(1024)S(1)} %reshape.431) | copy-start | bytes 196612
  51.7 130.6 %copy-start.36 = (s32[16384,1]{0,1:T(1,128)S(1)}, s32[16384,1]{0,1:T(1,128)}, u32[]{:S(2)}) copy-start(s32[16384,1]{0,1:T(1,128)} %reshape.373) | copy-start | bytes 196612
  51.7 192.9 %copy-start.60 = (bf16[1024]{0:T(1024)(128)(2,1)S(1)}, bf16[1024]{0:T(1024)(128)(2,1)}, u32[]{:S(2)}) copy-start(bf16[1024]{0:T(1024)(128)(2,1)} %param.18) | copy-start | bytes 6148
  182.3 74.6 copy-start.7
  396.5 133.7 %copy-start.23 = (s32[2,1024,8]{1,2,0:T(8,128)S(1)}, s32[2,1024,8]{1,2,0:T(8,128)}, u32[]{:S(2)}) copy-start(s32[2,1024,8]{1,2,0:T(8,128)} %param.17) | copy-start | bytes 196612
  396.5 137.3 %copy-start.27 = (s32[16384]{0:T(1024)S(1)}, s32[16384]{0:T(1024)}, u32[]{:S(2)}) copy-start(s32[16384]{0:T(1024)} %reshape.377) | copy-start | bytes 196612
  396.5 137.3 %copy-start.35 = (s32[20480]{0:T(1024)S(1)}, s32[20480]{0:T(1024)}, u32[]{:S(2)}) copy-start(s32[20480]{0:T(1024)} %get-tuple-element.37) | copy-start | bytes 245764
  527.1 119.8 %copy-start.9 = (f32[16384]{0:T(1024)}, f32[16384]{0:T(1024)S(1)}, u32[]{:S(2)}) copy-start(f32[16384]{0:T(1024)S(1)} %gather_fusion.2) | copy-start | bytes 196612
  533.9 113.1 %copy-start.26 = (s32[20480]{0:T(1024)S(1)}, s32[20480]{0:T(1024)}, u32[]{:S(2)}) copy-start(s32[20480]{0:T(1024)} %copy-done.25) | copy-start | bytes 245764
  533.9 113.1 %copy-start.31 = (s32[20480]{0:T(1024)S(1)}, s32[20480]{0:T(1024)}, u32[]{:S(2)}) copy-start(s32[20480]{0:T(1024)} %get-tuple-element.38) | copy-start | bytes 245764
  647.0 102.3 %copy-start.42 = (pred[20480]{0:T(1024)(128)(4,1)S(1)}, pred[20480]{0:T(1024)(128)(4,1)}, u32[]{:S(2)}) copy-start(pred[20480]{0:T(1024)(128)(4,1)} %compare_and_fusion) | copy-start | bytes 61444
  777.6 464.4 %all-to-all-start = ((bf16[4,16,320,1024]{3,2,1,0:T(8,128)(2,1)}), bf16[4,16,320,1024]{3,2,1,0:T(8,128)(2,1)}, u32[]{:S(2)}, u32[]{:S(2)}) async-start(bf16[4,16,320,1024]{3,2,1,0:T(8,128)(2,1)} %bitcast.261), calls=%async_computation | async-start | bytes 83886080 | tf_op jit(solution)/shard_map/all_to_all | solution.py:154
  1242.0 463.7 %all-to-all-start.1 = ((bf16[4,16,320,1024]{3,2,1,0:T(8,128)(2,1)}), bf16[4,16,320,1024]{3,2,1,0:T(8,128)(2,1)}, u32[]{:S(2)}, u32[]{:S(2)}) async-start(bf16[4,16,320,1024]{3,2,1,0:T(8,128)(2,1)} %bitcast.260), calls=%async_computation.1 | async-start | bytes 83886080 | tf_op jit(solution)/shard_map/all_to_all | solution.py:147
  2000.1 463.8 %all-to-all-start.3 = ((bf16[4,16,320,1024]{3,2,1,0:T(8,128)(2,1)}), bf16[4,16,320,1024]{3,2,1,0:T(8,128)(2,1)}, u32[]{:S(2)}, u32[]{:S(2)}) async-start(bf16[4,16,320,1024]{3,2,1,0:T(8,128)(2,1)} %copy.147), calls=%async_computation.3 | async-start | bytes 83886080 | tf_op jit(solution)/shard_map/all_to_all | solution.py:149
  2191.0 284.2 %copy-start.10 = (f32[16384]{0:T(1024)S(1)}, f32[16384]{0:T(1024)}, u32[]{:S(2)}) copy-start(f32[16384]{0:T(1024)} %copy-done.9) | copy-start | bytes 196612
  2191.0 285.1 %copy-start.32 = (s32[2048,8,1]{0,1,2:T(8,128)S(1)}, s32[2048,8,1]{0,1,2:T(8,128)}, u32[]{:S(2)}) copy-start(s32[2048,8,1]{0,1,2:T(8,128)} %get-tuple-element.39) | copy-start | bytes 196612
  2191.0 287.4 %copy-start.51 = (f32[2,1024]{1,0:T(2,128)S(1)}, f32[2,1024]{1,0:T(2,128)}, u32[]{:S(2)}) copy-start(f32[2,1024]{1,0:T(2,128)} %copy-done.50) | copy-start | bytes 24580
  2191.0 287.4 %copy-start.46 = (f32[2048]{0:T(1024)S(1)}, f32[2048]{0:T(1024)}, u32[]{:S(2)}) copy-start(f32[2048]{0:T(1024)} %copy-done.45) | copy-start | bytes 24580
  2191.0 288.9 %copy-start.8 = (s32[16384]{0:T(1024)S(1)}, s32[16384]{0:T(1024)}, u32[]{:S(2)}) copy-start(s32[16384]{0:T(1024)} %copy-done.7) | copy-start | bytes 196612
  2191.1 288.9 %copy-start.28 = (s32[16384]{0:T(1024)S(1)}, s32[16384]{0:T(1024)}, u32[]{:S(2)}) copy-start(s32[16384]{0:T(1024)} %reshape.377) | copy-start | bytes 196612
  2463.9 463.6 %all-to-all-start.2 = ((bf16[4,16,320,1024]{3,2,1,0:T(8,128)(2,1)}), bf16[4,16,320,1024]{3,2,1,0:T(8,128)(2,1)}, u32[]{:S(2)}, u32[]{:S(2)}) async-start(bf16[4,16,320,1024]{3,2,1,0:T(8,128)(2,1)} %copy.145), calls=%async_computation.2 | async-start | bytes 83886080 | tf_op jit(solution)/shard_map/all_to_all | solution.py:156
  2475.1 1267.1 %all-reduce.20.cloned.1.call-start = ((), (), s32[]{:S(2)}) async-start(), calls=%async_computation.7 | async-start | bytes 34078720 | tf_op jit(solution)/shard_map/psum | solution.py:160
  2480.0 301.1 %copy-start.52 = (pred[16384]{0:T(1024)(128)(4,1)}, pred[16384]{0:T(1024)(128)(4,1)S(1)}, u32[]{:S(2)}) copy-start(pred[16384]{0:T(1024)(128)(4,1)S(1)} %compare_and_fusion.1) | copy-start | bytes 49156
  2781.1 119.2 %copy-start.13 = (f32[2048,64]{0,1:T(8,128)S(1)}, f32[2048,64]{0,1:T(8,128)}, u32[]{:S(2)}) copy-start(f32[2048,64]{0,1:T(8,128)} %copy-done.12) | copy-start | bytes 1572868
  2781.2 119.2 %copy-start.41 = (f32[2048]{0:T(1024)S(1)}, f32[2048]{0:T(1024)}, u32[]{:S(2)}) copy-start(f32[2048]{0:T(1024)} %copy-done.40) | copy-start | bytes 24580
  2927.5 300.5 %copy-start.53 = (pred[16384]{0:T(1024)(128)(4,1)S(1)}, pred[16384]{0:T(1024)(128)(4,1)}, u32[]{:S(2)}) copy-start(pred[16384]{0:T(1024)(128)(4,1)} %copy-done.52) | copy-start | bytes 49156
  3308.2 37.2 copy-start.30
  3308.2 37.2 copy-start.39
  3507.3 1665.8 %all-reduce.18.cloned.1.call-start = ((), (), s32[]{:S(2)}) async-start(), calls=%async_computation.6 | async-start | bytes 134217728 | tf_op jit(solution)/shard_map/psum | solution.py:159
  3567.3 3062.5 %all-reduce.14.cloned.1.call-start = ((), (), s32[]{:S(2)}) async-start(), calls=%async_computation.4 | async-start | bytes 134217728 | tf_op jit(solution)/shard_map/psum | solution.py:159
  3627.3 4459.1 %all-reduce.16.cloned.1.call-start = ((), (), s32[]{:S(2)}) async-start(), calls=%async_computation.5 | async-start | bytes 134217728 | tf_op jit(solution)/shard_map/psum | solution.py:159
  (39 other events, 430.1 us)
Sparse Core Ops, SparseCore 0:
  3507.4 210.3 all-reduce.19
  3720.9 1452.1 all-reduce.17
  5176.1 1453.6 all-reduce.13
  6632.7 1453.6 all-reduce.15
where the time goes:
time: 8260 us; the launch traced here: 8240 us
  waiting for transfers between devices  5350 us (65%)
  local copies, waits for them, and re-layouts  1540 us (19%)
  matrix products  961 us (12%)
  other arithmetic  302 us (4%)
    psum x3, waiting for transfers between devices, local_step(): expert_grads = lax.psum((d_w_gate, d_w_up, d_w_down), 'dp')  4340 us
    gather x5, local copies, waits for them, and re-layouts, take_rows(): return jnp.take(table, row_ids, axis=0, mode='fill', fill_value=0)  919 us
    all_to_all x1, waiting for transfers between devices, local_step(): recv_rows = lax.all_to_all(send_rows, 'ep', 0, 0, tiled=True)  387 us
    all_to_all x1, waiting for transfers between devices, local_step(): lax.all_to_all(d_slot_out.reshape(ep_size, local_experts, capacity, model...  323 us
    all_to_all x1, waiting for transfers between devices, local_step(): lax.all_to_all(expert_out, 'ep', 0, 0, tiled=True)  273 us
  transfers between devices with their start and end apart: 8, of which 7 were waited for; matrix products, arithmetic and copies ran while one was open for 12% of the time, Pallas kernels for 0%

commit v1 on v0

v1 whole, which is shorter than its diff:
```python
import functools

import jax
import jax.numpy as jnp
from jax import lax
from jax.experimental import pallas as pl
from jax.experimental.pallas import tpu as pltpu
from jax.sharding import PartitionSpec as P

EPS = 1e-6
HEAD_DIM = 128
ROPE_BASE = 10000.0
TOK_BLOCK = 256
WIN = 64
ALIGN = 16
VMEM_MAX = 64 * 1024 * 1024 - 65536


def capacity_rows(num_tokens, top_k, num_experts):
    return 8 * ((5 * num_tokens * top_k + 32 * num_experts - 1) // (32 * num_experts))


def rms_norm(x_rows, gain_vec):
    x_f32 = x_rows.astype(jnp.float32)
    inv_rms = lax.rsqrt(jnp.mean(x_f32 * x_f32, axis=-1, keepdims=True) + EPS)
    return (x_f32 * inv_rms * gain_vec.astype(jnp.float32)).astype(jnp.bfloat16)


def rms_norm_bwd(x_rows, gain_vec, d_out):
    x_f32 = x_rows.astype(jnp.float32)
    inv_rms = lax.rsqrt(jnp.mean(x_f32 * x_f32, axis=-1, keepdims=True) + EPS)
    d_gain = jnp.sum(d_out * x_f32 * inv_rms, axis=0)
    d_scaled = d_out * gain_vec.astype(jnp.float32)
    d_x = inv_rms * d_scaled - x_f32 * inv_rms ** 3 * jnp.mean(d_scaled * x_f32, axis=-1, keepdims=True)
    return d_x, d_gain


def rope_rotate(head_vals):
    seq_len = head_vals.shape[1]
    half_dim = head_vals.shape[-1] // 2
    inv_freq = ROPE_BASE ** (-jnp.arange(half_dim, dtype=jnp.float32) / half_dim)
    angles = jnp.arange(seq_len, dtype=jnp.float32)[:, None] * inv_freq[None, :]
    cos_b = jnp.cos(angles)[None, :, None, :]
    sin_b = jnp.sin(angles)[None, :, None, :]
    lower_half = head_vals[..., :half_dim]
    upper_half = head_vals[..., half_dim:]
    return jnp.concatenate([lower_half * cos_b - upper_half * sin_b, upper_half * cos_b + lower_half * sin_b], axis=-1)


def attention_core(qkv_rows, num_seqs):
    num_tokens = qkv_rows.shape[0]
    seq_len = num_tokens // num_seqs
    model_width = qkv_rows.shape[1] // 3
    qkv_heads = qkv_rows.reshape(num_seqs, seq_len, 3, model_width // HEAD_DIM, HEAD_DIM)
    query_rot = rope_rotate(qkv_heads[:, :, 0]).astype(jnp.bfloat16)
    key_rot = rope_rotate(qkv_heads[:, :, 1]).astype(jnp.bfloat16)
    value_h = qkv_heads[:, :, 2].astype(jnp.bfloat16)
    scores = jnp.einsum('bqhd,bkhd->bhqk', query_rot, key_rot, preferred_element_type=jnp.float32) * HEAD_DIM ** -0.5
    causal = jnp.arange(seq_len)[:, None] >= jnp.arange(seq_len)[None, :]
    attn_probs = jax.nn.softmax(jnp.where(causal, scores, -1e30), axis=-1).astype(jnp.bfloat16)
    context = jnp.einsum('bhqk,bkhd->bqhd', attn_probs, value_h, preferred_element_type=jnp.float32)
    return context.astype(jnp.bfloat16).reshape(num_tokens, model_width)


def choice_mask(idx_rows, num_experts):
    return (idx_rows[:, :, None] == jnp.arange(num_experts, dtype=jnp.int32)[None, None, :])


def gate_forward(logits, idx_rows, num_experts):
    probs_all = jax.nn.softmax(logits, axis=-1)
    hits = jnp.sum(choice_mask(idx_rows, num_experts).astype(jnp.float32), axis=1)
    picked_sum = jnp.sum(probs_all * hits, axis=1, keepdims=True)
    return probs_all, hits, picked_sum


def gate_backward(probs_all, hits, picked_sum, d_gate_dense):
    gates = probs_all * hits / picked_sum
    d_probs = hits * (d_gate_dense - jnp.sum(d_gate_dense * gates, axis=1, keepdims=True)) / picked_sum
    return probs_all * (d_probs - jnp.sum(d_probs * probs_all, axis=1, keepdims=True))


def slot_positions(idx_t, first_expert, local_experts, capacity):
    num_dev, _, num_tokens = idx_t.shape
    experts = first_expert + jnp.arange(local_experts, dtype=jnp.int32)
    hits = jnp.sum((idx_t[:, None, :, :] == experts[None, :, None, None]).astype(jnp.float32), axis=2)
    blocks = num_tokens // TOK_BLOCK
    hit_blk = hits.reshape(num_dev, local_experts, blocks, TOK_BLOCK)
    upto = (jnp.arange(TOK_BLOCK)[:, None] <= jnp.arange(TOK_BLOCK)[None, :]).astype(jnp.bfloat16)
    within = jnp.einsum('debt,tu->debu', hit_blk.astype(jnp.bfloat16), upto, preferred_element_type=jnp.float32)
    totals = jnp.sum(hit_blk, axis=-1)
    strict = (jnp.arange(blocks)[:, None] < jnp.arange(blocks)[None, :])
    before = jnp.sum(jnp.where(strict[None, None], totals[:, :, :, None], 0.0), axis=2)
    position = (within + before[..., None] - 1.0).astype(jnp.int32)
    slot_of = jnp.where((hit_blk > 0) & (position < capacity), position, -1).reshape(num_dev, local_experts, num_tokens)
    begin = jnp.minimum(before.astype(jnp.int32), capacity)
    end = jnp.minimum((before + totals).astype(jnp.int32), capacity)
    win_start = jnp.minimum(begin // ALIGN * ALIGN, capacity - WIN)
    win_count = jnp.maximum((end - win_start + WIN - 1) // WIN, 1)
    return slot_of, win_start.reshape(-1), win_count.reshape(-1)


def gather_kernel(base_ref, start_ref, count_ref, x_ref, dy_ref, slot_ref, gate_ref, s_ref, dyr_ref, g_ref, *, experts, blocks, capacity, group):
    dev, blk = pl.program_id(0), pl.program_id(1)

    @pl.when(blk == 0)
    def _():
        s_ref[...] = jnp.zeros_like(s_ref)
        dyr_ref[...] = jnp.zeros_like(dyr_ref)
        g_ref[...] = jnp.zeros_like(g_ref)

    row_iota = lax.broadcasted_iota(jnp.int32, (WIN, TOK_BLOCK), 0)

    def window(e, first, floor):
        slot_row = slot_ref[0, e:e + 1, :]
        hit = (slot_row == row_iota + first) & (slot_row >= floor)
        gate_col = jnp.sum(jnp.where(hit, gate_ref[0, e:e + 1, :], 0.0), axis=1, keepdims=True)
        return jnp.where(hit, 1.0, 0.0).astype(jnp.bfloat16), gate_col

    def deposit(e, first, s_rows, dy_rows, gate_col):
        rows = pl.ds(pl.multiple_of(first, ALIGN), WIN)
        s_ref[e, 0, rows, :] += s_rows.astype(jnp.bfloat16)
        dyr_ref[e, 0, rows, :] += dy_rows.astype(jnp.bfloat16)
        g_ref[e, 0, rows, :] += gate_col

    for e0 in range(0, experts, group):
        firsts = [start_ref[(dev * experts + e0 + i) * blocks + blk] for i in range(group)]
        parts = [window(e0 + i, firsts[i], 0) for i in range(group)]
        pick = jnp.concatenate([p[0] for p in parts], axis=0)
        s_all = jnp.dot(pick, x_ref[...], preferred_element_type=jnp.float32)
        dy_all = jnp.dot(pick, dy_ref[...], preferred_element_type=jnp.float32)
        for i in range(group):
            rows = slice(i * WIN, (i + 1) * WIN)
            deposit(e0 + i, firsts[i], s_all[rows], dy_all[rows], parts[i][1])

    for e in range(experts):
        at = (dev * experts + e) * blocks + blk
        count = count_ref[at]

        @pl.when(count > 1)
        def _():
            def extra(w, carry):
                floor = start_ref[at] + w * WIN
                first = jnp.minimum(floor, capacity - WIN)
                pick, gate_col = window(e, first, floor)
                s_rows = jnp.dot(pick, x_ref[...], preferred_element_type=jnp.float32)
                dy_rows = jnp.dot(pick, dy_ref[...], preferred_element_type=jnp.float32)
                deposit(e, first, s_rows, dy_rows, gate_col)
                return carry
            lax.fori_loop(1, count, extra, 0)


def gather_slots(base_dev, win_start, win_count, x_all, dy_all, slot_of, gate_of, capacity):
    num_dev, experts, num_tokens = slot_of.shape
    width = x_all.shape[1]
    blocks = num_tokens // TOK_BLOCK

    def table_map(d, b, base_ref, start_ref, count_ref):
        return (lax.rem(d + base_ref[0], num_dev) * blocks + b, 0)

    def route_map(d, b, *_):
        return (d, 0, b)

    def out_map(d, b, *_):
        return (0, d, 0, 0)

    return pl.pallas_call(
        functools.partial(gather_kernel, experts=experts, blocks=blocks, capacity=capacity, group=4),
        out_shape=[jax.ShapeDtypeStruct((experts, num_dev, capacity, width), jnp.bfloat16),
                   jax.ShapeDtypeStruct((experts, num_dev, capacity, width), jnp.bfloat16),
                   jax.ShapeDtypeStruct((experts, num_dev, capacity, 1), jnp.float32)],
        grid_spec=pltpu.PrefetchScalarGridSpec(
            num_scalar_prefetch=3, grid=(num_dev, blocks),
            in_specs=[pl.BlockSpec((TOK_BLOCK, width), table_map), pl.BlockSpec((TOK_BLOCK, width), table_map),
                      pl.BlockSpec((1, experts, TOK_BLOCK), route_map), pl.BlockSpec((1, experts, TOK_BLOCK), route_map)],
            out_specs=[pl.BlockSpec((experts, 1, capacity, width), out_map), pl.BlockSpec((experts, 1, capacity, width), out_map),
                       pl.BlockSpec((experts, 1, capacity, 1), out_map)]),
        compiler_params=pltpu.CompilerParams(vmem_limit_bytes=VMEM_MAX, dimension_semantics=('arbitrary', 'arbitrary')),
        cost_estimate=pl.CostEstimate(flops=4 * num_dev * blocks * experts * WIN * TOK_BLOCK * width,
                                      bytes_accessed=4 * num_dev * (num_tokens + experts * capacity) * width, transcendentals=0),
        name='gather_slots',
    )(base_dev, win_start, win_count, x_all, dy_all, slot_of, gate_of)


def combine_kernel(start_ref, count_ref, ds_ref, dg_ref, slot_ref, out_ref, dgt_ref, *, experts, blocks, capacity, group):
    dev, blk = pl.program_id(0), pl.program_id(1)
    row_iota = lax.broadcasted_iota(jnp.int32, (WIN, TOK_BLOCK), 0)

    def window(e, first, floor):
        slot_row = slot_ref[0, e:e + 1, :]
        hit = (slot_row == row_iota + first) & (slot_row >= floor)
        rows = pl.ds(pl.multiple_of(first, ALIGN), WIN)
        gate_row = jnp.sum(jnp.where(hit, dg_ref[e, 0, rows, :], 0.0), axis=0, keepdims=True)
        return jnp.where(hit, 1.0, 0.0).astype(jnp.bfloat16), ds_ref[e, 0, rows, :], gate_row

    def spread(pick, rows):
        return lax.dot_general(pick, rows, (((0,), (0,)), ((), ())), preferred_element_type=jnp.float32)

    for e0 in range(0, experts, group):
        parts = [window(e0 + i, start_ref[(dev * experts + e0 + i) * blocks + blk], 0) for i in range(group)]
        total = spread(jnp.concatenate([p[0] for p in parts], axis=0), jnp.concatenate([p[1] for p in parts], axis=0))
        out_ref[...] = total if e0 == 0 else out_ref[...] + total
        for i in range(group):
            dgt_ref[0, e0 + i:e0 + i + 1, :] = parts[i][2]

    for e in range(experts):
        at = (dev * experts + e) * blocks + blk
        count = count_ref[at]

        @pl.when(count > 1)
        def _():
            def extra(w, carry):
                floor = start_ref[at] + w * WIN
                pick, rows, gate_row = window(e, jnp.minimum(floor, capacity - WIN), floor)
                out_ref[...] += spread(pick, rows)
                dgt_ref[0, e:e + 1, :] += gate_row
                return carry
            lax.fori_loop(1, count, extra, 0)


def combine_slots(win_start, win_count, d_slots, d_gate_slots, slot_of, num_dev):
    experts, _, capacity, width = d_slots.shape
    num_tokens = slot_of.shape[-1]
    blocks = num_tokens // TOK_BLOCK
    return pl.pallas_call(
        functools.partial(combine_kernel, experts=experts, blocks=blocks, capacity=capacity, group=4),
        out_shape=[jax.ShapeDtypeStruct((num_dev * num_tokens, width), jnp.float32),
                   jax.ShapeDtypeStruct((num_dev, experts, num_tokens), jnp.float32)],
        grid_spec=pltpu.PrefetchScalarGridSpec(
            num_scalar_prefetch=2, grid=(num_dev, blocks),
            in_specs=[pl.BlockSpec((experts, 1, capacity, width), lambda d, b, *_: (0, d, 0, 0)),
                      pl.BlockSpec((experts, 1, capacity, 1), lambda d, b, *_: (0, d, 0, 0)),
                      pl.BlockSpec((1, experts, TOK_BLOCK), lambda d, b, *_: (d, 0, b))],
            out_specs=[pl.BlockSpec((TOK_BLOCK, width), lambda d, b, *_: (d * blocks + b, 0)),
                       pl.BlockSpec((1, experts, TOK_BLOCK), lambda d, b, *_: (d, 0, b))]),
        compiler_params=pltpu.CompilerParams(vmem_limit_bytes=VMEM_MAX, dimension_semantics=('arbitrary', 'arbitrary')),
        cost_estimate=pl.CostEstimate(flops=2 * num_dev * blocks * experts * WIN * TOK_BLOCK * width,
                                      bytes_accessed=2 * num_dev * (2 * num_tokens + experts * capacity) * width, transcendentals=0),
        name='combine_slots',
    )(win_start, win_count, d_slots, d_gate_slots, slot_of)


def dense_backward(saved_state, x_rows, dy_rows, d_logits, d_normed2_moe, norm1_gain, norm2_gain, w_qkv, w_attn_out, w_router):
    normed1, attn_pullback, context, h_rows, normed2 = saved_state
    d_w_router = jnp.einsum('td,te->de', normed2, d_logits, preferred_element_type=jnp.float32)
    d_normed2 = d_normed2_moe + jnp.einsum('te,de->td', d_logits, w_router, preferred_element_type=jnp.float32)
    d_h_part, d_norm2_gain = rms_norm_bwd(h_rows, norm2_gain, d_normed2)
    d_h = (dy_rows.astype(jnp.float32) + d_h_part).astype(jnp.bfloat16)
    d_w_attn_out = jnp.einsum('td,te->de', context, d_h, preferred_element_type=jnp.float32)
    d_context = jnp.einsum('te,de->td', d_h, w_attn_out, preferred_element_type=jnp.float32).astype(jnp.bfloat16)
    d_qkv = attn_pullback(d_context)[0].astype(jnp.bfloat16)
    d_w_qkv = jnp.einsum('td,te->de', normed1, d_qkv, preferred_element_type=jnp.float32)
    d_normed1 = jnp.einsum('te,de->td', d_qkv, w_qkv, preferred_element_type=jnp.float32)
    d_x_part, d_norm1_gain = rms_norm_bwd(x_rows, norm1_gain, d_normed1)
    d_x = (d_h.astype(jnp.float32) + d_x_part).astype(jnp.bfloat16)
    return d_x, (d_norm1_gain, d_norm2_gain, d_w_qkv, d_w_attn_out, d_w_router)


def solution(mesh):
    ep_size, dp_size = mesh.shape['ep'], mesh.shape['dp']
    num_dev = ep_size * dp_size
    tok_spec = P(('dp', 'ep'), None, None)
    rep_spec = P()
    exp_spec = P('ep', None, None)

    def local_step(x_tokens, dy_tokens, route_idx, norm1_gain, norm2_gain, w_qkv, w_attn_out, w_router, w_gate, w_up, w_down):
        num_seqs, seq_len, model_width = x_tokens.shape
        num_tokens = num_seqs * seq_len
        top_k = route_idx.shape[-1]
        local_experts = w_gate.shape[0]
        num_experts = local_experts * ep_size
        capacity = capacity_rows(num_tokens, top_k, num_experts)
        x_rows = x_tokens.reshape(num_tokens, model_width)
        dy_rows = dy_tokens.reshape(num_tokens, model_width)
        idx_rows = route_idx.reshape(num_tokens, top_k)
        base = lax.axis_index('dp') * ep_size

        dy_all = lax.all_gather(dy_rows, ('dp', 'ep'), axis=0, tiled=True)
        idx_all = lax.all_gather(idx_rows.T, ('dp', 'ep'), axis=0)
        idx_all = jnp.roll(idx_all, -base, axis=0)
        slot_of, win_start, win_count = slot_positions(idx_all, lax.axis_index('ep') * local_experts, local_experts, capacity)

        normed1 = rms_norm(x_rows, norm1_gain)
        qkv_rows = jnp.dot(normed1, w_qkv, preferred_element_type=jnp.float32)
        context, attn_pullback = jax.vjp(lambda qkv_in: attention_core(qkv_in, num_seqs), qkv_rows)
        h_rows = (x_rows.astype(jnp.float32) + jnp.dot(context, w_attn_out, preferred_element_type=jnp.float32)).astype(jnp.bfloat16)
        normed2 = rms_norm(h_rows, norm2_gain)
        x_all = lax.all_gather(normed2, ('dp', 'ep'), axis=0, tiled=True)
        logits = jnp.dot(normed2, w_router, preferred_element_type=jnp.float32)
        probs_all, hits, picked_sum = gate_forward(logits, idx_rows, num_experts)
        gate_t = jnp.transpose(probs_all * hits / picked_sum)
        gate_all = lax.all_gather(gate_t.reshape(ep_size, local_experts, num_tokens), ('dp', 'ep'), axis=0)
        gate_of = jnp.roll(lax.dynamic_index_in_dim(gate_all, lax.axis_index('ep'), axis=1, keepdims=False), -base, axis=0)

        slots, dy_slots, gate_slots = gather_slots(base[None], win_start, win_count, x_all, dy_all, slot_of, gate_of, capacity)
        own = ep_size * capacity
        rows_of = lambda a: a.reshape(local_experts, num_dev * capacity, a.shape[-1])
        s_all, dy_s, g_s = rows_of(slots), rows_of(dy_slots), rows_of(gate_slots)
        mm = functools.partial(jnp.einsum, preferred_element_type=jnp.float32)
        act_gate = mm('ecd,edf->ecf', s_all, w_gate)
        act_up = mm('ecd,edf->ecf', s_all, w_up)
        hidden = (jax.nn.silu(act_gate) * act_up).astype(jnp.bfloat16)
        expert_out = mm('ecf,efd->ecd', hidden[:, :own], w_down).astype(jnp.bfloat16)
        d_gate_slots = jnp.sum(dy_s[:, :own].astype(jnp.float32) * expert_out.astype(jnp.float32), axis=-1, keepdims=True)
        d_out = (dy_s.astype(jnp.float32) * g_s).astype(jnp.bfloat16)
        d_hidden = mm('ecd,efd->ecf', d_out, w_down)
        sigmoid_g = jax.nn.sigmoid(act_gate)
        d_act_up = (d_hidden * act_gate * sigmoid_g).astype(jnp.bfloat16)
        d_act_gate = (d_hidden * act_up * sigmoid_g * (1.0 + act_gate * (1.0 - sigmoid_g))).astype(jnp.bfloat16)
        d_slots = (mm('ecf,edf->ecd', d_act_gate[:, :own], w_gate) + mm('ecf,edf->ecd', d_act_up[:, :own], w_up)).astype(jnp.bfloat16)
        d_tok, d_gate_t = combine_slots(win_start, win_count, d_slots.reshape(local_experts, ep_size, capacity, model_width),
                                        d_gate_slots.reshape(local_experts, ep_size, capacity, 1), slot_of, ep_size)
        d_normed2_moe = lax.psum_scatter(d_tok, 'ep', scatter_dimension=0, tiled=True)
        d_gate_dense = jnp.transpose(lax.all_to_all(d_gate_t, 'ep', 0, 0, tiled=True).reshape(num_experts, num_tokens))
        d_w_down = mm('ecf,ecd->efd', hidden, d_out)
        d_w_gate = mm('ecd,ecf->edf', s_all, d_act_gate)
        d_w_up = mm('ecd,ecf->edf', s_all, d_act_up)

        d_logits = gate_backward(probs_all, hits, picked_sum, d_gate_dense).astype(jnp.bfloat16)
        saved_state = (normed1, attn_pullback, context, h_rows, normed2)
        d_x, dense_grads = dense_backward(saved_state, x_rows, dy_rows, d_logits, d_normed2_moe, norm1_gain, norm2_gain, w_qkv, w_attn_out, w_router)
        dense_grads = lax.psum(dense_grads, ('dp', 'ep'))
        return (d_x.reshape(x_tokens.shape),) + tuple(dense_grads) + (d_w_gate, d_w_up, d_w_down)

    return jax.shard_map(local_step, mesh=mesh,
                         in_specs=(tok_spec, tok_spec, tok_spec, rep_spec, rep_spec, rep_spec, rep_spec, rep_spec, exp_spec, exp_spec, exp_spec),
                         out_specs=(tok_spec, rep_spec, rep_spec, rep_spec, rep_spec, rep_spec, exp_spec, exp_spec, exp_spec),
                         check_vma=False)
```

time: 8260 us -> 2260 us (0.27)
  waiting for transfers between devices: 5350 us -> 374 us
  local copies, waits for them, and re-layouts: 1540 us -> 192 us
  matrix products: 961 us -> 1300 us
  Pallas kernels: 0 us -> 215 us
  other arithmetic: 302 us -> 112 us
    psum x3 -> x0, waiting for transfers between devices: 4340 us -> none  [local_step(): expert_grads = lax.psum((d_w_gate, d_w_up, d_w_down), 'dp')]
    gather x14 -> x0, local copies, waits for them, and re-layouts: 1190 us -> none  [the longest x5 919 us: take_rows(): return jnp.take(table, row_ids, axis=0, mode='fill', fill_value=0)]
    all_to_all x4 -> x1, waiting for transfers between devices: 1010 us -> 0.01 us  [local_step(): lax.all_to_all(d_gate_t, 'ep', 0, 0, tiled=True)]
    dot_general x13, matrix products: 716 us -> 1050 us  [the longest x1 254 us: local_step(): act_up = mm('ecd,edf->ecf', s_all, w_up)]
    all_gather x0 -> x3, waiting for transfers between devices: none -> 323 us  [the longest x1 157 us: local_step(): dy_all = lax.all_gather(dy_rows, ('dp', 'ep'), axis=0, tiled=True)]
    pallas_call x0 -> x2, Pallas kernels: none -> 215 us  [the longest x1 163 us: gather_slots(): pl.pallas_call(functools.partial(gather_kernel, experts=experts, blocks=b...]
    unnamed x5 -> x1, other arithmetic: 88.7 us -> 0.61 us
  transfers between devices with their start and end apart: 8 -> 6, of which waited for: 7 -> 4; matrix products, arithmetic and copies ran while one was open for 12% -> 17% of each run, Pallas kernels for 0% -> 0%
where the time goes in v1:
time: 2260 us; the launch traced here: 2250 us
  matrix products  1300 us (58%)
  waiting for transfers between devices  374 us (17%)
  Pallas kernels  215 us (10%)
  local copies, waits for them, and re-layouts  192 us (8%)
  other arithmetic  112 us (5%)
  blocking collectives  43.3 us (2%)
    dot_general x1, matrix products, local_step(): act_up = mm('ecd,edf->ecf', s_all, w_up)  254 us
    pallas_call x1, Pallas kernels, gather_slots(): pl.pallas_call(functools.partial(gather_kernel, experts=experts, blocks=b...  163 us
    all_gather x1, waiting for transfers between devices, local_step(): dy_all = lax.all_gather(dy_rows, ('dp', 'ep'), axis=0, tiled=True)  157 us
    all_gather x1, waiting for transfers between devices, local_step(): x_all = lax.all_gather(normed2, ('dp', 'ep'), axis=0, tiled=True)  155 us
    dot_general x1, matrix products, local_step(): d_hidden = mm('ecd,efd->ecf', d_out, w_down)  126 us
    dot_general x1, matrix products, local_step(): act_gate = mm('ecd,edf->ecf', s_all, w_gate)  122 us
    dot_general x1, matrix products, local_step(): d_w_down = mm('ecf,ecd->efd', hidden, d_out)  113 us
    dot_general x1, matrix products, local_step(): d_w_gate = mm('ecd,ecf->edf', s_all, d_act_gate)  108 us
  transfers between devices with their start and end apart: 6, of which 4 were waited for; matrix products, arithmetic and copies ran while one was open for 17% of the time, Pallas kernels for 0%

profile of v1, /device:TPU:0, one launch (start us, length us, event | category | flops | bytes accessed | tf_op | source)
XLA Modules:
  0.0 2253.5 jit_solution(7682995545679974675)
XLA Ops:
  25.5 16.4 fusion.48
  54.5 34.7 %fusion.97 = (f32[2,8,1024]{2,1,0:T(8,128)S(1)}, f32[2,8,1024,1024]{2,3,1,0:T(8,128)}) fusion(pred[1024,1024]{0,1:T(8,128)(4,1)S(1)} %iota_compare_fusion.1, bf16[2,1024,8,64]{1,3,2,0:T(8,128)(2,1)} %get-tuple-element.43, bf16[2,1024,8,64]{1,3,2,0:T(8,128)(2,1)} %get-tuple-element.44, bf16[2,1024,8,64]{1,3,2,0:T(8,128)(2,1)} %get-tuple-element.38, ...), kind=kOutput, calls=%fused_computation.175 | convolution fusion | flops 4378854400 | bytes 76611584 | tf_op jit(solution)/shard_map/jvp()/sub | solution.py:60
  89.2 32.8 %divide_convert_fusion = bf16[2,8,1024,1024]{2,3,1,0:T(8,128)(2,1)} fusion(f32[2,8,1024,1024]{2,3,1,0:T(8,128)} %get-tuple-element.56, f32[2,8,1024]{2,1,0:T(8,128)S(1)} %get-tuple-element.55), kind=kLoop, calls=%fused_computation.18 | loop fusion | flops 33554432 | bytes 100728832 | tf_op jit(solution)/shard_map/jvp()/convert_element_type | solution.py:60
  122.0 17.5 convert_bitcast_fusion.4
  166.8 17.4 all-gather
  204.0 154.6 %all-gather.5.cloned.1.call-done.x_ref = bf16[16384,1024]{1,0:T(8,128)(2,1)} async-done(((bf16[2048,1024]{1,0:T(8,128)(2,1)}), bf16[16384,1024]{1,0:T(8,128)(2,1)}) %all-gather.5.cloned.1.call-update) | async-done | bytes 33554448 | tf_op jit(solution)/shard_map/all_gather | solution.py:287
  358.6 157.1 %all-gather.7.cloned.1.call-done.dy_ref = bf16[16384,1024]{1,0:T(8,128)(2,1)} async-done(((bf16[2048,1024]{1,0:T(8,128)(2,1)}), bf16[16384,1024]{1,0:T(8,128)(2,1)}) %all-gather.7.cloned.1.call-update) | async-done | bytes 33554448 | tf_op jit(solution)/shard_map/all_gather | solution.py:277
  515.7 162.8 %gather_slots.1 = (bf16[16,8,320,1024]{3,2,1,0:T(8,128)(2,1)}, bf16[16,8,320,1024]{3,2,1,0:T(8,128)(2,1)}, f32[16,8,320,1]{3,2,1,0:T(8,128)}) custom-call(s32[1]{0:T(128)} %bitcast.14.base_ref, s32[1024]{0:T(1024)} %get-tuple-element.52.start_ref, s32[1024]{0:T(1024)} %get-tuple-element.51.count_ref, bf16[16384,1024]{1,0:T(8,128)(2,1)} %all-gather.5.cloned.1.call-done.x_ref, ...), custom_call_target="tpu_custom_call" | custom-call | flops 68719476736 | bytes 234881024 | tf_op jit(solution)/shard_map/gather_slots/pallas_call | solution.py:166
  688.8 28.2 %slice.54 = bf16[16,1280,1024]{2,1,0:T(8,128)(2,1)} slice(bf16[16,2560,1024]{2,1,0:T(8,128)(2,1)} %bitcast.21), slice={[0:16], [0:1280], [0:1024]} | slice | bytes 83886080 | tf_op jit(solution)/shard_map/slice | solution.py:303
  717.0 58.1 %copy.117 = bf16[16,1280,1024]{1,2,0:T(8,128)(2,1)} copy(bf16[16,1280,1024]{2,1,0:T(8,128)(2,1)} %slice.54) | data formatting | bytes 83886080
  775.1 126.5 %fusion.2 = f32[16,2560,1024]{2,1,0:T(8,128)} fusion(bf16[16,1024,1024]{2,1,0:T(8,128)(2,1)} %param.21, bf16[16,2560,1024]{2,1,0:T(8,128)(2,1)} %bitcast.21, f32[16,2560]{1,0:T(8,128)S(1)} %mul.502), kind=kOutput, calls=%fused_computation.11 | convolution fusion | flops 86025175040 | bytes 285376512 | tf_op jit(solution)/shard_map/ecd,efd->ecf/dot_general | solution.py:305
  901.5 121.8 %fusion.99 = f32[16,2560,1024]{2,1,0:T(8,128)} fusion(bf16[16,2560,1024]{2,1,0:T(8,128)(2,1)} %bitcast.22, bf16[16,1024,1024]{2,1,0:T(8,128)(2,1)} %param.19), kind=kOutput, calls=%fused_computation.177 | convolution fusion | flops 85899345920 | bytes 285212672 | tf_op jit(solution)/shard_map/ecd,edf->ecf/dot_general | solution.py:299
  1023.4 253.8 %multiply_convert_fusion = (bf16[16,2560,1024]{2,1,0:T(8,128)(2,1)}, bf16[16,2560,1024]{2,1,0:T(8,128)(2,1)}, bf16[16,2560,1024]{2,1,0:T(8,128)(2,1)}) fusion(f32[16,2560,1024]{2,1,0:T(8,128)} %fusion.99, f32[16,2560,1024]{2,1,0:T(8,128)} %fusion.2, bf16[16,2560,1024]{2,1,0:T(8,128)(2,1)} %bitcast.22, bf16[16,1024,1024]{2,1,0:T(8,128)(2,1)} %param.20), kind=kOutput, calls=%fused_computation.1 | convolution fusion | flops 86570434560 | bytes 704643072 | tf_op jit(solution)/shard_map/ecd,edf->ecf/dot_general | solution.py:300
  1277.1 51.4 %multiply_reduce_fusion = f32[16,1280]{1,0:T(8,128)S(1)} fusion(bf16[16,1280,1024]{1,2,0:T(8,128)(2,1)} %copy.117, bf16[16,1024,1024]{2,1,0:T(8,128)(2,1)} %param.21, bf16[16,2560,1024]{2,1,0:T(8,128)(2,1)} %get-tuple-element.28), kind=kOutput, calls=%fused_computation.8 | convolution fusion | flops 43054510080 | bytes 117522432 | tf_op jit(solution)/shard_map/ecf,efd->ecd/dot_general | solution.py:302
  1328.5 15.3 reshape_broadcast_in_dim.4.dg_ref
  1343.8 65.0 %fusion.13 = f32[16,1280,1024]{2,1,0:T(8,128)} fusion(bf16[16,1024,1024]{2,1,0:T(8,128)(2,1)} %param.19, bf16[16,2560,1024]{2,1,0:T(8,128)(2,1)} %get-tuple-element.29), kind=kOutput, calls=%fused_computation.25 | convolution fusion | flops 42949672960 | bytes 159383552 | tf_op jit(solution)/shard_map/ecf,edf->ecd/dot_general | solution.py:309
  1408.8 75.8 %add_convert_fusion = bf16[16,1280,1024]{2,1,0:T(8,128)(2,1)} fusion(f32[16,1280,1024]{2,1,0:T(8,128)} %fusion.13, bf16[16,1024,1024]{2,1,0:T(8,128)(2,1)} %param.20, bf16[16,2560,1024]{2,1,0:T(8,128)(2,1)} %get-tuple-element.30), kind=kOutput, calls=%fused_computation.9 | convolution fusion | flops 42991616000 | bytes 201326592 | tf_op jit(solution)/shard_map/ecf,edf->ecd/dot_general | solution.py:309
  1484.7 52.6 %combine_slots.1 = (f32[8192,1024]{1,0:T(8,128)}, f32[4,16,2048]{2,1,0:T(8,128)}) custom-call(s32[1024]{0:T(1024)} %get-tuple-element.52.start_ref, s32[1024]{0:T(1024)} %get-tuple-element.51.count_ref, bf16[16,4,320,1024]{3,2,1,0:T(8,128)(2,1)} %bitcast.206, f32[16,4,320,1]{3,2,1,0:T(8,128)} %reshape_broadcast_in_dim.4.dg_ref, s32[8,16,2048]{2,1,0:T(8,128)} %reshape.231.slot_ref), custom_call_target="tpu_custom_call" | custom-call | flops 17179869184 | bytes 75497472 | tf_op jit(solution)/shard_map/combine_slots/pallas_call | solution.py:224
  1544.0 113.2 %fusion.1 = f32[16,1024,1024]{2,1,0:T(8,128)} fusion(bf16[16,2560,1024]{2,1,0:T(8,128)(2,1)} %get-tuple-element.28, bf16[16,2560,1024]{2,1,0:T(8,128)(2,1)} %bitcast.21, f32[16,2560]{1,0:T(8,128)S(1)} %copy-done.35), kind=kOutput, calls=%fused_computation.10 | convolution fusion | flops 86025175040 | bytes 235044864 | tf_op jit(solution)/shard_map/ecf,ecd->efd/dot_general | solution.py:314
  1657.2 108.4 %fusion.101 = f32[16,1024,1024]{2,1,0:T(8,128)} fusion(bf16[16,2560,1024]{2,1,0:T(8,128)(2,1)} %bitcast.22, bf16[16,2560,1024]{2,1,0:T(8,128)(2,1)} %get-tuple-element.29), kind=kOutput, calls=%fused_computation.179 | convolution fusion | flops 85899345920 | bytes 234881024 | tf_op jit(solution)/shard_map/ecd,ecf->edf/dot_general | solution.py:315
  1803.8 18.5 convert_bitcast_fusion.2
  1822.3 37.0 %fusion.8 = (f32[2,8,1024]{2,1,0:T(8,128)S(1)}, bf16[2,8,1024,1024]{2,3,1,0:T(8,128)(2,1)}) fusion(f32[2,8,1024,1024]{2,3,1,0:T(8,128)} %get-tuple-element.56, f32[2,8,1024]{2,1,0:T(8,128)S(1)} %copy-done.15, f32[2,1024,3,8,128]{1,4,3,2,0:T(8,128)} %fusion.48, bf16[2,1024,8,128]{1,3,2,0:T(8,128)(2,1)} %copy.93), kind=kOutput, calls=%fused_computation.17 | convolution fusion | flops 4378836992 | bytes 109182976 | tf_op jit(solution)/shard_map/transpose(jvp(bhqk,bkhd->bqhd))/dot_general | solution.py:61
  1859.3 38.3 %convert_bitcast_fusion = f32[2,1024,8,128]{1,3,2,0:T(8,128)} fusion(bf16[2,1024,8,64]{1,3,2,0:T(8,128)(2,1)} %get-tuple-element.43, bf16[2,1024,8,64]{1,3,2,0:T(8,128)(2,1)} %get-tuple-element.44, f32[2,8,1024,1024]{2,3,1,0:T(8,128)} %get-tuple-element.56, bf16[2,8,1024,1024]{2,3,1,0:T(8,128)(2,1)} %get-tuple-element.63, f32[2,8,1024]{2,1,0:T(8,128)S(1)} %neg.62, ...), kind=kOutput, calls=%fused_computation.67 | convolution fusion | flops 4408213504 | bytes 114425856 | tf_op jit(solution)/shard_map/transpose(jvp(bqhd,bkhd->bhqk))/dot_general | solution.py:58
  1897.6 36.4 %convert_bitcast_fusion.1 = f32[2,1024,8,128]{1,3,2,0:T(8,128)} fusion(bf16[2,1024,8,64]{1,3,2,0:T(8,128)(2,1)} %get-tuple-element.38, bf16[2,1024,8,64]{1,3,2,0:T(8,128)(2,1)S(1)} %copy-done.21, f32[2,8,1024,1024]{2,3,1,0:T(8,128)} %get-tuple-element.56, bf16[2,8,1024,1024]{2,3,1,0:T(8,128)(2,1)} %get-tuple-element.63, f32[2,8,1024]{2,1,0:T(8,128)S(1)} %neg.62, ...), kind=kOutput, calls=%fused_computation.68 | convolution fusion | flops 4408213504 | bytes 114425856 | tf_op jit(solution)/shard_map/transpose(jvp(bqhd,bkhd->bhqk))/dot_general | solution.py:58
  1934.1 11.4 multiply_add_fusion.3
  1963.3 17.5 copy.98
  1980.8 19.3 convert_element_type.208
  2000.1 19.7 fusion.100
  2019.8 108.2 %fusion.102 = f32[16,1024,1024]{2,1,0:T(8,128)} fusion(bf16[16,2560,1024]{2,1,0:T(8,128)(2,1)} %bitcast.22, bf16[16,2560,1024]{2,1,0:T(8,128)(2,1)} %get-tuple-element.30), kind=kOutput, calls=%fused_computation.180 | convolution fusion | flops 85899345920 | bytes 234881024 | tf_op jit(solution)/shard_map/ecd,ecf->edf/dot_general | solution.py:316
  2128.1 20.3 fusion.40
  2148.4 25.9 %all-reduce.7 = (f32[1024]{0:T(1024)}, f32[1024]{0:T(1024)}) all-reduce(f32[1024]{0:T(1024)S(1)} %get-tuple-element.21, f32[1024]{0:T(1024)S(1)} %copy-done.48), channel_id=1, replica_groups=mesh['dp'=2,'ep'=4] {'dp','ep'}, use_global_device_ids=true, to_apply=%region_19.20 | all-reduce | flops 2048 | bytes 16384 | tf_op jit(solution)/shard_map/psum | solution.py:321
  2183.0 49.9 %all-reduce.11.cloned.1.call-done = (f32[1024,3072]{1,0:T(8,128)}, f32[1024,1024]{1,0:T(8,128)}, f32[1024,64]{0,1:T(8,128)}) async-done(((f32[1024,3072]{1,0:T(8,128)}, f32[1024,1024]{1,0:T(8,128)}, f32[1024,64]{0,1:T(8,128)}), (f32[1024,3072]{1,0:T(8,128)}, f32[1024,1024]{1,0:T(8,128)}, f32[1024,64]{0,1:T(8,128)})) %all-reduce.11.cloned.1.call-update) | async-done | bytes 17039376 | tf_op jit(solution)/shard_map/psum | solution.py:321
  (179 shorter events, 173.2 us)
Async XLA Ops:
  7.2 194.4 %all-gather.9.cloned.1.call-start = ((), (), s32[]{:S(2)}) async-start(), calls=%async_computation.4 | async-start | bytes 4718592 | tf_op jit(solution)/shard_map/all_gather | solution.py:291
  7.6 47.0 %copy-start.22 = (pred[1024,1024]{0,1:T(8,128)(4,1)}, pred[1024,1024]{0,1:T(8,128)(4,1)S(1)}, u32[]{:S(2)}) copy-start(pred[1024,1024]{0,1:T(8,128)(4,1)S(1)} %iota_compare_fusion.1) | copy-start | bytes 3145732
  8.3 12.3 copy-start.43
  54.5 34.7 %copy-start.20 = (bf16[2,1024,8,64]{1,3,2,0:T(8,128)(2,1)}, bf16[2,1024,8,64]{1,3,2,0:T(8,128)(2,1)S(1)}, u32[]{:S(2)}) copy-start(bf16[2,1024,8,64]{1,3,2,0:T(8,128)(2,1)S(1)} %get-tuple-element.37) | copy-start | bytes 6291460
  89.2 32.9 %copy-start.29 = (f32[2,8,1024]{2,1,0:T(8,128)}, f32[2,8,1024]{2,1,0:T(8,128)S(1)}, u32[]{:S(2)}) copy-start(f32[2,8,1024]{2,1,0:T(8,128)S(1)} %get-tuple-element.55) | copy-start | bytes 196612
  146.4 9.5 copy-start.27
  163.5 23.5 %copy-start.32 = (f32[2048]{0:T(1024)}, f32[2048]{0:T(1024)S(1)}, u32[]{:S(2)}) copy-start(f32[2048]{0:T(1024)S(1)} %fusion.72) | copy-start | bytes 24580
  164.2 22.9 %copy-start.36 = (f32[2048]{0:T(1024)}, f32[2048]{0:T(1024)S(1)}, u32[]{:S(2)}) copy-start(f32[2048]{0:T(1024)S(1)} %fusion.94) | copy-start | bytes 24580
  165.2 193.4 %all-gather.5.cloned.1.call-start = ((), (), s32[]{:S(2)}) async-start(), calls=%async_computation.2 | async-start | bytes 37748736 | tf_op jit(solution)/shard_map/all_gather | solution.py:287
  165.9 349.7 %all-gather.7.cloned.1.call-start = ((), (), s32[]{:S(2)}) async-start(), calls=%async_computation.3 | async-start | bytes 37748736 | tf_op jit(solution)/shard_map/all_gather | solution.py:277
  166.7 1606.4 %reduce-scatter.2.cloned.1.call-start = ((), (), s32[]{:S(2)}) async-start(), calls=%async_computation.5 | async-start | bytes 41943040 | tf_op jit(solution)/shard_map/reduce_scatter | solution.py:312
  688.8 86.3 %copy-start.34 = (f32[16,2560]{1,0:T(8,128)}, f32[16,2560]{1,0:T(8,128)S(1)}, u32[]{:S(2)}) copy-start(f32[16,2560]{1,0:T(8,128)S(1)} %mul.502) | copy-start | bytes 491524
  1539.8 225.8 %all-to-all-start = ((f32[4,16,2048]{2,1,0:T(8,128)}), f32[4,16,2048]{2,1,0:T(8,128)}, u32[]{:S(2)}, u32[]{:S(2)}) async-start(f32[4,16,2048]{2,1,0:T(8,128)} %get-tuple-element.18), calls=%async_computation.1 | async-start | bytes 1048576 | tf_op jit(solution)/shard_map/all_to_all | solution.py:313
  1543.9 689.0 %all-reduce.11.cloned.1.call-start = ((), (), s32[]{:S(2)}) async-start(), calls=%async_computation.6 | async-start | bytes 34078720 | tf_op jit(solution)/shard_map/psum | solution.py:321
  1657.2 108.4 %copy-start.11 = (f32[2048,64]{0,1:T(8,128)S(1)}, f32[2048,64]{0,1:T(8,128)}, u32[]{:S(2)}) copy-start(f32[2048,64]{0,1:T(8,128)} %broadcast_divide_fusion) | copy-start | bytes 1572868
  1657.2 109.6 %copy-start.4 = (f32[2048,64]{0,1:T(8,128)S(1)}, f32[2048,64]{0,1:T(8,128)}, u32[]{:S(2)}) copy-start(f32[2048,64]{0,1:T(8,128)} %copy-done.3) | copy-start | bytes 1572868
  1657.2 109.6 %copy-start.9 = (f32[2048,64]{0,1:T(8,128)S(1)}, f32[2048,64]{0,1:T(8,128)}, u32[]{:S(2)}) copy-start(f32[2048,64]{0,1:T(8,128)} %copy-done.8) | copy-start | bytes 1572868
  1657.2 109.6 %copy-start.26 = (f32[2048]{0:T(1024)S(1)}, f32[2048]{0:T(1024)}, u32[]{:S(2)}) copy-start(f32[2048]{0:T(1024)} %copy-done.25) | copy-start | bytes 24580
  1657.2 109.6 %copy-start.33 = (f32[2048]{0:T(1024)S(1)}, f32[2048]{0:T(1024)}, u32[]{:S(2)}) copy-start(f32[2048]{0:T(1024)} %copy-done.32) | copy-start | bytes 24580
  1657.2 109.6 %copy-start.37 = (f32[2048]{0:T(1024)S(1)}, f32[2048]{0:T(1024)}, u32[]{:S(2)}) copy-start(f32[2048]{0:T(1024)} %copy-done.36) | copy-start | bytes 24580
  1803.8 18.5 copy-start.15
  1822.3 37.0 %copy-start.31 = (f32[2,8,1024]{2,1,0:T(8,128)S(1)}, f32[2,8,1024]{2,1,0:T(8,128)}, u32[]{:S(2)}) copy-start(f32[2,8,1024]{2,1,0:T(8,128)} %copy-done.29) | copy-start | bytes 196612
  1859.3 38.3 %copy-start.21 = (bf16[2,1024,8,64]{1,3,2,0:T(8,128)(2,1)S(1)}, bf16[2,1024,8,64]{1,3,2,0:T(8,128)(2,1)}, u32[]{:S(2)}) copy-start(bf16[2,1024,8,64]{1,3,2,0:T(8,128)(2,1)} %copy-done.20) | copy-start | bytes 6291460
  1897.6 36.5 %copy-start.17 = (f32[1024,64]{0,1:T(8,128)S(1)}, f32[1024,64]{0,1:T(8,128)}, u32[]{:S(2)}) copy-start(f32[1024,64]{0,1:T(8,128)} %copy-done.16) | copy-start | bytes 786436
  1897.6 36.5 %copy-start.19 = (f32[1024,64]{0,1:T(8,128)S(1)}, f32[1024,64]{0,1:T(8,128)}, u32[]{:S(2)}) copy-start(f32[1024,64]{0,1:T(8,128)} %copy-done.18) | copy-start | bytes 786436
  1945.5 9.6 copy-start.7
  2019.8 108.3 %copy-start = (bf16[2,1024,1024]{2,1,0:T(8,128)(2,1)S(1)}, bf16[2,1024,1024]{2,1,0:T(8,128)(2,1)}, u32[]{:S(2)}) copy-start(bf16[2,1024,1024]{2,1,0:T(8,128)(2,1)} %param.11) | copy-start | bytes 12582916
  2019.8 108.3 %copy-start.44 = (f32[1024]{0:T(1024)S(1)}, f32[1024]{0:T(1024)}, u32[]{:S(2)}) copy-start(f32[1024]{0:T(1024)} %copy-done.43) | copy-start | bytes 12292
  2019.8 108.3 %copy-start.46 = (f32[1,8,2,128]{3,1,2,0:T(8,128)S(1)}, f32[1,8,2,128]{3,1,2,0:T(8,128)}, u32[]{:S(2)}) copy-start(f32[1,8,2,128]{3,1,2,0:T(8,128)} %copy.137) | copy-start | bytes 24580
  2128.1 20.3 copy-start.48
  2128.1 46.2 %copy-start.47 = (f32[2048]{0:T(1024)S(1)}, f32[2048]{0:T(1024)}, u32[]{:S(2)}) copy-start(f32[2048]{0:T(1024)} %multiply_multiply_fusion) | copy-start | bytes 24580
  2232.9 11.1 copy-start.14
  (26 other events, 123.1 us)
Sparse Core Ops, SparseCore 0:
  165.3 36.1 all-gather.8
  203.3 155.1 all-gather.4
  360.4 155.2 all-gather.6
  1537.4 227.8 reduce-scatter.1
  2019.9 212.9 all-reduce.10

commit v2 on v1

v2 whole, which is shorter than its diff:
```python
import functools

import jax
import jax.numpy as jnp
from jax import lax
from jax.experimental import pallas as pl
from jax.experimental.pallas import tpu as pltpu
from jax.sharding import PartitionSpec as P

EPS = 1e-6
HEAD_DIM = 128
ROPE_BASE = 10000.0
TOK_BLOCK = 256
WIN = 64
ALIGN = 16
VMEM_MAX = 64 * 1024 * 1024 - 65536


def capacity_rows(num_tokens, top_k, num_experts):
    return 8 * ((5 * num_tokens * top_k + 32 * num_experts - 1) // (32 * num_experts))


def rms_norm(x_rows, gain_vec):
    x_f32 = x_rows.astype(jnp.float32)
    inv_rms = lax.rsqrt(jnp.mean(x_f32 * x_f32, axis=-1, keepdims=True) + EPS)
    return (x_f32 * inv_rms * gain_vec.astype(jnp.float32)).astype(jnp.bfloat16)


def rms_norm_bwd(x_rows, gain_vec, d_out):
    x_f32 = x_rows.astype(jnp.float32)
    inv_rms = lax.rsqrt(jnp.mean(x_f32 * x_f32, axis=-1, keepdims=True) + EPS)
    d_gain = jnp.sum(d_out * x_f32 * inv_rms, axis=0)
    d_scaled = d_out * gain_vec.astype(jnp.float32)
    d_x = inv_rms * d_scaled - x_f32 * inv_rms ** 3 * jnp.mean(d_scaled * x_f32, axis=-1, keepdims=True)
    return d_x, d_gain


def rope_rotate(head_vals):
    seq_len = head_vals.shape[1]
    half_dim = head_vals.shape[-1] // 2
    inv_freq = ROPE_BASE ** (-jnp.arange(half_dim, dtype=jnp.float32) / half_dim)
    angles = jnp.arange(seq_len, dtype=jnp.float32)[:, None] * inv_freq[None, :]
    cos_b = jnp.cos(angles)[None, :, None, :]
    sin_b = jnp.sin(angles)[None, :, None, :]
    lower_half = head_vals[..., :half_dim]
    upper_half = head_vals[..., half_dim:]
    return jnp.concatenate([lower_half * cos_b - upper_half * sin_b, upper_half * cos_b + lower_half * sin_b], axis=-1)


def attention_core(qkv_rows, num_seqs):
    num_tokens = qkv_rows.shape[0]
    seq_len = num_tokens // num_seqs
    model_width = qkv_rows.shape[1] // 3
    qkv_heads = qkv_rows.reshape(num_seqs, seq_len, 3, model_width // HEAD_DIM, HEAD_DIM)
    query_rot = rope_rotate(qkv_heads[:, :, 0]).astype(jnp.bfloat16)
    key_rot = rope_rotate(qkv_heads[:, :, 1]).astype(jnp.bfloat16)
    value_h = qkv_heads[:, :, 2].astype(jnp.bfloat16)
    scores = jnp.einsum('bqhd,bkhd->bhqk', query_rot, key_rot, preferred_element_type=jnp.float32) * HEAD_DIM ** -0.5
    causal = jnp.arange(seq_len)[:, None] >= jnp.arange(seq_len)[None, :]
    attn_probs = jax.nn.softmax(jnp.where(causal, scores, -1e30), axis=-1).astype(jnp.bfloat16)
    context = jnp.einsum('bhqk,bkhd->bqhd', attn_probs, value_h, preferred_element_type=jnp.float32)
    return context.astype(jnp.bfloat16).reshape(num_tokens, model_width)


def choice_mask(idx_rows, num_experts):
    return (idx_rows[:, :, None] == jnp.arange(num_experts, dtype=jnp.int32)[None, None, :])


def gate_forward(logits, idx_rows, num_experts):
    probs_all = jax.nn.softmax(logits, axis=-1)
    hits = jnp.sum(choice_mask(idx_rows, num_experts).astype(jnp.float32), axis=1)
    picked_sum = jnp.sum(probs_all * hits, axis=1, keepdims=True)
    return probs_all, hits, picked_sum


def gate_backward(probs_all, hits, picked_sum, d_gate_dense):
    gates = probs_all * hits / picked_sum
    d_probs = hits * (d_gate_dense - jnp.sum(d_gate_dense * gates, axis=1, keepdims=True)) / picked_sum
    return probs_all * (d_probs - jnp.sum(d_probs * probs_all, axis=1, keepdims=True))


def slot_positions(idx_t, first_expert, local_experts, capacity):
    num_dev, _, num_tokens = idx_t.shape
    experts = first_expert + jnp.arange(local_experts, dtype=jnp.int32)
    hits = jnp.sum((idx_t[:, None, :, :] == experts[None, :, None, None]).astype(jnp.float32), axis=2)
    blocks = num_tokens // TOK_BLOCK
    hit_blk = hits.reshape(num_dev, local_experts, blocks, TOK_BLOCK)
    upto = (jnp.arange(TOK_BLOCK)[:, None] <= jnp.arange(TOK_BLOCK)[None, :]).astype(jnp.bfloat16)
    within = jnp.einsum('debt,tu->debu', hit_blk.astype(jnp.bfloat16), upto, preferred_element_type=jnp.float32)
    totals = jnp.sum(hit_blk, axis=-1)
    strict = (jnp.arange(blocks)[:, None] < jnp.arange(blocks)[None, :])
    before = jnp.sum(jnp.where(strict[None, None], totals[:, :, :, None], 0.0), axis=2)
    position = (within + before[..., None] - 1.0).astype(jnp.int32)
    slot_of = jnp.where((hit_blk > 0) & (position < capacity), position, -1)
    begin = jnp.minimum(before.astype(jnp.int32), capacity)
    end = jnp.minimum((before + totals).astype(jnp.int32), capacity)
    win_start = jnp.minimum(begin // ALIGN * ALIGN, capacity - WIN)
    win_count = jnp.maximum((end - win_start + WIN - 1) // WIN, 1)
    return jnp.transpose(slot_of, (0, 2, 1, 3)), win_start, win_count


def expand_routes(idx_t, values_t, first_expert, local_experts):
    num_dev, _, num_tokens = idx_t.shape
    experts = first_expert + jnp.arange(local_experts, dtype=jnp.int32)
    dense = jnp.sum(jnp.where(idx_t[:, None, :, :] == experts[None, :, None, None], values_t[:, None, :, :], 0.0), axis=2)
    return jnp.transpose(dense.reshape(num_dev, local_experts, num_tokens // TOK_BLOCK, TOK_BLOCK), (0, 2, 1, 3))


def gather_kernel(base_ref, start_ref, count_ref, most_ref, x_ref, dy_ref, slot_ref, gate_ref, *rest, blocks, capacity, group, scaled):
    s_ref, dyr_ref = rest[-3:-1] if not scaled else rest[-2:]
    g_ref = None if scaled else rest[-1]
    dev, part = pl.program_id(0), pl.program_id(1)
    experts = group * pl.num_programs(1)
    s_ref[...] = jnp.zeros_like(s_ref)
    dyr_ref[...] = jnp.zeros_like(dyr_ref)
    if g_ref is not None:
        g_ref[...] = jnp.zeros_like(g_ref)
    row_iota = lax.broadcasted_iota(jnp.int32, (WIN, TOK_BLOCK), 0)

    def at(i, blk):
        return (dev * experts + part * group + i) * blocks + blk

    def window(i, blk, first, floor=None):
        slot_row = slot_ref[0, blk, pl.ds(part * group + i, 1), :]
        hit = slot_row == row_iota + first
        if floor is not None:
            hit = hit & (slot_row >= floor)
        gate_row = gate_ref[0, blk, pl.ds(part * group + i, 1), :]
        gate_col = jnp.sum(jnp.where(hit, gate_row, 0.0), axis=1, keepdims=True)
        return jnp.where(hit, 1.0, 0.0).astype(jnp.bfloat16), gate_col

    def deposit(i, first, s_rows, dy_rows, gate_col):
        rows = pl.ds(pl.multiple_of(first, ALIGN), WIN)
        s_ref[i, 0, rows, :] += s_rows.astype(jnp.bfloat16)
        if scaled:
            dyr_ref[i, 0, rows, :] += (dy_rows * gate_col).astype(jnp.bfloat16)
        else:
            dyr_ref[i, 0, rows, :] += dy_rows.astype(jnp.bfloat16)
            g_ref[i, 0, rows, :] += gate_col

    for blk in range(blocks):
        tokens = slice(blk * TOK_BLOCK, (blk + 1) * TOK_BLOCK)
        firsts = [start_ref[at(i, blk)] for i in range(group)]
        parts = [window(i, blk, firsts[i]) for i in range(group)]
        pick = jnp.concatenate([p[0] for p in parts], axis=0)
        s_all = jnp.dot(pick, x_ref[tokens, :], preferred_element_type=jnp.float32)
        dy_all = jnp.dot(pick, dy_ref[tokens, :], preferred_element_type=jnp.float32)
        for i in range(group):
            rows = slice(i * WIN, (i + 1) * WIN)
            deposit(i, firsts[i], s_all[rows], dy_all[rows], parts[i][1])

    @pl.when(most_ref[dev * pl.num_programs(1) + part] > 1)
    def _():
        for i in range(group):
            def per_block(blk, carry):
                def extra(w, inner):
                    floor = start_ref[at(i, blk)] + w * WIN
                    first = jnp.minimum(floor, capacity - WIN)
                    pick, gate_col = window(i, blk, first, floor)
                    tokens = pl.ds(pl.multiple_of(blk * TOK_BLOCK, TOK_BLOCK), TOK_BLOCK)
                    s_rows = jnp.dot(pick, x_ref[tokens, :], preferred_element_type=jnp.float32)
                    dy_rows = jnp.dot(pick, dy_ref[tokens, :], preferred_element_type=jnp.float32)
                    deposit(i, first, s_rows, dy_rows, gate_col)
                    return inner
                return lax.fori_loop(1, count_ref[at(i, blk)], extra, carry)
            lax.fori_loop(0, blocks, per_block, 0)


def gather_slots(base_dev, routes, dev_from, num_dev, x_table, dy_table, filled, total_dev, capacity, scaled, from_all):
    slot_of, win_start, win_count, gate_of = (r[dev_from:dev_from + num_dev] for r in routes)
    _, blocks, experts, _ = slot_of.shape
    width = x_table.shape[1]
    num_tokens = blocks * TOK_BLOCK
    group = 4
    most = jnp.max(win_count.reshape(num_dev, experts // group, group * blocks), axis=2).reshape(-1)

    def table_map(d, p, base_ref, *_):
        return (lax.bitwise_xor(d + dev_from, base_ref[0]) if from_all else 0, 0)

    def route_map(d, p, *_):
        return (d, 0, 0, 0)

    def out_map(d, p, *_):
        return (p, d + dev_from, 0, 0)

    def gate_map(d, p, *_):
        return (p, d, 0, 0)

    rows_shape = jax.ShapeDtypeStruct((experts, total_dev, capacity, width), jnp.bfloat16)
    row_spec = pl.BlockSpec((group, 1, capacity, width), out_map)
    out_shape, out_specs = [rows_shape, rows_shape], [row_spec, row_spec]
    if not scaled:
        out_shape.append(jax.ShapeDtypeStruct((experts, num_dev, capacity, 1), jnp.float32))
        out_specs.append(pl.BlockSpec((group, 1, capacity, 1), gate_map))
    held = () if filled is None else tuple(filled)
    return pl.pallas_call(
        functools.partial(gather_kernel, blocks=blocks, capacity=capacity, group=group, scaled=scaled),
        out_shape=out_shape,
        grid_spec=pltpu.PrefetchScalarGridSpec(
            num_scalar_prefetch=4, grid=(num_dev, experts // group),
            in_specs=[pl.BlockSpec((num_tokens, width), table_map), pl.BlockSpec((num_tokens, width), table_map),
                      pl.BlockSpec((1, blocks, experts, TOK_BLOCK), route_map), pl.BlockSpec((1, blocks, experts, TOK_BLOCK), route_map)]
                     + [pl.BlockSpec(memory_space=pl.ANY)] * len(held),
            out_specs=out_specs),
        input_output_aliases={8 + i: i for i in range(len(held))},
        compiler_params=pltpu.CompilerParams(vmem_limit_bytes=VMEM_MAX, dimension_semantics=('arbitrary', 'arbitrary')),
        cost_estimate=pl.CostEstimate(flops=4 * num_dev * blocks * experts * WIN * TOK_BLOCK * width,
                                      bytes_accessed=4 * num_dev * (num_tokens + experts * capacity) * width, transcendentals=0),
        name='gather_slots',
    )(base_dev, win_start.reshape(-1), win_count.reshape(-1), most, x_table, dy_table, slot_of, gate_of, *held)


def dot_nn(left, right):
    return jnp.dot(left, right, preferred_element_type=jnp.float32)


def dot_nt(left, right):
    return lax.dot_general(left, right, (((1,), (1,)), ((), ())), preferred_element_type=jnp.float32)


def expert_kernel(*refs, own, chunk, held):
    if own:
        s_ref, dy_ref, g_ref, wg_ref, wu_ref, wd_ref = refs[:6]
        hid_ref, dag_ref, dau_ref, do_ref, ds_ref, dgate_ref = refs[6 + held:]
        do_ref[0] = (dy_ref[0].astype(jnp.float32) * g_ref[0]).astype(jnp.bfloat16)
    else:
        s_ref, do_ref, wg_ref, wu_ref, wd_ref = refs[:5]
        hid_ref, dag_ref, dau_ref = refs[5 + held:]
    width = s_ref.shape[-1]
    for c in range(0, width, chunk):
        cols = slice(c, c + chunk)
        act_gate = dot_nn(s_ref[0], wg_ref[0, :, cols])
        act_up = dot_nn(s_ref[0], wu_ref[0, :, cols])
        d_hidden = dot_nt(do_ref[0], wd_ref[0, cols, :])
        sig = jax.nn.sigmoid(act_gate)
        silu = act_gate * sig
        hid_ref[0, :, cols] = (silu * act_up).astype(jnp.bfloat16)
        dau_ref[0, :, cols] = (d_hidden * silu).astype(jnp.bfloat16)
        dag_ref[0, :, cols] = (d_hidden * act_up * (sig * (1.0 + act_gate * (1.0 - sig)))).astype(jnp.bfloat16)
    if own:
        d_gate = None
        for c in range(0, width, chunk):
            cols = slice(c, c + chunk)
            out = dot_nn(hid_ref[0], wd_ref[0, :, cols]).astype(jnp.bfloat16).astype(jnp.float32)
            part = jnp.sum(out * dy_ref[0, :, cols].astype(jnp.float32), axis=1, keepdims=True)
            d_gate = part if d_gate is None else d_gate + part
            ds_ref[0, :, cols] = (dot_nt(dag_ref[0], wg_ref[0, cols, :]) + dot_nt(dau_ref[0], wu_ref[0, cols, :])).astype(jnp.bfloat16)
        dgate_ref[0] = d_gate


def expert_pass(own, tile, first_tile, num_tiles, s_rows, dy_rows, gate_col, w_gate, w_up, w_down, filled):
    experts, rows, width = s_rows.shape
    row_spec = pl.BlockSpec((1, tile, width), lambda e, r: (e, first_tile + r, 0))
    near_spec = pl.BlockSpec((1, tile, width), lambda e, r: (e, r, 0))
    col_spec = pl.BlockSpec((1, tile, 1), lambda e, r: (e, r, 0))
    w_spec = pl.BlockSpec((1, width, width), lambda e, r: (e, 0, 0))
    full = jax.ShapeDtypeStruct((experts, rows, width), jnp.bfloat16)
    out_shape, out_specs = [full] * 3, [row_spec] * 3
    args, in_specs = [s_rows, dy_rows], [row_spec, row_spec]
    aliases = {}
    if own:
        args.append(gate_col)
        in_specs.append(col_spec)
        out_shape += [full, jax.ShapeDtypeStruct((experts, num_tiles * tile, width), jnp.bfloat16),
                      jax.ShapeDtypeStruct((experts, num_tiles * tile, 1), jnp.float32)]
        out_specs += [row_spec, near_spec, col_spec]
        aliases[1] = 3
    args += [w_gate, w_up, w_down]
    in_specs += [w_spec] * 3
    held = () if filled is None else tuple(filled)
    for i, arr in enumerate(held):
        aliases[len(args)] = i
        args.append(arr)
        in_specs.append(pl.BlockSpec(memory_space=pl.ANY))
    units = 6 if own else 3
    return pl.pallas_call(
        functools.partial(expert_kernel, own=own, chunk=min(256, width), held=len(held)),
        out_shape=out_shape, grid=(experts, num_tiles), in_specs=in_specs, out_specs=out_specs,
        input_output_aliases=aliases,
        compiler_params=pltpu.CompilerParams(vmem_limit_bytes=VMEM_MAX, dimension_semantics=('arbitrary', 'arbitrary')),
        cost_estimate=pl.CostEstimate(flops=2 * units * experts * num_tiles * tile * width * width,
                                      bytes_accessed=2 * experts * width * (3 * width + 7 * num_tiles * tile),
                                      transcendentals=experts * num_tiles * tile * width),
        name='expert_own' if own else 'expert_far',
    )(*args)


def combine_kernel(home_ref, start_ref, count_ref, most_ref, ds_ref, dg_ref, slot_ref, *rest, experts, blocks, capacity):
    out_ref, dgt_ref = rest[-2:]
    dev, blk = pl.program_id(0), pl.program_id(1)
    row_iota = lax.broadcasted_iota(jnp.int32, (WIN, TOK_BLOCK), 0)

    def window(e, first, floor=None):
        slot_row = slot_ref[0, 0, e:e + 1, :]
        hit = slot_row == row_iota + first
        if floor is not None:
            hit = hit & (slot_row >= floor)
        rows = pl.ds(pl.multiple_of(first, ALIGN), WIN)
        gate_row = jnp.sum(jnp.where(hit, dg_ref[e, 0, rows, :], 0.0), axis=0, keepdims=True)
        return jnp.where(hit, 1.0, 0.0).astype(jnp.bfloat16), ds_ref[e, 0, rows, :], gate_row

    def spread(pick, rows):
        return lax.dot_general(pick, rows, (((0,), (0,)), ((), ())), preferred_element_type=jnp.float32)

    parts = [window(e, start_ref[(dev * experts + e) * blocks + blk]) for e in range(experts)]
    out_ref[...] = spread(jnp.concatenate([p[0] for p in parts], axis=0), jnp.concatenate([p[1] for p in parts], axis=0))
    for e in range(experts):
        dgt_ref[0, 0, e:e + 1, :] = parts[e][2]

    @pl.when(most_ref[dev * blocks + blk] > 1)
    def _():
        for e in range(experts):
            at = (dev * experts + e) * blocks + blk

            def extra(w, carry):
                floor = start_ref[at] + w * WIN
                pick, rows, gate_row = window(e, jnp.minimum(floor, capacity - WIN), floor)
                out_ref[...] += spread(pick, rows)
                dgt_ref[0, 0, e:e + 1, :] += gate_row
                return carry
            lax.fori_loop(1, count_ref[at], extra, 0)


def combine_slots(home, routes, dev_from, num_dev, total_dev, d_slots, d_gate_slots, filled):
    slot_of, win_start, win_count = (r[dev_from:dev_from + num_dev] for r in routes[:3])
    experts, _, capacity, width = d_slots.shape
    blocks = slot_of.shape[1]
    num_tokens = blocks * TOK_BLOCK
    most = jnp.max(win_count, axis=1).reshape(-1)

    def home_of(d, home_ref):
        return lax.bitwise_xor(d + dev_from, home_ref[0])

    held = () if filled is None else tuple(filled)
    return pl.pallas_call(
        functools.partial(combine_kernel, experts=experts, blocks=blocks, capacity=capacity),
        out_shape=[jax.ShapeDtypeStruct((total_dev * num_tokens, width), jnp.float32),
                   jax.ShapeDtypeStruct((total_dev, blocks, experts, TOK_BLOCK), jnp.float32)],
        grid_spec=pltpu.PrefetchScalarGridSpec(
            num_scalar_prefetch=4, grid=(num_dev, blocks),
            in_specs=[pl.BlockSpec((experts, 1, capacity, width), lambda d, b, *_: (0, d, 0, 0)),
                      pl.BlockSpec((experts, 1, capacity, 1), lambda d, b, *_: (0, d, 0, 0)),
                      pl.BlockSpec((1, 1, experts, TOK_BLOCK), lambda d, b, *_: (d, b, 0, 0))]
                     + [pl.BlockSpec(memory_space=pl.ANY)] * len(held),
            out_specs=[pl.BlockSpec((TOK_BLOCK, width), lambda d, b, home_ref, *_: (home_of(d, home_ref) * blocks + b, 0)),
                       pl.BlockSpec((1, 1, experts, TOK_BLOCK), lambda d, b, home_ref, *_: (home_of(d, home_ref), b, 0, 0))]),
        input_output_aliases={7 + i: i for i in range(len(held))},
        compiler_params=pltpu.CompilerParams(vmem_limit_bytes=VMEM_MAX, dimension_semantics=('arbitrary', 'arbitrary')),
        cost_estimate=pl.CostEstimate(flops=2 * num_dev * blocks * experts * WIN * TOK_BLOCK * width,
                                      bytes_accessed=2 * num_dev * (2 * num_tokens + experts * capacity) * width, transcendentals=0),
        name='combine_slots',
    )(home, win_start.reshape(-1), win_count.reshape(-1), most, d_slots, d_gate_slots, slot_of, *held)


def dense_backward(saved_state, x_rows, dy_rows, d_logits, d_normed2_moe, norm1_gain, norm2_gain, w_qkv, w_attn_out, w_router):
    normed1, attn_pullback, context, h_rows, normed2 = saved_state
    d_w_router = jnp.einsum('td,te->de', normed2, d_logits, preferred_element_type=jnp.float32)
    d_normed2 = d_normed2_moe + jnp.einsum('te,de->td', d_logits, w_router, preferred_element_type=jnp.float32)
    d_h_part, d_norm2_gain = rms_norm_bwd(h_rows, norm2_gain, d_normed2)
    d_h = (dy_rows.astype(jnp.float32) + d_h_part).astype(jnp.bfloat16)
    d_w_attn_out = jnp.einsum('td,te->de', context, d_h, preferred_element_type=jnp.float32)
    d_context = jnp.einsum('te,de->td', d_h, w_attn_out, preferred_element_type=jnp.float32).astype(jnp.bfloat16)
    d_qkv = attn_pullback(d_context)[0].astype(jnp.bfloat16)
    d_w_qkv = jnp.einsum('td,te->de', normed1, d_qkv, preferred_element_type=jnp.float32)
    d_normed1 = jnp.einsum('te,de->td', d_qkv, w_qkv, preferred_element_type=jnp.float32)
    d_x_part, d_norm1_gain = rms_norm_bwd(x_rows, norm1_gain, d_normed1)
    d_x = (d_h.astype(jnp.float32) + d_x_part).astype(jnp.bfloat16)
    return d_x, (d_norm1_gain, d_norm2_gain, d_w_qkv, d_w_attn_out, d_w_router)


def solution(mesh):
    ep_size, dp_size = mesh.shape['ep'], mesh.shape['dp']
    num_dev = ep_size * dp_size
    tok_spec = P(('dp', 'ep'), None, None)
    rep_spec = P()
    exp_spec = P('ep', None, None)
    pair = [(r, r ^ 1) for r in range(ep_size)]

    def local_step(x_tokens, dy_tokens, route_idx, norm1_gain, norm2_gain, w_qkv, w_attn_out, w_router, w_gate, w_up, w_down):
        num_seqs, seq_len, model_width = x_tokens.shape
        num_tokens = num_seqs * seq_len
        top_k = route_idx.shape[-1]
        local_experts = w_gate.shape[0]
        num_experts = local_experts * ep_size
        capacity = capacity_rows(num_tokens, top_k, num_experts)
        x_rows = x_tokens.reshape(num_tokens, model_width)
        dy_rows = dy_tokens.reshape(num_tokens, model_width)
        idx_rows = route_idx.reshape(num_tokens, top_k)
        ep_rank = lax.axis_index('ep')
        me = lax.axis_index('dp') * ep_size + ep_rank
        first_expert = ep_rank * local_experts
        order = jnp.bitwise_xor(me, jnp.arange(num_dev, dtype=jnp.int32))

        idx_wide = lax.all_gather(jnp.concatenate([idx_rows.T] * 4, axis=0), ('dp', 'ep'), axis=0)
        dy_all = lax.all_gather(dy_rows, ('dp', 'ep'), axis=0, tiled=True)
        dy_pair = lax.ppermute(dy_rows, 'ep', pair)
        idx_all = jnp.take(idx_wide[:, :top_k], order, axis=0)
        slot_of, win_start, win_count = slot_positions(idx_all, first_expert, local_experts, capacity)

        normed1 = rms_norm(x_rows, norm1_gain)
        qkv_rows = jnp.dot(normed1, w_qkv, preferred_element_type=jnp.float32)
        context, attn_pullback = jax.vjp(lambda qkv_in: attention_core(qkv_in, num_seqs), qkv_rows)
        h_rows = (x_rows.astype(jnp.float32) + jnp.dot(context, w_attn_out, preferred_element_type=jnp.float32)).astype(jnp.bfloat16)
        normed2 = rms_norm(h_rows, norm2_gain)
        x_pair = lax.ppermute(normed2, 'ep', pair)
        logits = jnp.dot(normed2, w_router, preferred_element_type=jnp.float32)
        probs_all, hits, picked_sum = gate_forward(logits, idx_rows, num_experts)
        gates = probs_all * hits / picked_sum
        gate_t = jnp.sum(jnp.where(choice_mask(idx_rows, num_experts), gates[:, None, :], 0.0), axis=2).T
        gate_pair = lax.ppermute(gate_t, 'ep', pair)
        gate_wide = lax.all_gather(jnp.concatenate([gate_t] * 4, axis=0), ('dp', 'ep'), axis=0)
        normed2_out, _ = lax.optimization_barrier((normed2, dy_all))
        x_all = lax.all_gather(normed2_out, ('dp', 'ep'), axis=0, tiled=True)
        gate_near = expand_routes(idx_all[:2], jnp.stack([gate_t, gate_pair]), first_expert, local_experts)
        gate_far = expand_routes(idx_all[2:], jnp.take(gate_wide[:, :top_k], order[2:], axis=0), first_expert, local_experts)

        near_routes = (slot_of[:2], win_start[:2], win_count[:2], gate_near)
        all_routes = (slot_of, win_start, win_count, jnp.concatenate([jnp.zeros_like(gate_near), gate_far], axis=0))
        gather = functools.partial(gather_slots, me[None], total_dev=num_dev, capacity=capacity)
        s_arr, dy_arr, g0 = gather(near_routes, 0, 1, normed2, dy_rows, None, scaled=False, from_all=False)
        s_arr, dy_arr, g1 = gather(near_routes, 1, 1, x_pair, dy_pair, (s_arr, dy_arr), scaled=False, from_all=False)
        tile = 2 * capacity
        rows_of = lambda a: a.reshape(local_experts, -1, a.shape[-1])
        slots_of = lambda a, n: a.reshape(local_experts, n, capacity, a.shape[-1])
        g_near = rows_of(jnp.concatenate([g0, g1], axis=1))
        hidden, dag, dau, d_out, ds_near, dg_near = expert_pass(True, tile, 0, 1, rows_of(s_arr), rows_of(dy_arr), g_near, w_gate, w_up, w_down, None)
        s_arr, dy_arr, g_x = gather(all_routes, 2, 2, x_all, dy_all, (s_arr, slots_of(d_out, num_dev)), scaled=False, from_all=True)
        hidden, dag, dau, d_out, ds_x, dg_x = expert_pass(True, tile, 1, 1, rows_of(s_arr), rows_of(dy_arr), rows_of(g_x), w_gate, w_up, w_down, (hidden, dag, dau))
        combined = combine_slots(ep_rank[None], all_routes, 2, 2, ep_size, slots_of(ds_x, 2), slots_of(dg_x, 2), None)
        d_tok, d_gate_t = combine_slots(ep_rank[None], all_routes, 0, 2, ep_size, slots_of(ds_near, 2), slots_of(dg_near, 2), combined)
        d_normed2_moe = lax.psum_scatter(d_tok, 'ep', scatter_dimension=0, tiled=True)
        d_gate_blk = lax.all_to_all(d_gate_t, 'ep', 0, 0, tiled=True)
        d_gate_dense = jnp.transpose(d_gate_blk, (1, 3, 0, 2)).reshape(num_tokens, num_experts)
        d_out, _ = lax.optimization_barrier((d_out, d_tok))
        s_arr, dy_arr = gather(all_routes, 4, 4, x_all, dy_all, (s_arr, slots_of(d_out, num_dev)), scaled=True, from_all=True)
        s_all, d_out = rows_of(s_arr), rows_of(dy_arr)
        hidden, dag, dau = expert_pass(False, tile, 2, 2, s_all, d_out, None, w_gate, w_up, w_down, (hidden, dag, dau))
        mm = functools.partial(jnp.einsum, preferred_element_type=jnp.float32)
        d_w_down = mm('ecf,ecd->efd', hidden, d_out)
        d_w_gate = mm('ecd,ecf->edf', s_all, dag)
        d_w_up = mm('ecd,ecf->edf', s_all, dau)

        d_logits = gate_backward(probs_all, hits, picked_sum, d_gate_dense).astype(jnp.bfloat16)
        saved_state = (normed1, attn_pullback, context, h_rows, normed2)
        d_x, dense_grads = dense_backward(saved_state, x_rows, dy_rows, d_logits, d_normed2_moe, norm1_gain, norm2_gain, w_qkv, w_attn_out, w_router)
        dense_grads = lax.psum(dense_grads, ('dp', 'ep'))
        return (d_x.reshape(x_tokens.shape),) + tuple(dense_grads) + (d_w_gate, d_w_up, d_w_down)

    return jax.shard_map(local_step, mesh=mesh,
                         in_specs=(tok_spec, tok_spec, tok_spec, rep_spec, rep_spec, rep_spec, rep_spec, rep_spec, exp_spec, exp_spec, exp_spec),
                         out_specs=(tok_spec, rep_spec, rep_spec, rep_spec, rep_spec, rep_spec, exp_spec, exp_spec, exp_spec),
                         check_vma=False)
```

time: 2260 us -> 1610 us (0.71)
  matrix products: 1300 us -> 602 us
  Pallas kernels: 215 us -> 647 us
  waiting for transfers between devices: 374 us -> 73.6 us
  local copies, waits for them, and re-layouts: 192 us -> 125 us
    dot_general x8 -> x2, matrix products: 911 us -> 217 us  [the longest x1 109 us: local_step(): d_w_gate = mm('ecd,ecf->edf', s_all, dag)]
    pallas_call x1 -> x7, Pallas kernels: 163 us -> 596 us  [the longest x3 455 us: expert_pass(): pl.pallas_call(functools.partial(expert_kernel, own=own, chunk=min(256, w...]
    all_gather x1, waiting for transfers between devices: 157 us -> 0.02 us  [local_step(): dy_all = lax.all_gather(dy_rows, ('dp', 'ep'), axis=0, tiled=True)]
    all_gather x2 -> x3, waiting for transfers between devices: 166 us -> 15.4 us  [the longest x1 8.39 us: local_step(): lax.all_gather(jnp.concatenate([gate_t] * 4, axis=0), ('dp', 'ep'), axis=0)]
    unnamed x111 -> x125, local copies, waits for them, and re-layouts: 80.5 us -> 26.4 us
    pallas_call x1 -> x2, Pallas kernels: 52.6 us -> 51.3 us  [combine_slots(): pl.pallas_call(functools.partial(combine_kernel, experts=experts, blocks=...]
  transfers between devices with their start and end apart: 6 -> 10, of which waited for: 4 -> 4; matrix products, arithmetic and copies ran while one was open for 17% -> 35% of each run, Pallas kernels for 0% -> 26%
where the time goes in v2:
time: 1610 us
  Pallas kernels  647 us (40%)
  matrix products  602 us (37%)
  local copies, waits for them, and re-layouts  125 us (8%)
  other arithmetic  109 us (7%)
  waiting for transfers between devices  73.6 us (5%)
  blocking collectives  26.1 us (2%)
    pallas_call x3, Pallas kernels, expert_pass(): pl.pallas_call(functools.partial(expert_kernel, own=own, chunk=min(256, w...  455 us
    pallas_call x4, Pallas kernels, gather_slots(): pl.pallas_call(functools.partial(gather_kernel, blocks=blocks, capacity=c...  141 us
    dot_general x1, matrix products, local_step(): d_w_gate = mm('ecd,ecf->edf', s_all, dag)  109 us
    dot_general x1, matrix products, local_step(): d_w_down = mm('ecf,ecd->efd', hidden, d_out)  108 us
    dot_general x1, matrix products, local_step(): d_w_up = mm('ecd,ecf->edf', s_all, dau)  108 us
    dot_general x2, matrix products, attention_core(): jnp.einsum('bqhd,bkhd->bhqk', query_rot, key_rot, preferred_element_type=...  74.4 us
    dot_general x3, matrix products, attention_core(): jnp.einsum('bhqk,bkhd->bqhd', attn_probs, value_h, preferred_element_type...  73.9 us
    pallas_call x2, Pallas kernels, combine_slots(): pl.pallas_call(functools.partial(combine_kernel, experts=experts, blocks=...  51.3 us
  transfers between devices with their start and end apart: 10, of which 4 were waited for; matrix products, arithmetic and copies ran while one was open for 35% of the time, Pallas kernels for 26%

profile of v2, /device:TPU:0, one launch (start us, length us, event | category | flops | bytes accessed | tf_op | source)
XLA Modules:
  0.0 1608.1 jit_solution(15032530542535354030)
XLA Ops:
  17.7 8.8 copy.204
  31.4 16.5 %fusion.39 = f32[2,1024,3,8,128]{1,4,3,2,0:T(8,128)} fusion(bf16[3,8,128,1024,1]{3,2,1,0,4:T(8,128)(2,1)S(1)} %bitcast.204, bf16[2,1024,1024]{2,1,0:T(8,128)(2,1)S(1)} %fusion.23), kind=kOutput, calls=%fused_computation.70 | convolution fusion | flops 12884901888 | bytes 35651584 | tf_op jit(solution)/shard_map/dot_general | solution.py:401
  59.5 38.0 %fusion.89 = (f32[2,8,1024]{2,1,0:T(8,128)S(1)}, f32[2,8,1024,1024]{2,3,1,0:T(8,128)}) fusion(pred[1024,1024]{0,1:T(8,128)(4,1)} %iota_compare_fusion.1, bf16[2,1024,8,64]{1,3,2,0:T(8,128)(2,1)} %get-tuple-element.105, bf16[2,1024,8,64]{1,3,2,0:T(8,128)(2,1)} %get-tuple-element.106, bf16[2,1024,8,64]{1,3,2,0:T(8,128)(2,1)} %get-tuple-element.96, ...), kind=kOutput, calls=%fused_computation.184 | convolution fusion | flops 4378854400 | bytes 76611584 | tf_op jit(solution)/shard_map/jvp()/sub | solution.py:60
  97.5 32.9 %divide_convert_fusion = bf16[2,8,1024,1024]{2,3,1,0:T(8,128)(2,1)} fusion(f32[2,8,1024,1024]{2,3,1,0:T(8,128)} %get-tuple-element.128, f32[2,8,1024]{2,1,0:T(8,128)S(1)} %get-tuple-element.127), kind=kLoop, calls=%fused_computation.11 | loop fusion | flops 33554432 | bytes 100728832 | tf_op jit(solution)/shard_map/jvp()/convert_element_type | solution.py:60
  130.4 17.7 %convert_bitcast_fusion.4 = bf16[2,1024,8,128]{1,3,2,0:T(8,128)(2,1)} fusion(bf16[2,8,1024,1024]{2,3,1,0:T(8,128)(2,1)} %divide_convert_fusion, f32[2,1024,3,8,128]{1,4,3,2,0:T(8,128)} %fusion.39), kind=kOutput, calls=%fused_computation.84 | convolution fusion | flops 4297064448 | bytes 41943040 | tf_op jit(solution)/shard_map/jvp(bhqk,bkhd->bqhd)/dot_general | solution.py:61
  208.4 8.4 all-gather.13.cloned.1.call-done
  225.3 20.5 %gather_slots.4 = (bf16[16,8,320,1024]{3,2,1,0:T(8,128)(2,1)}, bf16[16,8,320,1024]{3,2,1,0:T(8,128)(2,1)}, f32[16,1,320,1]{3,2,1,0:T(8,128)}) custom-call(s32[1]{0:T(128)} %bitcast.16.base_ref, s32[128]{0:T(128)} %reshape.352.start_ref, s32[128]{0:T(128)} %reshape.353.count_ref, s32[4]{0:T(128)} %reduce_max.108.most_ref, bf16[2048,1024]{1,0:T(8,128)(2,1)} %fusion.13.x_ref, ...), custom_call_target="tpu_custom_call" | custom-call | flops 8589934592 | bytes 29360128 | tf_op jit(solution)/shard_map/gather_slots/pallas_call | solution.py:196
  251.0 19.0 %gather_slots.5 = (bf16[16,8,320,1024]{3,2,1,0:T(8,128)(2,1)}, bf16[16,8,320,1024]{3,2,1,0:T(8,128)(2,1)}, f32[16,1,320,1]{3,2,1,0:T(8,128)}) custom-call(s32[1]{0:T(128)} %bitcast.16.base_ref, s32[128]{0:T(128)} %reshape.349.start_ref, s32[128]{0:T(128)} %reshape.350.count_ref, ...), custom_call_target="tpu_custom_call", output_to_operand_aliasing={{0}: (8, {}), {1}: (9, {})} | custom-call | flops 8589934592 | bytes 29360128 | tf_op jit(solution)/shard_map/gather_slots/pallas_call | solution.py:196
  280.0 149.1 %expert_own.2 = (bf16[16,2560,1024]{2,1,0:T(8,128)(2,1)}, bf16[16,2560,1024]{2,1,0:T(8,128)(2,1)}, bf16[16,2560,1024]{2,1,0:T(8,128)(2,1)}, bf16[16,2560,1024]{2...) custom-call(bf16[16,2560,1024]{2,1,0:T(8,128)(2,1)} %bitcast.24.refs_0_, ...), custom_call_target="tpu_custom_call", output_to_operand_aliasing={{3}: (1, {})} | custom-call | flops 128849018880 | bytes 247463936 | tf_op jit(solution)/shard_map/expert_own/pallas_call | solution.py:276
  429.1 36.1 %gather_slots.6 = (bf16[16,8,320,1024]{3,2,1,0:T(8,128)(2,1)}, bf16[16,8,320,1024]{3,2,1,0:T(8,128)(2,1)}, f32[16,2,320,1]{3,2,1,0:T(8,128)}) custom-call(s32[1]{0:T(128)} %bitcast.16.base_ref, s32[256]{0:T(256)} %reshape.359.start_ref, s32[256]{0:T(256)} %reshape.360.count_ref, s32[8]{0:T(128)} %reshape.362.most_ref, ...), custom_call_target="tpu_custom_call", output_to_operand_aliasing={{0}: (8, {}), {1}: (9, {})} | custom-call | flops 17179869184 | bytes 58720256 | tf_op jit(solution)/shard_map/gather_slots/pallas_call | solution.py:196
  465.3 148.3 %expert_own.3 = (bf16[16,2560,1024]{2,1,0:T(8,128)(2,1)}, bf16[16,2560,1024]{2,1,0:T(8,128)(2,1)}, bf16[16,2560,1024]{2,1,0:T(8,128)(2,1)}, bf16[16,2560,1024]{2...) custom-call(bf16[16,2560,1024]{2,1,0:T(8,128)(2,1)} %bitcast.31.refs, ...), custom_call_target="tpu_custom_call", output_to_operand_aliasing={{3}: (1, {}), {0}: (6, {}), {1}: (7, {}), {2}: (8, {})} | custom-call | flops 128849018880 | bytes 247463936 | tf_op jit(solution)/shard_map/expert_own/pallas_call | solution.py:276
  613.6 25.0 %combine_slots.2 = (f32[8192,1024]{1,0:T(8,128)}, f32[4,8,16,256]{3,2,1,0:T(8,128)}) custom-call(s32[1]{0:T(128)} %bitcast.11.home_ref, s32[256]{0:T(256)} %reshape.359.start_ref, s32[256]{0:T(256)} %reshape.360.count_ref, s32[16]{0:T(128)} %reshape.361.most_ref, bf16[16,2,320,1024]{3,2,1,0:T(8,128)(2,1)} %bitcast.230, f32[16,2,320,1]{3,2,1,0:T(8,128)} %bitcast.231, ...), custom_call_target="tpu_custom_call" | custom-call | flops 8589934592 | bytes 37748736 | tf_op jit(solution)/shard_map/combine_slots/pallas_call | solution.py:335
  638.6 26.3 %combine_slots.3 = (f32[8192,1024]{1,0:T(8,128)}, f32[4,8,16,256]{3,2,1,0:T(8,128)}) custom-call(s32[1]{0:T(128)} %bitcast.11.home_ref, s32[256]{0:T(256)} %reshape.346.start_ref, s32[256]{0:T(256)} %reshape.347.count_ref, s32[16]{0:T(128)} %reshape.348.most_ref, bf16[16,2,320,1024]{3,2,1,0:T(8,128)(2,1)} %bitcast.193, ...), custom_call_target="tpu_custom_call", output_to_operand_aliasing={{0}: (7, {}), {1}: (8, {})} | custom-call | flops 8589934592 | bytes 37748736 | tf_op jit(solution)/shard_map/combine_slots/pallas_call | solution.py:335
  679.3 65.1 %gather_slots.7 = (bf16[16,8,320,1024]{3,2,1,0:T(8,128)(2,1)}, bf16[16,8,320,1024]{3,2,1,0:T(8,128)(2,1)}) custom-call(s32[1]{0:T(128)} %bitcast.16.base_ref, s32[512]{0:T(512)} %reshape.373.start_ref, s32[512]{0:T(512)} %reshape.374.count_ref, s32[16]{0:T(128)} %reshape.375.most_ref, ...), custom_call_target="tpu_custom_call", output_to_operand_aliasing={{0}: (8, {}), {1}: (9, {})} | custom-call | flops 34359738368 | bytes 117440512 | tf_op jit(solution)/shard_map/gather_slots/pallas_call | solution.py:196
  744.4 157.7 %expert_far.1 = (bf16[16,2560,1024]{2,1,0:T(8,128)(2,1)}, bf16[16,2560,1024]{2,1,0:T(8,128)(2,1)}, bf16[16,2560,1024]{2,1,0:T(8,128)(2,1)}) custom-call(bf16[16,2560,1024]{2,1,0:T(8,128)(2,1)} %bitcast.47.refs_0_, bf16[16,2560,1024]{2,1,0:T(8,128)(2,1)} %bitcast.48.refs_1_, ...), custom_call_target="tpu_custom_call", output_to_operand_aliasing={{0}: (5, {}), {1}: (6, {}), {2}: (7, {})} | custom-call | flops 128849018880 | bytes 394264576 | tf_op jit(solution)/shard_map/expert_far/pallas_call | solution.py:276
  902.1 108.3 %fusion.94 = f32[16,1024,1024]{2,1,0:T(8,128)} fusion(bf16[16,2560,1024]{2,1,0:T(8,128)(2,1)} %get-tuple-element.72, bf16[16,2560,1024]{2,1,0:T(8,128)(2,1)} %bitcast.48.refs_1_), kind=kOutput, calls=%fused_computation.189 | convolution fusion | flops 85899345920 | bytes 234881024 | tf_op jit(solution)/shard_map/ecf,ecd->efd/dot_general | solution.py:439
  1010.5 108.6 %fusion.92 = f32[16,1024,1024]{2,1,0:T(8,128)} fusion(bf16[16,2560,1024]{2,1,0:T(8,128)(2,1)} %bitcast.47.refs_0_, bf16[16,2560,1024]{2,1,0:T(8,128)(2,1)} %get-tuple-element.70), kind=kOutput, calls=%fused_computation.187 | convolution fusion | flops 85899345920 | bytes 234881024 | tf_op jit(solution)/shard_map/ecd,ecf->edf/dot_general | solution.py:440
  1155.7 18.5 %convert_bitcast_fusion.2 = bf16[2,1024,1,8,128]{1,4,3,0,2:T(8,128)(2,1)} fusion(bf16[2,8,1024,1024]{2,3,1,0:T(8,128)(2,1)} %divide_convert_fusion, bf16[2,1024,8,128]{1,3,2,0:T(8,128)(2,1)} %copy.181), kind=kOutput, calls=%fused_computation.79 | convolution fusion | flops 4297064448 | bytes 41943040 | tf_op jit(solution)/shard_map/transpose(jvp(bhqk,bkhd->bqhd))/dot_general | solution.py:61
  1174.2 37.7 %fusion.6 = (f32[2,8,1024]{2,1,0:T(8,128)S(1)}, bf16[2,8,1024,1024]{2,3,1,0:T(8,128)(2,1)}) fusion(f32[2,8,1024,1024]{2,3,1,0:T(8,128)} %get-tuple-element.128, f32[2,8,1024]{2,1,0:T(8,128)S(1)} %copy-done.16, f32[2,1024,3,8,128]{1,4,3,2,0:T(8,128)} %fusion.39, bf16[2,1024,8,128]{1,3,2,0:T(8,128)(2,1)} %copy.181), kind=kOutput, calls=%fused_computation.10 | convolution fusion | flops 4378836992 | bytes 109182976 | tf_op jit(solution)/shard_map/transpose(jvp(bhqk,bkhd->bqhd))/dot_general | solution.py:61
  1212.0 37.5 %convert_bitcast_fusion = f32[2,1024,8,128]{1,3,2,0:T(8,128)} fusion(bf16[2,1024,8,64]{1,3,2,0:T(8,128)(2,1)S(1)} %copy-done.24, bf16[2,1024,8,64]{1,3,2,0:T(8,128)(2,1)} %get-tuple-element.106, f32[2,8,1024,1024]{2,3,1,0:T(8,128)} %get-tuple-element.128, bf16[2,8,1024,1024]{2,3,1,0:T(8,128)(2,1)} %get-tuple-element.135, f32[2,8,1024]{2,1,0:T(8,128)S(1)} %neg.51, ...), kind=kOutput, calls=%fused_computation.55 | convolution fusion | flops 4408213504 | bytes 114425856 | tf_op jit(solution)/shard_map/transpose(jvp(bqhd,bkhd->bhqk))/dot_general | solution.py:58
  1249.5 36.9 %convert_bitcast_fusion.1 = f32[2,1024,8,128]{1,3,2,0:T(8,128)} fusion(bf16[2,1024,8,64]{1,3,2,0:T(8,128)(2,1)} %get-tuple-element.96, bf16[2,1024,8,64]{1,3,2,0:T(8,128)(2,1)} %copy-done.23, f32[2,8,1024,1024]{2,3,1,0:T(8,128)} %get-tuple-element.128, bf16[2,8,1024,1024]{2,3,1,0:T(8,128)(2,1)} %get-tuple-element.135, f32[2,8,1024]{2,1,0:T(8,128)S(1)} %neg.51, ...), kind=kOutput, calls=%fused_computation.56 | convolution fusion | flops 4408213504 | bytes 114425856 | tf_op jit(solution)/shard_map/transpose(jvp(bqhd,bkhd->bhqk))/dot_general | solution.py:58
  1286.4 10.3 multiply_add_fusion.3
  1300.2 8.7 add_bitcast_fusion
  1317.2 17.5 %copy.186 = bf16[2,1024,3,8,128]{4,3,2,1,0:T(8,128)(2,1)} copy(bf16[2,1024,3,8,128]{1,4,3,0,2:T(8,128)(2,1)} %add_convert_fusion) | data formatting | bytes 25165824 | tf_op jit(solution)/shard_map/convert_element_type | solution.py:363
  1334.7 19.3 %convert_element_type.167 = bf16[2048,3072]{1,0:T(8,128)(2,1)} reshape(bf16[2,1024,3,8,128]{4,3,2,1,0:T(8,128)(2,1)} %copy.186) | data formatting | bytes 25165824 | tf_op jit(solution)/shard_map/convert_element_type | solution.py:363
  1354.0 19.6 %fusion.91 = f32[1024,3072]{1,0:T(8,128)} fusion(bf16[2048,1024]{1,0:T(8,128)(2,1)} %bitcast.207, bf16[2048,3072]{1,0:T(8,128)(2,1)} %convert_element_type.167), kind=kOutput, calls=%fused_computation.186 | convolution fusion | flops 12884901888 | bytes 29360128 | tf_op jit(solution)/shard_map/td,te->de/dot_general | solution.py:364
  1373.6 108.2 %fusion.93 = f32[16,1024,1024]{2,1,0:T(8,128)} fusion(bf16[16,2560,1024]{2,1,0:T(8,128)(2,1)} %bitcast.47.refs_0_, bf16[16,2560,1024]{2,1,0:T(8,128)(2,1)} %get-tuple-element.71), kind=kOutput, calls=%fused_computation.188 | convolution fusion | flops 85899345920 | bytes 234881024 | tf_op jit(solution)/shard_map/ecd,ecf->edf/dot_general | solution.py:441
  1481.9 20.4 %fusion.31 = (f32[1024]{0:T(1024)S(1)}, f32[2048]{0:T(1024)S(1)}, f32[2048,1024]{1,0:T(8,128)}) fusion(bf16[2,1024,1024]{2,1,0:T(8,128)(2,1)S(1)} %copy-done, f32[2048]{0:T(1024)S(1)} %bitcast.228, f32[1024]{0:T(1024)S(1)} %copy-done.52, bf16[2048,3072]{1,0:T(8,128)(2,1)} %convert_element_type.167, bf16[1024,3072]{1,0:T(8,128)(2,1)} %param.16), kind=kOutput, calls=%fused_computation.54 | convolution fusion | flops 12899578880 | bytes 31481856 | tf_op jit(solution)/shard_map/te,de->td/dot_general | solution.py:365
  1502.3 26.1 %all-reduce.7 = (f32[1024]{0:T(1024)}, f32[1024]{0:T(1024)}) all-reduce(f32[1024]{0:T(1024)S(1)} %get-tuple-element.75, f32[1024]{0:T(1024)S(1)} %copy-done.56), channel_id=1, replica_groups=mesh['dp'=2,'ep'=4] {'dp','ep'}, use_global_device_ids=true, to_apply=%region_29.30 | all-reduce | flops 2048 | bytes 16384 | tf_op jit(solution)/shard_map/psum | solution.py:446
  1528.4 8.7 fusion.28
  1537.2 50.0 %all-reduce.11.cloned.1.call-done = (f32[1024,3072]{1,0:T(8,128)}, f32[1024,1024]{1,0:T(8,128)}, f32[1024,64]{0,1:T(8,128)}) async-done(((f32[1024,3072]{1,0:T(8,128)}, f32[1024,1024]{1,0:T(8,128)}, f32[1024,64]{0,1:T(8,128)}), (f32[1024,3072]{1,0:T(8,128)}, f32[1024,1024]{1,0:T(8,128)}, f32[1024,64]{0,1:T(8,128)})) %all-reduce.11.cloned.1.call-update) | async-done | bytes 17039376 | tf_op jit(solution)/shard_map/psum | solution.py:446
  1587.1 11.1 copy.260
  (253 shorter events, 175.9 us)
Async XLA Ops:
  7.2 168.8 %all-gather.7.cloned.1.call-start = ((), (), s32[]{:S(2)}) async-start(), calls=%async_computation.2 | async-start | bytes 37748736 | tf_op jit(solution)/shard_map/all_gather | solution.py:395
  7.9 184.5 %all-gather.11.cloned.1.call-start = ((), (), s32[]{:S(2)}) async-start(), calls=%async_computation.5 | async-start | bytes 2359296 | tf_op jit(solution)/shard_map/all_gather | solution.py:394
  9.7 207.1 %all-gather.13.cloned.1.call-start = ((), (), s32[]{:S(2)}) async-start(), calls=%async_computation.6 | async-start | bytes 2359296 | tf_op jit(solution)/shard_map/all_gather | solution.py:411
  11.7 14.8 copy-start.51
  17.7 36.9 %copy-start.19 = (f32[1024,64]{0,1:T(8,128)}, f32[1024,64]{0,1:T(8,128)S(1)}, u32[]{:S(2)}) copy-start(f32[1024,64]{0,1:T(8,128)S(1)} %get-tuple-element.125) | copy-start | bytes 786436
  17.7 36.9 %copy-start.21 = (f32[1024,64]{0,1:T(8,128)}, f32[1024,64]{0,1:T(8,128)S(1)}, u32[]{:S(2)}) copy-start(f32[1024,64]{0,1:T(8,128)S(1)} %get-tuple-element.126) | copy-start | bytes 786436
  59.5 38.0 %copy-start.23 = (bf16[2,1024,8,64]{1,3,2,0:T(8,128)(2,1)}, bf16[2,1024,8,64]{1,3,2,0:T(8,128)(2,1)S(1)}, u32[]{:S(2)}) copy-start(bf16[2,1024,8,64]{1,3,2,0:T(8,128)(2,1)S(1)} %get-tuple-element.95) | copy-start | bytes 6291460
  97.5 32.9 %copy-start.39 = (f32[2,8,1024]{2,1,0:T(8,128)}, f32[2,8,1024]{2,1,0:T(8,128)S(1)}, u32[]{:S(2)}) copy-start(f32[2,8,1024]{2,1,0:T(8,128)S(1)} %get-tuple-element.127) | copy-start | bytes 196612
  175.9 253.3 %all-gather.9.cloned.1.call-start = ((), (), s32[]{:S(2)}) async-start(), calls=%async_computation.3 | async-start | bytes 37748736 | tf_op jit(solution)/shard_map/all_gather | solution.py:413
  176.4 948.5 %reduce-scatter.2.cloned.1.call-start = ((), (), s32[]{:S(2)}) async-start(), calls=%async_computation.4 | async-start | bytes 41943040 | tf_op jit(solution)/shard_map/reduce_scatter | solution.py:431
  176.9 74.0 %collective-permute-start.1 = (bf16[2048,1024]{1,0:T(8,128)(2,1)}, bf16[2048,1024]{1,0:T(8,128)(2,1)}, u32[]{:S(2)}, u32[]{:S(2)}) collective-permute-start(bf16[2048,1024]{1,0:T(8,128)(2,1)} %bitcast.196), channel_id=1, source_target_pairs={{0,1},{1,0},{2,3},{3,2},{4,5},{5,4},{6,7},{7,6}} | collective-permute-start | bytes 12582920 | tf_op jit(solution)/shard_map/ppermute | solution.py:396
  177.8 7.6 collective-permute-start.2
  177.8 73.1 %collective-permute-start = (bf16[2048,1024]{1,0:T(8,128)(2,1)}, bf16[2048,1024]{1,0:T(8,128)(2,1)}, u32[]{:S(2)}, u32[]{:S(2)}) collective-permute-start(bf16[2048,1024]{1,0:T(8,128)(2,1)} %fusion.13.x_ref), channel_id=1, source_target_pairs={{0,1},{1,0},{2,3},{3,2},{4,5},{5,4},{6,7},{7,6}} | collective-permute-start | bytes 12582920 | tf_op jit(solution)/shard_map/ppermute | solution.py:405
  671.5 447.6 %all-to-all-start = ((f32[4,8,16,256]{3,2,1,0:T(8,128)}), f32[4,8,16,256]{3,2,1,0:T(8,128)}, u32[]{:S(2)}, u32[]{:S(2)}) async-start(f32[4,8,16,256]{3,2,1,0:T(8,128)} %get-tuple-element.62), calls=%async_computation.1 | async-start | bytes 1048576 | tf_op jit(solution)/shard_map/all_to_all | solution.py:432
  679.3 907.9 %all-reduce.11.cloned.1.call-start = ((), (), s32[]{:S(2)}) async-start(), calls=%async_computation.7 | async-start | bytes 34078720 | tf_op jit(solution)/shard_map/psum | solution.py:446
  1010.4 110.3 %copy-start.12 = (f32[2048,64]{0,1:T(8,128)S(1)}, f32[2048,64]{0,1:T(8,128)}, u32[]{:S(2)}) copy-start(f32[2048,64]{0,1:T(8,128)} %copy-done.11) | copy-start | bytes 1572868
  1010.4 110.3 %copy-start.4 = (f32[2048,64]{0,1:T(8,128)S(1)}, f32[2048,64]{0,1:T(8,128)}, u32[]{:S(2)}) copy-start(f32[2048,64]{0,1:T(8,128)} %copy-done.3) | copy-start | bytes 1572868
  1010.4 110.3 %copy-start.9 = (f32[2048,64]{0,1:T(8,128)S(1)}, f32[2048,64]{0,1:T(8,128)}, u32[]{:S(2)}) copy-start(f32[2048,64]{0,1:T(8,128)} %copy-done.8) | copy-start | bytes 1572868
  1010.4 110.3 %copy-start.37 = (f32[2048]{0:T(1024)S(1)}, f32[2048]{0:T(1024)}, u32[]{:S(2)}) copy-start(f32[2048]{0:T(1024)} %copy-done.36) | copy-start | bytes 24580
  1010.5 110.3 %copy-start.43 = (f32[2048]{0:T(1024)S(1)}, f32[2048]{0:T(1024)}, u32[]{:S(2)}) copy-start(f32[2048]{0:T(1024)} %copy-done.42) | copy-start | bytes 24580
  1010.5 110.3 %copy-start.45 = (f32[2048]{0:T(1024)S(1)}, f32[2048]{0:T(1024)}, u32[]{:S(2)}) copy-start(f32[2048]{0:T(1024)} %copy-done.44) | copy-start | bytes 24580
  1155.6 18.5 %copy-start.16 = (f32[2,8,1024]{2,1,0:T(8,128)S(1)}, f32[2,8,1024]{2,1,0:T(8,128)}, u32[]{:S(2)}) copy-start(f32[2,8,1024]{2,1,0:T(8,128)} %multiply_divide_fusion.1) | copy-start | bytes 196612
  1174.2 37.8 %copy-start.24 = (bf16[2,1024,8,64]{1,3,2,0:T(8,128)(2,1)S(1)}, bf16[2,1024,8,64]{1,3,2,0:T(8,128)(2,1)}, u32[]{:S(2)}) copy-start(bf16[2,1024,8,64]{1,3,2,0:T(8,128)(2,1)} %get-tuple-element.105) | copy-start | bytes 6291460
  1174.2 37.8 %copy-start.27 = (pred[1024,1024]{0,1:T(8,128)(4,1)S(1)}, pred[1024,1024]{0,1:T(8,128)(4,1)}, u32[]{:S(2)}) copy-start(pred[1024,1024]{0,1:T(8,128)(4,1)} %iota_compare_fusion.1) | copy-start | bytes 3145732
  1174.2 37.8 %copy-start.41 = (f32[2,8,1024]{2,1,0:T(8,128)S(1)}, f32[2,8,1024]{2,1,0:T(8,128)}, u32[]{:S(2)}) copy-start(f32[2,8,1024]{2,1,0:T(8,128)} %copy-done.39) | copy-start | bytes 196612
  1249.5 36.9 %copy-start.20 = (f32[1024,64]{0,1:T(8,128)S(1)}, f32[1024,64]{0,1:T(8,128)}, u32[]{:S(2)}) copy-start(f32[1024,64]{0,1:T(8,128)} %copy-done.19) | copy-start | bytes 786436
  1249.5 36.9 %copy-start.22 = (f32[1024,64]{0,1:T(8,128)S(1)}, f32[1024,64]{0,1:T(8,128)}, u32[]{:S(2)}) copy-start(f32[1024,64]{0,1:T(8,128)} %copy-done.21) | copy-start | bytes 786436
  1373.6 108.3 %copy-start = (bf16[2,1024,1024]{2,1,0:T(8,128)(2,1)S(1)}, bf16[2,1024,1024]{2,1,0:T(8,128)(2,1)}, u32[]{:S(2)}) copy-start(bf16[2,1024,1024]{2,1,0:T(8,128)(2,1)} %param.11) | copy-start | bytes 12582916
  1373.6 108.3 %copy-start.52 = (f32[1024]{0:T(1024)S(1)}, f32[1024]{0:T(1024)}, u32[]{:S(2)}) copy-start(f32[1024]{0:T(1024)} %copy-done.51) | copy-start | bytes 12292
  1373.6 108.3 %copy-start.54 = (f32[1,8,2,128]{3,1,2,0:T(8,128)S(1)}, f32[1,8,2,128]{3,1,2,0:T(8,128)}, u32[]{:S(2)}) copy-start(f32[1,8,2,128]{3,1,2,0:T(8,128)} %copy.240) | copy-start | bytes 24580
  1481.9 20.4 %copy-start.56 = (f32[1024]{0:T(1024)S(1)}, f32[1024]{0:T(1024)}, u32[]{:S(2)}) copy-start(f32[1024]{0:T(1024)} %get-tuple-element.73) | copy-start | bytes 12292
  1481.9 46.5 %copy-start.55 = (f32[2048]{0:T(1024)S(1)}, f32[2048]{0:T(1024)}, u32[]{:S(2)}) copy-start(f32[2048]{0:T(1024)} %multiply_multiply_fusion) | copy-start | bytes 24580
  (37 other events, 160.6 us)
Sparse Core Ops, SparseCore 0:
  9.8 158.0 all-gather.6
  170.3 22.0 all-gather.10
  194.8 21.9 all-gather.12
  218.5 155.2 all-gather.8
  665.1 231.0 reduce-scatter.1
  1373.7 213.3 all-reduce.10

commit v3 on v2

--- a/solution.py
+++ b/solution.py
@@ -13,6 +13,7 @@
 TOK_BLOCK = 256
 WIN = 64
 ALIGN = 16
+GROUP = 4
 VMEM_MAX = 64 * 1024 * 1024 - 65536
 
 
@@ -35,31 +36,163 @@
     return d_x, d_gain
 
 
-def rope_rotate(head_vals):
-    seq_len = head_vals.shape[1]
-    half_dim = head_vals.shape[-1] // 2
+def dot_nn(left, right):
+    return jnp.dot(left, right, preferred_element_type=jnp.float32)
+
+
+def dot_nt(left, right):
+    return lax.dot_general(left, right, (((1,), (1,)), ((), ())), preferred_element_type=jnp.float32)
+
+
+def rope_tables(seq_len):
+    half_dim = HEAD_DIM // 2
     inv_freq = ROPE_BASE ** (-jnp.arange(half_dim, dtype=jnp.float32) / half_dim)
     angles = jnp.arange(seq_len, dtype=jnp.float32)[:, None] * inv_freq[None, :]
-    cos_b = jnp.cos(angles)[None, :, None, :]
-    sin_b = jnp.sin(angles)[None, :, None, :]
-    lower_half = head_vals[..., :half_dim]
-    upper_half = head_vals[..., half_dim:]
-    return jnp.concatenate([lower_half * cos_b - upper_half * sin_b, upper_half * cos_b + lower_half * sin_b], axis=-1)
-
-
-def attention_core(qkv_rows, num_seqs):
-    num_tokens = qkv_rows.shape[0]
-    seq_len = num_tokens // num_seqs
-    model_width = qkv_rows.shape[1] // 3
-    qkv_heads = qkv_rows.reshape(num_seqs, seq_len, 3, model_width // HEAD_DIM, HEAD_DIM)
-    query_rot = rope_rotate(qkv_heads[:, :, 0]).astype(jnp.bfloat16)
-    key_rot = rope_rotate(qkv_heads[:, :, 1]).astype(jnp.bfloat16)
-    value_h = qkv_heads[:, :, 2].astype(jnp.bfloat16)
-    scores = jnp.einsum('bqhd,bkhd->bhqk', query_rot, key_rot, preferred_element_type=jnp.float32) * HEAD_DIM ** -0.5
-    causal = jnp.arange(seq_len)[:, None] >= jnp.arange(seq_len)[None, :]
-    attn_probs = jax.nn.softmax(jnp.where(causal, scores, -1e30), axis=-1).astype(jnp.bfloat16)
-    context = jnp.einsum('bhqk,bkhd->bqhd', attn_probs, value_h, preferred_element_type=jnp.float32)
-    return context.astype(jnp.bfloat16).reshape(num_tokens, model_width)
+    cos_b, sin_b = jnp.cos(angles), jnp.sin(angles)
+    return jnp.concatenate([cos_b, cos_b], axis=1), jnp.concatenate([-sin_b, sin_b], axis=1)
+
+
+def qkv_kernel(x_ref, gain_ref, w_ref, cos_ref, sin_ref, normed_ref, qkv_ref, *, rotated, chunk):
+    x_f32 = x_ref[...].astype(jnp.float32)
+    inv_rms = lax.rsqrt(jnp.mean(x_f32 * x_f32, axis=-1, keepdims=True) + EPS)
+    normed_ref[...] = (x_f32 * inv_rms * gain_ref[...]).astype(jnp.bfloat16)
+    for c in range(0, w_ref.shape[1], chunk):
+        acc = dot_nn(normed_ref[...], w_ref[:, c:c + chunk])
+        for h in range(0, chunk, HEAD_DIM):
+            head = acc[:, h:h + HEAD_DIM]
+            if c + h < rotated:
+                head = head * cos_ref[...] + pltpu.roll(head, HEAD_DIM // 2, 1) * sin_ref[...]
+            qkv_ref[:, c + h:c + h + HEAD_DIM] = head.astype(jnp.bfloat16)
+
+
+def qkv_project(x_rows, gain_vec, w_qkv, cos_t, sin_t):
+    num_tokens, width = x_rows.shape
+    seq_len = cos_t.shape[0]
+    tile = min(512, seq_len)
+    per_seq = seq_len // tile
+    row_spec = pl.BlockSpec((tile, width), lambda r: (r, 0))
+    table_spec = pl.BlockSpec((tile, HEAD_DIM), lambda r: (lax.rem(r, per_seq), 0))
+    return pl.pallas_call(
+        functools.partial(qkv_kernel, rotated=2 * width, chunk=256),
+        out_shape=[jax.ShapeDtypeStruct((num_tokens, width), jnp.bfloat16), jax.ShapeDtypeStruct((num_tokens, 3 * width), jnp.bfloat16)],
+        grid=(num_tokens // tile,),
+        in_specs=[row_spec, pl.BlockSpec((1, width), lambda r: (0, 0)), pl.BlockSpec((width, 3 * width), lambda r: (0, 0)), table_spec, table_spec],
+        out_specs=[row_spec, pl.BlockSpec((tile, 3 * width), lambda r: (r, 0))],
+        compiler_params=pltpu.CompilerParams(vmem_limit_bytes=VMEM_MAX, dimension_semantics=('arbitrary',)),
+        cost_estimate=pl.CostEstimate(flops=6 * num_tokens * width * width, bytes_accessed=2 * width * (5 * num_tokens + 3 * width), transcendentals=num_tokens),
+        name='qkv_project',
+    )(x_rows, gain_vec.astype(jnp.float32)[None, :], w_qkv, cos_t, sin_t)
+
+
+def attend_kernel(q_ref, k_ref, v_ref, ctx_ref, *, block):
+    seq_len = q_ref.shape[0]
+    diag = lax.broadcasted_iota(jnp.int32, (block, block), 0) >= lax.broadcasted_iota(jnp.int32, (block, block), 1)
+    for start in range(0, seq_len, block):
+        stop = start + block
+        scores = dot_nt(q_ref[start:stop, :], k_ref[:stop, :]) * HEAD_DIM ** -0.5
+        last = jnp.where(diag, scores[:, start:], -1e30)
+        scores = last if start == 0 else jnp.concatenate([scores[:, :start], last], axis=1)
+        raised = jnp.exp(scores - jnp.max(scores, axis=1, keepdims=True))
+        probs = (raised * (1.0 / jnp.sum(raised, axis=1, keepdims=True))).astype(jnp.bfloat16)
+        ctx_ref[start:stop, :] = dot_nn(probs, v_ref[:stop, :]).astype(jnp.bfloat16)
+
+
+def head_spec(seq_len, offset):
+    return pl.BlockSpec((seq_len, HEAD_DIM), lambda s, h: (s, h + offset))
+
+
+def attend(qkv_rot, num_seqs):
+    num_tokens, width = qkv_rot.shape[0], qkv_rot.shape[1] // 3
+    seq_len, heads = num_tokens // num_seqs, width // HEAD_DIM
+    return pl.pallas_call(
+        functools.partial(attend_kernel, block=min(256, seq_len)),
+        out_shape=jax.ShapeDtypeStruct((num_tokens, width), jnp.bfloat16),
+        grid=(num_seqs, heads),
+        in_specs=[head_spec(seq_len, 0), head_spec(seq_len, heads), head_spec(seq_len, 2 * heads)],
+        out_specs=head_spec(seq_len, 0),
+        compiler_params=pltpu.CompilerParams(vmem_limit_bytes=VMEM_MAX, dimension_semantics=('arbitrary', 'arbitrary')),
+        cost_estimate=pl.CostEstimate(flops=4 * num_tokens * seq_len * width, bytes_accessed=8 * num_tokens * width, transcendentals=num_tokens * seq_len * heads),
+        name='attend',
+    )(qkv_rot, qkv_rot, qkv_rot)
+
+
+def attend_back_kernel(q_ref, k_ref, v_ref, dctx_ref, cos_ref, sin_ref, out_ref, stage, d_key, d_val, sems, *, block, heads):
+    seq, head = pl.program_id(0), pl.program_id(1)
+    step = seq * heads + head
+    slot = lax.rem(step, 2)
+    seq_len = q_ref.shape[0]
+    scale = HEAD_DIM ** -0.5
+    causal = lax.broadcasted_iota(jnp.int32, (block, block), 0) <= lax.broadcasted_iota(jnp.int32, (block, block), 1)
+
+    def copies(at_step, at_slot):
+        at_seq, at_head = at_step // heads, lax.rem(at_step, heads)
+        rows = pl.ds(pl.multiple_of(at_seq * seq_len, seq_len), seq_len)
+        return [pltpu.make_async_copy(stage.at[at_slot, i],
+                                      out_ref.at[rows, pl.ds(pl.multiple_of((at_head + i * heads) * HEAD_DIM, HEAD_DIM), HEAD_DIM)],
+                                      sems.at[at_slot, i]) for i in range(3)]
+
+    @pl.when(step >= 2)
+    def _():
+        for copy in copies(step - 2, slot):
+            copy.wait()
+
+    def unrotate(grad):
+        grad = grad.astype(jnp.bfloat16).astype(jnp.float32)
+        return lambda cos, sin: (grad * cos + pltpu.roll(grad * sin, HEAD_DIM // 2, 1)).astype(jnp.bfloat16)
+
+    key_t = jnp.transpose(k_ref[...])
+    for start in range(0, seq_len, block):
+        stop = start + block
+        query, d_ctx = q_ref[start:stop, :], dctx_ref[start:stop, :]
+        scores = dot_nt(k_ref[:stop, :], query) * scale
+        last = jnp.where(causal, scores[start:, :], -1e30)
+        scores = last if start == 0 else jnp.concatenate([scores[:start, :], last], axis=0)
+        raised = jnp.exp(scores - jnp.max(scores, axis=0, keepdims=True))
+        probs = raised * (1.0 / jnp.sum(raised, axis=0, keepdims=True))
+        d_probs = dot_nt(v_ref[:stop, :], d_ctx).astype(jnp.bfloat16).astype(jnp.float32)
+        mean_d = jnp.sum(d_probs * probs, axis=0, keepdims=True)
+        d_scores = (probs * (d_probs - mean_d) * scale).astype(jnp.bfloat16)
+        d_v = dot_nn(probs.astype(jnp.bfloat16), d_ctx)
+        d_k = dot_nn(d_scores, query)
+        if start == 0:
+            d_val[:stop, :] = d_v
+            d_key[:stop, :] = d_k
+        else:
+            d_val[:start, :] += d_v[:start]
+            d_key[:start, :] += d_k[:start]
+            d_val[start:stop, :] = d_v[start:]
+            d_key[start:stop, :] = d_k[start:]
+        d_q = jnp.transpose(dot_nn(key_t[:, :stop], d_scores))
+        stage[slot, 0, start:stop, :] = unrotate(d_q)(cos_ref[start:stop, :], sin_ref[start:stop, :])
+    stage[slot, 1] = unrotate(d_key[...])(cos_ref[...], sin_ref[...])
+    stage[slot, 2] = d_val[...].astype(jnp.bfloat16)
+    for copy in copies(step, slot):
+        copy.start()
+
+    @pl.when(step == pl.num_programs(0) * heads - 1)
+    def _():
+        for copy in copies(step - 1, 1 - slot):
+            copy.wait()
+        for copy in copies(step, slot):
+            copy.wait()
+
+
+def attend_back(qkv_rot, d_context, cos_t, sin_t, num_seqs):
+    num_tokens, width = d_context.shape
+    seq_len, heads = num_tokens // num_seqs, width // HEAD_DIM
+    table_spec = pl.BlockSpec((seq_len, HEAD_DIM), lambda s, h: (0, 0))
+    return pl.pallas_call(
+        functools.partial(attend_back_kernel, block=min(256, seq_len), heads=heads),
+        out_shape=jax.ShapeDtypeStruct((num_tokens, 3 * width), jnp.bfloat16),
+        grid=(num_seqs, heads),
+        in_specs=[head_spec(seq_len, 0), head_spec(seq_len, heads), head_spec(seq_len, 2 * heads), head_spec(seq_len, 0), table_spec, table_spec],
+        out_specs=pl.BlockSpec(memory_space=pl.ANY),
+        scratch_shapes=[pltpu.VMEM((2, 3, seq_len, HEAD_DIM), jnp.bfloat16), pltpu.VMEM((seq_len, HEAD_DIM), jnp.float32),
+                        pltpu.VMEM((seq_len, HEAD_DIM), jnp.float32), pltpu.SemaphoreType.DMA((2, 3))],
+        compiler_params=pltpu.CompilerParams(vmem_limit_bytes=VMEM_MAX, dimension_semantics=('arbitrary', 'arbitrary')),
+        cost_estimate=pl.CostEstimate(flops=10 * num_tokens * seq_len * width, bytes_accessed=14 * num_tokens * width, transcendentals=num_tokens * seq_len * heads),
+        name='attend_back',
+    )(qkv_rot, qkv_rot, qkv_rot, d_context, cos_t, sin_t)
 
 
 def choice_mask(idx_rows, num_experts):
@@ -96,7 +229,9 @@
     end = jnp.minimum((before + totals).astype(jnp.int32), capacity)
     win_start = jnp.minimum(begin // ALIGN * ALIGN, capacity - WIN)
     win_count = jnp.maximum((end - win_start + WIN - 1) // WIN, 1)
-    return jnp.transpose(slot_of, (0, 2, 1, 3)), win_start, win_count
+    most_group = jnp.max(win_count.reshape(num_dev, local_experts // GROUP, GROUP * blocks), axis=2)
+    most_block = jnp.max(win_count, axis=1)
+    return jnp.transpose(slot_of, (0, 2, 1, 3)), win_start.reshape(-1), win_count.reshape(-1), most_group.reshape(-1), most_block.reshape(-1)
 
 
 def expand_routes(idx_t, values_t, first_expert, local_experts):
@@ -106,10 +241,10 @@
     return jnp.transpose(dense.reshape(num_dev, local_experts, num_tokens // TOK_BLOCK, TOK_BLOCK), (0, 2, 1, 3))
 
 
-def gather_kernel(base_ref, start_ref, count_ref, most_ref, x_ref, dy_ref, slot_ref, gate_ref, *rest, blocks, capacity, group, scaled):
-    s_ref, dyr_ref = rest[-3:-1] if not scaled else rest[-2:]
+def gather_kernel(base_ref, start_ref, count_ref, most_ref, x_ref, dy_ref, slot_ref, gate_ref, *rest, blocks, capacity, group, scaled, dev_from):
+    s_ref, dyr_ref = rest[-2:] if scaled else rest[-3:-1]
     g_ref = None if scaled else rest[-1]
-    dev, part = pl.program_id(0), pl.program_id(1)
+    dev, part = pl.program_id(0) + dev_from, pl.program_id(1)
     experts = group * pl.num_programs(1)
     s_ref[...] = jnp.zeros_like(s_ref)
     dyr_ref[...] = jnp.zeros_like(dyr_ref)
@@ -162,44 +297,46 @@
                     dy_rows = jnp.dot(pick, dy_ref[tokens, :], preferred_element_type=jnp.float32)
                     deposit(i, first, s_rows, dy_rows, gate_col)
                     return inner
+
                 return lax.fori_loop(1, count_ref[at(i, blk)], extra, carry)
+
             lax.fori_loop(0, blocks, per_block, 0)
 
 
-def gather_slots(base_dev, routes, dev_from, num_dev, x_table, dy_table, filled, total_dev, capacity, scaled, from_all):
-    slot_of, win_start, win_count, gate_of = (r[dev_from:dev_from + num_dev] for r in routes)
-    _, blocks, experts, _ = slot_of.shape
+def gather_slots(base_dev, routes, dev_from, num_dev, gate_of, x_table, dy_table, filled, own_dev, capacity, scaled, from_all):
+    slot_of, win_start, win_count, most, _ = routes
+    total_dev, blocks, experts, _ = slot_of.shape
     width = x_table.shape[1]
     num_tokens = blocks * TOK_BLOCK
-    group = 4
-    most = jnp.max(win_count.reshape(num_dev, experts // group, group * blocks), axis=2).reshape(-1)
+    group = GROUP
 
     def table_map(d, p, base_ref, *_):
         return (lax.bitwise_xor(d + dev_from, base_ref[0]) if from_all else 0, 0)
 
-    def route_map(d, p, *_):
+    def slot_map(d, p, *_):
+        return (d + dev_from, 0, 0, 0)
+
+    def gate_map(d, p, *_):
         return (d, 0, 0, 0)
 
     def out_map(d, p, *_):
         return (p, d + dev_from, 0, 0)
-
-    def gate_map(d, p, *_):
-        return (p, d, 0, 0)
 
     rows_shape = jax.ShapeDtypeStruct((experts, total_dev, capacity, width), jnp.bfloat16)
     row_spec = pl.BlockSpec((group, 1, capacity, width), out_map)
     out_shape, out_specs = [rows_shape, rows_shape], [row_spec, row_spec]
     if not scaled:
-        out_shape.append(jax.ShapeDtypeStruct((experts, num_dev, capacity, 1), jnp.float32))
-        out_specs.append(pl.BlockSpec((group, 1, capacity, 1), gate_map))
+        out_shape.append(jax.ShapeDtypeStruct((experts, own_dev, capacity, 1), jnp.float32))
+        out_specs.append(pl.BlockSpec((group, 1, capacity, 1), out_map))
     held = () if filled is None else tuple(filled)
+    route_block = (1, blocks, experts, TOK_BLOCK)
     return pl.pallas_call(
-        functools.partial(gather_kernel, blocks=blocks, capacity=capacity, group=group, scaled=scaled),
+        functools.partial(gather_kernel, blocks=blocks, capacity=capacity, group=group, scaled=scaled, dev_from=dev_from),
         out_shape=out_shape,
         grid_spec=pltpu.PrefetchScalarGridSpec(
             num_scalar_prefetch=4, grid=(num_dev, experts // group),
             in_specs=[pl.BlockSpec((num_tokens, width), table_map), pl.BlockSpec((num_tokens, width), table_map),
-                      pl.BlockSpec((1, blocks, experts, TOK_BLOCK), route_map), pl.BlockSpec((1, blocks, experts, TOK_BLOCK), route_map)]
+                      pl.BlockSpec(route_block, slot_map), pl.BlockSpec(route_block, gate_map)]
                      + [pl.BlockSpec(memory_space=pl.ANY)] * len(held),
             out_specs=out_specs),
         input_output_aliases={8 + i: i for i in range(len(held))},
@@ -207,15 +344,7 @@
         cost_estimate=pl.CostEstimate(flops=4 * num_dev * blocks * experts * WIN * TOK_BLOCK * width,
                                       bytes_accessed=4 * num_dev * (num_tokens + experts * capacity) * width, transcendentals=0),
         name='gather_slots',
-    )(base_dev, win_start.reshape(-1), win_count.reshape(-1), most, x_table, dy_table, slot_of, gate_of, *held)
-
-
-def dot_nn(left, right):
-    return jnp.dot(left, right, preferred_element_type=jnp.float32)
-
-
-def dot_nt(left, right):
-    return lax.dot_general(left, right, (((1,), (1,)), ((), ())), preferred_element_type=jnp.float32)
+    )(base_dev, win_start, win_count, most, x_table, dy_table, slot_of, gate_of, *held)
 
 
 def expert_kernel(*refs, own, chunk, held):
@@ -252,7 +381,8 @@
     experts, rows, width = s_rows.shape
     row_spec = pl.BlockSpec((1, tile, width), lambda e, r: (e, first_tile + r, 0))
     near_spec = pl.BlockSpec((1, tile, width), lambda e, r: (e, r, 0))
-    col_spec = pl.BlockSpec((1, tile, 1), lambda e, r: (e, r, 0))
+    col_spec = pl.BlockSpec((1, tile, 1), lambda e, r: (e, first_tile + r, 0))
+    near_col_spec = pl.BlockSpec((1, tile, 1), lambda e, r: (e, r, 0))
     w_spec = pl.BlockSpec((1, width, width), lambda e, r: (e, 0, 0))
     full = jax.ShapeDtypeStruct((experts, rows, width), jnp.bfloat16)
     out_shape, out_specs = [full] * 3, [row_spec] * 3
@@ -263,7 +393,7 @@
         in_specs.append(col_spec)
         out_shape += [full, jax.ShapeDtypeStruct((experts, num_tiles * tile, width), jnp.bfloat16),
                       jax.ShapeDtypeStruct((experts, num_tiles * tile, 1), jnp.float32)]
-        out_specs += [row_spec, near_spec, col_spec]
+        out_specs += [row_spec, near_spec, near_col_spec]
         aliases[1] = 3
     args += [w_gate, w_up, w_down]
     in_specs += [w_spec] * 3
@@ -285,9 +415,9 @@
     )(*args)
 
 
-def combine_kernel(home_ref, start_ref, count_ref, most_ref, ds_ref, dg_ref, slot_ref, *rest, experts, blocks, capacity):
+def combine_kernel(home_ref, start_ref, count_ref, most_ref, ds_ref, dg_ref, slot_ref, *rest, experts, blocks, capacity, dev_from):
     out_ref, dgt_ref = rest[-2:]
-    dev, blk = pl.program_id(0), pl.program_id(1)
+    dev, blk = pl.program_id(0) + dev_from, pl.program_id(1)
     row_iota = lax.broadcasted_iota(jnp.int32, (WIN, TOK_BLOCK), 0)
 
     def window(e, first, floor=None):
@@ -318,29 +448,29 @@
                 out_ref[...] += spread(pick, rows)
                 dgt_ref[0, 0, e:e + 1, :] += gate_row
                 return carry
+
             lax.fori_loop(1, count_ref[at], extra, 0)
 
 
 def combine_slots(home, routes, dev_from, num_dev, total_dev, d_slots, d_gate_slots, filled):
-    slot_of, win_start, win_count = (r[dev_from:dev_from + num_dev] for r in routes[:3])
+    slot_of, win_start, win_count, _, most = routes
     experts, _, capacity, width = d_slots.shape
     blocks = slot_of.shape[1]
     num_tokens = blocks * TOK_BLOCK
-    most = jnp.max(win_count, axis=1).reshape(-1)
 
     def home_of(d, home_ref):
         return lax.bitwise_xor(d + dev_from, home_ref[0])
 
     held = () if filled is None else tuple(filled)
     return pl.pallas_call(
-        functools.partial(combine_kernel, experts=experts, blocks=blocks, capacity=capacity),
+        functools.partial(combine_kernel, experts=experts, blocks=blocks, capacity=capacity, dev_from=dev_from),
         out_shape=[jax.ShapeDtypeStruct((total_dev * num_tokens, width), jnp.float32),
                    jax.ShapeDtypeStruct((total_dev, blocks, experts, TOK_BLOCK), jnp.float32)],
         grid_spec=pltpu.PrefetchScalarGridSpec(
             num_scalar_prefetch=4, grid=(num_dev, blocks),
             in_specs=[pl.BlockSpec((experts, 1, capacity, width), lambda d, b, *_: (0, d, 0, 0)),
                       pl.BlockSpec((experts, 1, capacity, 1), lambda d, b, *_: (0, d, 0, 0)),
-                      pl.BlockSpec((1, 1, experts, TOK_BLOCK), lambda d, b, *_: (d, b, 0, 0))]
+                      pl.BlockSpec((1, 1, experts, TOK_BLOCK), lambda d, b, *_: (d + dev_from, b, 0, 0))]
                      + [pl.BlockSpec(memory_space=pl.ANY)] * len(held),
             out_specs=[pl.BlockSpec((TOK_BLOCK, width), lambda d, b, home_ref, *_: (home_of(d, home_ref) * blocks + b, 0)),
                        pl.BlockSpec((1, 1, experts, TOK_BLOCK), lambda d, b, home_ref, *_: (home_of(d, home_ref), b, 0, 0))]),
@@ -349,23 +479,24 @@
         cost_estimate=pl.CostEstimate(flops=2 * num_dev * blocks * experts * WIN * TOK_BLOCK * width,
                                       bytes_accessed=2 * num_dev * (2 * num_tokens + experts * capacity) * width, transcendentals=0),
         name='combine_slots',
-    )(home, win_start.reshape(-1), win_count.reshape(-1), most, d_slots, d_gate_slots, slot_of, *held)
+    )(home, win_start, win_count, most, d_slots, d_gate_slots, slot_of, *held)
 
 
 def dense_backward(saved_state, x_rows, dy_rows, d_logits, d_normed2_moe, norm1_gain, norm2_gain, w_qkv, w_attn_out, w_router):
-    normed1, attn_pullback, context, h_rows, normed2 = saved_state
+    normed1, qkv_rot, context, h_rows, normed2, cos_t, sin_t, num_seqs = saved_state
     d_w_router = jnp.einsum('td,te->de', normed2, d_logits, preferred_element_type=jnp.float32)
     d_normed2 = d_normed2_moe + jnp.einsum('te,de->td', d_logits, w_router, preferred_element_type=jnp.float32)
     d_h_part, d_norm2_gain = rms_norm_bwd(h_rows, norm2_gain, d_normed2)
     d_h = (dy_rows.astype(jnp.float32) + d_h_part).astype(jnp.bfloat16)
     d_w_attn_out = jnp.einsum('td,te->de', context, d_h, preferred_element_type=jnp.float32)
     d_context = jnp.einsum('te,de->td', d_h, w_attn_out, preferred_element_type=jnp.float32).astype(jnp.bfloat16)
-    d_qkv = attn_pullback(d_context)[0].astype(jnp.bfloat16)
+    d_qkv = attend_back(qkv_rot, d_context, cos_t, sin_t, num_seqs)
     d_w_qkv = jnp.einsum('td,te->de', normed1, d_qkv, preferred_element_type=jnp.float32)
     d_normed1 = jnp.einsum('te,de->td', d_qkv, w_qkv, preferred_element_type=jnp.float32)
     d_x_part, d_norm1_gain = rms_norm_bwd(x_rows, norm1_gain, d_normed1)
     d_x = (d_h.astype(jnp.float32) + d_x_part).astype(jnp.bfloat16)
-    return d_x, (d_norm1_gain, d_norm2_gain, d_w_qkv, d_w_attn_out, d_w_router)
+    small = jnp.concatenate([d_w_router, d_norm1_gain[:, None], d_norm2_gain[:, None]], axis=1)
+    return d_x, d_qkv, (d_w_qkv, d_w_attn_out, small)
 
 
 def solution(mesh):
@@ -374,7 +505,15 @@
     tok_spec = P(('dp', 'ep'), None, None)
     rep_spec = P()
     exp_spec = P('ep', None, None)
-    pair = [(r, r ^ 1) for r in range(ep_size)]
+
+    def swap(value, distance):
+        return lax.ppermute(value, 'ep', [(r, r ^ distance) for r in range(ep_size)])
+
+    def spread_routes(value):
+        near = jnp.stack([value, swap(value, 1)])
+        row = [near, jnp.stack([swap(value, 2), swap(value, 3)])]
+        far = lax.ppermute(jnp.concatenate(row, axis=0), 'dp', [(r, r ^ 1) for r in range(dp_size)])
+        return row + [far]
 
     def local_step(x_tokens, dy_tokens, route_idx, norm1_gain, norm2_gain, w_qkv, w_attn_out, w_router, w_gate, w_up, w_down):
         num_seqs, seq_len, model_width = x_tokens.shape
@@ -389,62 +528,58 @@
         ep_rank = lax.axis_index('ep')
         me = lax.axis_index('dp') * ep_size + ep_rank
         first_expert = ep_rank * local_experts
-        order = jnp.bitwise_xor(me, jnp.arange(num_dev, dtype=jnp.int32))
-
-        idx_wide = lax.all_gather(jnp.concatenate([idx_rows.T] * 4, axis=0), ('dp', 'ep'), axis=0)
+
         dy_all = lax.all_gather(dy_rows, ('dp', 'ep'), axis=0, tiled=True)
-        dy_pair = lax.ppermute(dy_rows, 'ep', pair)
-        idx_all = jnp.take(idx_wide[:, :top_k], order, axis=0)
-        slot_of, win_start, win_count = slot_positions(idx_all, first_expert, local_experts, capacity)
-
-        normed1 = rms_norm(x_rows, norm1_gain)
-        qkv_rows = jnp.dot(normed1, w_qkv, preferred_element_type=jnp.float32)
-        context, attn_pullback = jax.vjp(lambda qkv_in: attention_core(qkv_in, num_seqs), qkv_rows)
+        idx_parts = spread_routes(idx_rows.T)
+        dy_pair = swap(dy_rows, 1)
+        routes = slot_positions(jnp.concatenate(idx_parts, axis=0), first_expert, local_experts, capacity)
+
+        cos_t, sin_t = rope_tables(seq_len)
+        normed1, qkv_rot = qkv_project(x_rows, norm1_gain, w_qkv, cos_t, sin_t)
+        qkv_rot, routes = lax.optimization_barrier((qkv_rot, routes))
+        context = attend(qkv_rot, num_seqs)
         h_rows = (x_rows.astype(jnp.float32) + jnp.dot(context, w_attn_out, preferred_element_type=jnp.float32)).astype(jnp.bfloat16)
         normed2 = rms_norm(h_rows, norm2_gain)
-        x_pair = lax.ppermute(normed2, 'ep', pair)
+        x_pair = swap(normed2, 1)
         logits = jnp.dot(normed2, w_router, preferred_element_type=jnp.float32)
         probs_all, hits, picked_sum = gate_forward(logits, idx_rows, num_experts)
         gates = probs_all * hits / picked_sum
         gate_t = jnp.sum(jnp.where(choice_mask(idx_rows, num_experts), gates[:, None, :], 0.0), axis=2).T
-        gate_pair = lax.ppermute(gate_t, 'ep', pair)
-        gate_wide = lax.all_gather(jnp.concatenate([gate_t] * 4, axis=0), ('dp', 'ep'), axis=0)
-        normed2_out, _ = lax.optimization_barrier((normed2, dy_all))
-        x_all = lax.all_gather(normed2_out, ('dp', 'ep'), axis=0, tiled=True)
-        gate_near = expand_routes(idx_all[:2], jnp.stack([gate_t, gate_pair]), first_expert, local_experts)
-        gate_far = expand_routes(idx_all[2:], jnp.take(gate_wide[:, :top_k], order[2:], axis=0), first_expert, local_experts)
-
-        near_routes = (slot_of[:2], win_start[:2], win_count[:2], gate_near)
-        all_routes = (slot_of, win_start, win_count, jnp.concatenate([jnp.zeros_like(gate_near), gate_far], axis=0))
-        gather = functools.partial(gather_slots, me[None], total_dev=num_dev, capacity=capacity)
-        s_arr, dy_arr, g0 = gather(near_routes, 0, 1, normed2, dy_rows, None, scaled=False, from_all=False)
-        s_arr, dy_arr, g1 = gather(near_routes, 1, 1, x_pair, dy_pair, (s_arr, dy_arr), scaled=False, from_all=False)
-        tile = 2 * capacity
+        x_all = lax.all_gather(normed2, ('dp', 'ep'), axis=0, tiled=True)
+        gate_near, gate_x, gate_far = (expand_routes(i, g, first_expert, local_experts) for i, g in zip(idx_parts, spread_routes(gate_t)))
+
+        gather = functools.partial(gather_slots, me[None], routes, own_dev=ep_size, capacity=capacity)
         rows_of = lambda a: a.reshape(local_experts, -1, a.shape[-1])
         slots_of = lambda a, n: a.reshape(local_experts, n, capacity, a.shape[-1])
-        g_near = rows_of(jnp.concatenate([g0, g1], axis=1))
-        hidden, dag, dau, d_out, ds_near, dg_near = expert_pass(True, tile, 0, 1, rows_of(s_arr), rows_of(dy_arr), g_near, w_gate, w_up, w_down, None)
-        s_arr, dy_arr, g_x = gather(all_routes, 2, 2, x_all, dy_all, (s_arr, slots_of(d_out, num_dev)), scaled=False, from_all=True)
-        hidden, dag, dau, d_out, ds_x, dg_x = expert_pass(True, tile, 1, 1, rows_of(s_arr), rows_of(dy_arr), rows_of(g_x), w_gate, w_up, w_down, (hidden, dag, dau))
-        combined = combine_slots(ep_rank[None], all_routes, 2, 2, ep_size, slots_of(ds_x, 2), slots_of(dg_x, 2), None)
-        d_tok, d_gate_t = combine_slots(ep_rank[None], all_routes, 0, 2, ep_size, slots_of(ds_near, 2), slots_of(dg_near, 2), combined)
+        combine = functools.partial(combine_slots, ep_rank[None], routes, total_dev=ep_size)
+        weights = (w_gate, w_up, w_down)
+        tile = 2 * capacity
+        arrays = gather(0, 1, gate_near[:1], normed2, dy_rows, None, scaled=False, from_all=False)
+        s_arr, dy_arr, g_arr = gather(1, 1, gate_near[1:], x_pair, dy_pair, arrays, scaled=False, from_all=False)
+        hidden, dag, dau, d_out, ds_near, dg_near = expert_pass(True, tile, 0, 1, rows_of(s_arr), rows_of(dy_arr), rows_of(g_arr), *weights, None)
+        combined = combine(0, 2, d_slots=slots_of(ds_near, 2), d_gate_slots=slots_of(dg_near, 2), filled=None)
+        s_arr, dy_arr, g_arr = gather(2, 2, gate_x, x_all, dy_all, (s_arr, slots_of(d_out, num_dev), g_arr), scaled=False, from_all=True)
+        hidden, dag, dau, d_out, ds_x, dg_x = expert_pass(True, tile, 1, 1, rows_of(s_arr), rows_of(dy_arr), rows_of(g_arr), *weights, (hidden, dag, dau))
+        d_tok, d_gate_t = combine(2, 2, d_slots=slots_of(ds_x, 2), d_gate_slots=slots_of(dg_x, 2), filled=combined)
         d_normed2_moe = lax.psum_scatter(d_tok, 'ep', scatter_dimension=0, tiled=True)
         d_gate_blk = lax.all_to_all(d_gate_t, 'ep', 0, 0, tiled=True)
         d_gate_dense = jnp.transpose(d_gate_blk, (1, 3, 0, 2)).reshape(num_tokens, num_experts)
         d_out, _ = lax.optimization_barrier((d_out, d_tok))
-        s_arr, dy_arr = gather(all_routes, 4, 4, x_all, dy_all, (s_arr, slots_of(d_out, num_dev)), scaled=True, from_all=True)
+        s_arr, dy_arr = gather(4, 4, gate_far, x_all, dy_all, (s_arr, slots_of(d_out, num_dev)), scaled=True, from_all=True)
         s_all, d_out = rows_of(s_arr), rows_of(dy_arr)
-        hidden, dag, dau = expert_pass(False, tile, 2, 2, s_all, d_out, None, w_gate, w_up, w_down, (hidden, dag, dau))
+        hidden, dag, dau = expert_pass(False, tile, 2, 2, s_all, d_out, None, *weights, (hidden, dag, dau))
         mm = functools.partial(jnp.einsum, preferred_element_type=jnp.float32)
         d_w_down = mm('ecf,ecd->efd', hidden, d_out)
+
+        d_logits = gate_backward(probs_all, hits, picked_sum, d_gate_dense).astype(jnp.bfloat16)
+        saved_state = (normed1, qkv_rot, context, h_rows, normed2, cos_t, sin_t, num_seqs)
+        d_x, d_qkv, dense_grads = dense_backward(saved_state, x_rows, dy_rows, d_logits, d_normed2_moe, norm1_gain, norm2_gain, w_qkv, w_attn_out, w_router)
+        d_w_qkv, d_w_attn_out, small = lax.psum(dense_grads, ('dp', 'ep'))
+        s_all, dag, dau, _ = lax.optimization_barrier((s_all, dag, dau, d_qkv))
         d_w_gate = mm('ecd,ecf->edf', s_all, dag)
         d_w_up = mm('ecd,ecf->edf', s_all, dau)
-
-        d_logits = gate_backward(probs_all, hits, picked_sum, d_gate_dense).astype(jnp.bfloat16)
-        saved_state = (normed1, attn_pullback, context, h_rows, normed2)
-        d_x, dense_grads = dense_backward(saved_state, x_rows, dy_rows, d_logits, d_normed2_moe, norm1_gain, norm2_gain, w_qkv, w_attn_out, w_router)
-        dense_grads = lax.psum(dense_grads, ('dp', 'ep'))
-        return (d_x.reshape(x_tokens.shape),) + tuple(dense_grads) + (d_w_gate, d_w_up, d_w_down)
+        return (d_x.reshape(x_tokens.shape), small[:, num_experts], small[:, num_experts + 1], d_w_qkv, d_w_attn_out, small[:, :num_experts],
+                d_w_gate, d_w_up, d_w_down)
 
     return jax.shard_map(local_step, mesh=mesh,
                          in_specs=(tok_spec, tok_spec, tok_spec, rep_spec, rep_spec, rep_spec, rep_spec, rep_spec, exp_spec, exp_spec, exp_spec),

time: 1610 us -> 1410 us (0.88)
  matrix products: 602 us -> 406 us
  Pallas kernels: 647 us -> 772 us
  local copies, waits for them, and re-layouts: 125 us -> 33.7 us
  other arithmetic: 109 us -> 38.1 us
  waiting for transfers between devices: 73.6 us -> 123 us
  blocking collectives: 26.1 us -> 0 us
    dot_general x6 -> x0, matrix products: 165 us -> none  [the longest x2 74.4 us: attention_core(): jnp.einsum('bqhd,bkhd->bhqk', query_rot, key_rot, preferred_element_type=...]
    pallas_call x0 -> x3, Pallas kernels: none -> 114 us  [the longest x1 55.2 us: attend_back(): pl.pallas_call(functools.partial(attend_back_kernel, block=min(256, seq_l...]
    psum x1, waiting for transfers between devices: 50 us -> 102 us  [local_step(): d_w_qkv, d_w_attn_out, small = lax.psum(dense_grads, ('dp', 'ep'))]
    convert_element_type x3 -> x0, local copies, waits for them, and re-layouts: 43.6 us -> none  [the longest x2 36.8 us: dense_backward(): d_qkv = attn_pullback(d_context)[0].astype(jnp.bfloat16)]
    convert_element_type x2 -> x1, other arithmetic: 41.2 us -> 1.27 us  [qkv_project(): gain_vec.astype(jnp.float32)[None, :]]
    sub x1 -> x0, matrix products: 38 us -> none  [attention_core(): jax.nn.softmax(jnp.where(causal, scores, -1e+30), axis=-1)]
    psum x1 -> x0, blocking collectives: 26.1 us -> none  [local_step(): dense_grads = lax.psum(dense_grads, ('dp', 'ep'))]
    reshape x16 -> x2, local copies, waits for them, and re-layouts: 22.3 us -> 1.34 us  [the longest x1 0.67 us: slot_positions(): most_block.reshape(-1)]
  transfers between devices with their start and end apart: 10 -> 15, of which waited for: 4 -> 5; matrix products, arithmetic and copies ran while one was open for 35% -> 20% of each run, Pallas kernels for 26% -> 36%
where the time goes in v3:
time: 1410 us; the launch traced here: 1400 us
  Pallas kernels  772 us (55%)
  matrix products  406 us (29%)
  waiting for transfers between devices  123 us (9%)
  other arithmetic  38.1 us (3%)
  local copies, waits for them, and re-layouts  33.7 us (2%)
  between operations  15 us (1%)
  starting transfers between devices  14.1 us (1%)
    pallas_call x3, Pallas kernels, expert_pass(): pl.pallas_call(functools.partial(expert_kernel, own=own, chunk=min(256, w...  458 us
    pallas_call x4, Pallas kernels, gather_slots(): pl.pallas_call(functools.partial(gather_kernel, blocks=blocks, capacity=c...  149 us
    dot_general x1, matrix products, local_step(): d_w_up = mm('ecd,ecf->edf', s_all, dau)  110 us
    dot_general x1, matrix products, local_step(): d_w_down = mm('ecf,ecd->efd', hidden, d_out)  108 us
    dot_general x1, matrix products, local_step(): d_w_gate = mm('ecd,ecf->edf', s_all, dag)  108 us
    psum x1, waiting for transfers between devices, local_step(): d_w_qkv, d_w_attn_out, small = lax.psum(dense_grads, ('dp', 'ep'))  102 us
    pallas_call x1, Pallas kernels, attend_back(): pl.pallas_call(functools.partial(attend_back_kernel, block=min(256, seq_l...  55.2 us
    pallas_call x2, Pallas kernels, combine_slots(): pl.pallas_call(functools.partial(combine_kernel, experts=experts, blocks=...  51.1 us
  transfers between devices with their start and end apart: 15, of which 5 were waited for; matrix products, arithmetic and copies ran while one was open for 20% of the time, Pallas kernels for 36%

profile of v3, /device:TPU:0, one launch (start us, length us, event | category | flops | bytes accessed | tf_op | source)
XLA Modules:
  0.0 1402.2 jit_solution(2459792765309037790)
XLA Ops:
  18.5 21.0 %qkv_project.1 = (bf16[2048,1024]{1,0:T(8,128)(2,1)}, bf16[2048,3072]{1,0:T(8,128)(2,1)}) custom-call(bf16[2048,1024]{1,0:T(8,128)(2,1)} %bitcast.130, f32[1,1024]{1,0:T(1,128)} %bitcast.170, bf16[1024,3072]{1,0:T(8,128)(2,1)} %w_ref.1, f32[1024,128]{1,0:T(8,128)} %get-tuple-element.124.cos_ref, f32[1024,128]{1,0:T(8,128)} %get-tuple-element.125.sin_ref), custom_call_target="tpu_custom_call" | custom-call | flops 12884901888 | bytes 27262976 | tf_op jit(solution)/shard_map/qkv_project/pallas_call | solution.py:75
  46.7 8.4 collective-permute-done.3
  56.5 3.9 convert_reduce_fusion
  66.1 37.9 %attend.1 = bf16[2048,1024]{1,0:T(8,128)(2,1)} custom-call(bf16[2048,3072]{1,0:T(8,128)(2,1)} %get-tuple-element.52.q_ref.k_ref.v_ref, bf16[2048,3072]{1,0:T(8,128)(2,1)} %get-tuple-element.52.q_ref.k_ref.v_ref, bf16[2048,3072]{1,0:T(8,128)(2,1)} %get-tuple-element.52.q_ref.k_ref.v_ref), custom_call_target="tpu_custom_call" | custom-call | flops 8589934592 | bytes 16777216 | tf_op jit(solution)/shard_map/attend/pallas_call | solution.py:107
  104.0 9.1 fusion.8
  119.7 3.6 fusion.50
  129.4 4.1 collective-permute-done.8
  139.9 19.3 %gather_slots.4 = (bf16[16,8,320,1024]{3,2,1,0:T(8,128)(2,1)}, bf16[16,8,320,1024]{3,2,1,0:T(8,128)(2,1)}, f32[16,4,320,1]{3,2,1,0:T(8,128)}) custom-call(s32[1]{0:T(128)} %bitcast.16.base_ref, s32[1024]{0:T(1024)} %get-tuple-element.53.start_ref, s32[1024]{0:T(1024)} %get-tuple-element.54.count_ref, s32[32]{0:T(128)} %reshape.200.most_ref, ...), custom_call_target="tpu_custom_call" | custom-call | flops 8589934592 | bytes 29360128 | tf_op jit(solution)/shard_map/gather_slots/pallas_call | solution.py:333
  159.3 20.5 %gather_slots.5 = (bf16[16,8,320,1024]{3,2,1,0:T(8,128)(2,1)}, bf16[16,8,320,1024]{3,2,1,0:T(8,128)(2,1)}, f32[16,4,320,1]{3,2,1,0:T(8,128)}) custom-call(s32[1]{0:T(128)} %bitcast.16.base_ref, s32[1024]{0:T(1024)} %get-tuple-element.53.start_ref, s32[1024]{0:T(1024)} %get-tuple-element.54.count_ref, ...), custom_call_target="tpu_custom_call", output_to_operand_aliasing={{0}: (8, {}), {1}: (9, {}), {2}: (10, {})} | custom-call | flops 8589934592 | bytes 29360128 | tf_op jit(solution)/shard_map/gather_slots/pallas_call | solution.py:333
  179.8 150.7 %expert_own.2 = (bf16[16,2560,1024]{2,1,0:T(8,128)(2,1)}, bf16[16,2560,1024]{2,1,0:T(8,128)(2,1)}, bf16[16,2560,1024]{2,1,0:T(8,128)(2,1)}, bf16[16,2560,1024]{2...) custom-call(bf16[16,2560,1024]{2,1,0:T(8,128)(2,1)} %bitcast.24.refs_0_, ...), custom_call_target="tpu_custom_call", output_to_operand_aliasing={{3}: (1, {})} | custom-call | flops 128849018880 | bytes 247463936 | tf_op jit(solution)/shard_map/expert_own/pallas_call | solution.py:406
  330.4 26.0 %combine_slots.2 = (f32[8192,1024]{1,0:T(8,128)}, f32[4,8,16,256]{3,2,1,0:T(8,128)}) custom-call(s32[1]{0:T(128)} %bitcast.15.home_ref, s32[1024]{0:T(1024)} %get-tuple-element.53.start_ref, s32[1024]{0:T(1024)} %get-tuple-element.54.count_ref, s32[64]{0:T(128)} %reshape.201.most_ref, bf16[16,2,320,1024]{3,2,1,0:T(8,128)(2,1)} %bitcast.175, ...), custom_call_target="tpu_custom_call" | custom-call | flops 8589934592 | bytes 37748736 | tf_op jit(solution)/shard_map/combine_slots/pallas_call | solution.py:465
  356.5 36.3 %gather_slots.6 = (bf16[16,8,320,1024]{3,2,1,0:T(8,128)(2,1)}, bf16[16,8,320,1024]{3,2,1,0:T(8,128)(2,1)}, f32[16,4,320,1]{3,2,1,0:T(8,128)}) custom-call(s32[1]{0:T(128)} %bitcast.16.base_ref, s32[1024]{0:T(1024)} %get-tuple-element.53.start_ref, s32[1024]{0:T(1024)} %get-tuple-element.54.count_ref, ...), custom_call_target="tpu_custom_call", output_to_operand_aliasing={{0}: (8, {}), {1}: (9, {}), {2}: (10, {})} | custom-call | flops 17179869184 | bytes 58720256 | tf_op jit(solution)/shard_map/gather_slots/pallas_call | solution.py:333
  392.8 147.5 %expert_own.3 = (bf16[16,2560,1024]{2,1,0:T(8,128)(2,1)}, bf16[16,2560,1024]{2,1,0:T(8,128)(2,1)}, bf16[16,2560,1024]{2,1,0:T(8,128)(2,1)}, bf16[16,2560,1024]{2...) custom-call(bf16[16,2560,1024]{2,1,0:T(8,128)(2,1)} %bitcast.28.refs, ...), custom_call_target="tpu_custom_call", output_to_operand_aliasing={{3}: (1, {}), {0}: (6, {}), {1}: (7, {}), {2}: (8, {})} | custom-call | flops 128849018880 | bytes 247463936 | tf_op jit(solution)/shard_map/expert_own/pallas_call | solution.py:406
  540.3 25.1 %combine_slots.3 = (f32[8192,1024]{1,0:T(8,128)}, f32[4,8,16,256]{3,2,1,0:T(8,128)}) custom-call(s32[1]{0:T(128)} %bitcast.15.home_ref, s32[1024]{0:T(1024)} %get-tuple-element.53.start_ref, s32[1024]{0:T(1024)} %get-tuple-element.54.count_ref, s32[64]{0:T(128)} %reshape.201.most_ref, ...), custom_call_target="tpu_custom_call", output_to_operand_aliasing={{0}: (7, {}), {1}: (8, {})} | custom-call | flops 8589934592 | bytes 37748736 | tf_op jit(solution)/shard_map/combine_slots/pallas_call | solution.py:465
  565.5 3.2 multiply_reduce_fusion
  571.6 5.3 collective-permute-done.9
  579.2 4.2 all-to-all-start
  583.4 73.0 %gather_slots.7 = (bf16[16,8,320,1024]{3,2,1,0:T(8,128)(2,1)}, bf16[16,8,320,1024]{3,2,1,0:T(8,128)(2,1)}) custom-call(s32[1]{0:T(128)} %bitcast.16.base_ref, s32[1024]{0:T(1024)} %get-tuple-element.53.start_ref, s32[1024]{0:T(1024)} %get-tuple-element.54.count_ref, s32[32]{0:T(128)} %reshape.200.most_ref, ...), custom_call_target="tpu_custom_call", output_to_operand_aliasing={{0}: (8, {}), {1}: (9, {})} | custom-call | flops 34359738368 | bytes 117440512 | tf_op jit(solution)/shard_map/gather_slots/pallas_call | solution.py:333
  656.4 159.5 %expert_far.1 = (bf16[16,2560,1024]{2,1,0:T(8,128)(2,1)}, bf16[16,2560,1024]{2,1,0:T(8,128)(2,1)}, bf16[16,2560,1024]{2,1,0:T(8,128)(2,1)}) custom-call(bf16[16,2560,1024]{2,1,0:T(8,128)(2,1)} %bitcast.44.refs_0_, bf16[16,2560,1024]{2,1,0:T(8,128)(2,1)} %bitcast.45.refs_1_, ...), custom_call_target="tpu_custom_call", output_to_operand_aliasing={{0}: (5, {}), {1}: (6, {}), {2}: (7, {})} | custom-call | flops 128849018880 | bytes 394264576 | tf_op jit(solution)/shard_map/expert_far/pallas_call | solution.py:406
  816.0 108.4 %fusion.55 = f32[16,1024,1024]{2,1,0:T(8,128)} fusion(bf16[16,2560,1024]{2,1,0:T(8,128)(2,1)} %get-tuple-element.92, bf16[16,2560,1024]{2,1,0:T(8,128)(2,1)} %bitcast.45.refs_1_), kind=kOutput, calls=%fused_computation.137 | convolution fusion | flops 85899345920 | bytes 234881024 | tf_op jit(solution)/shard_map/ecf,ecd->efd/dot_general | solution.py:572
  926.5 3.7 fusion.56
  930.3 6.8 fusion.17
  940.2 6.4 convolution_convert_fusion.dctx_ref
  946.6 6.1 fusion.52
  952.7 55.2 %attend_back.1 = bf16[2048,3072]{1,0:T(8,128)(2,1)} custom-call(bf16[2048,3072]{1,0:T(8,128)(2,1)} %get-tuple-element.52.q_ref.k_ref.v_ref, bf16[2048,3072]{1,0:T(8,128)(2,1)} %get-tuple-element.52.q_ref.k_ref.v_ref, bf16[2048,3072]{1,0:T(8,128)(2,1)} %get-tuple-element.52.q_ref.k_ref.v_ref, bf16[2048,1024]{1,0:T(8,128)(2,1)} %convolution_convert_fusion.dctx_ref, ...), custom_call_target="tpu_custom_call" | custom-call | flops 21474836480 | bytes 29360128 | tf_op jit(solution)/shard_map/attend_back/pallas_call | solution.py:184
  1007.9 24.0 %fusion.7 = (f32[1024]{0:T(1024)}, f32[2048]{0:T(1024)S(1)}, f32[2048,1024]{1,0:T(8,128)}) fusion(f32[2048]{0:T(1024)} %bitcast.167, bf16[2,1024,1024]{2,1,0:T(8,128)(2,1)} %param.11, f32[1024]{0:T(1024)} %convert_element_type.73, bf16[2048,3072]{1,0:T(8,128)(2,1)} %attend_back.1, bf16[1024,3072]{1,0:T(8,128)(2,1)} %w_ref.1), kind=kOutput, calls=%fused_computation.16 | convolution fusion | flops 12899578880 | bytes 31481856 | tf_op jit(solution)/shard_map/te,de->td/dot_general | solution.py:495
  1032.6 18.4 %fusion.51 = f32[1024,3072]{1,0:T(8,128)} fusion(bf16[2048,1024]{1,0:T(8,128)(2,1)S(1)} %copy-done.49, bf16[2048,3072]{1,0:T(8,128)(2,1)} %attend_back.1), kind=kOutput, calls=%fused_computation.133 | convolution fusion | flops 12884901888 | bytes 29360128 | tf_op jit(solution)/shard_map/td,te->de/dot_general | solution.py:494
  1051.0 108.3 %fusion.53 = f32[16,1024,1024]{2,1,0:T(8,128)} fusion(bf16[16,2560,1024]{2,1,0:T(8,128)(2,1)} %bitcast.44.refs_0_, bf16[16,2560,1024]{2,1,0:T(8,128)(2,1)} %get-tuple-element.90), kind=kOutput, calls=%fused_computation.135 | convolution fusion | flops 85899345920 | bytes 234881024 | tf_op jit(solution)/shard_map/ecd,ecf->edf/dot_general | solution.py:579
  1159.4 7.3 fusion.4
  1167.4 109.5 %fusion.54 = f32[16,1024,1024]{2,1,0:T(8,128)} fusion(bf16[16,2560,1024]{2,1,0:T(8,128)(2,1)} %bitcast.44.refs_0_, bf16[16,2560,1024]{2,1,0:T(8,128)(2,1)} %get-tuple-element.91), kind=kOutput, calls=%fused_computation.136 | convolution fusion | flops 85899345920 | bytes 234881024 | tf_op jit(solution)/shard_map/ecd,ecf->edf/dot_general | solution.py:580
  1277.0 101.9 %all-reduce.3.cloned.1.call-done = (f32[1024,66]{0,1:T(8,128)}, f32[1024,3072]{1,0:T(8,128)}, f32[1024,1024]{1,0:T(8,128)}) async-done(((f32[1024,66]{0,1:T(8,128)}, f32[1024,3072]{1,0:T(8,128)}, f32[1024,1024]{1,0:T(8,128)}), (f32[1024,66]{0,1:T(8,128)}, f32[1024,3072]{1,0:T(8,128)}, f32[1024,1024]{1,0:T(8,128)})) %all-reduce.3.cloned.1.call-update) | async-done | bytes 17047568 | tf_op jit(solution)/shard_map/psum | solution.py:577
  1382.0 11.1 copy.158
  (192 shorter events, 61.4 us)
Async XLA Ops:
  7.2 349.3 %all-gather.5.cloned.1.call-start = ((), (), s32[]{:S(2)}) async-start(), calls=%async_computation.3 | async-start | bytes 37748736 | tf_op jit(solution)/shard_map/all_gather | solution.py:532
  7.9 348.6 %all-gather.3.cloned.1.call-start = ((), (), s32[]{:S(2)}) async-start(), calls=%async_computation.2 | async-start | bytes 37748736 | tf_op jit(solution)/shard_map/all_gather | solution.py:548
  8.0 31.5 %collective-permute-start = (s32[8,2048]{1,0:T(8,128)}, s32[8,2048]{1,0:T(8,128)}, u32[]{:S(2)}, u32[]{:S(2)}) collective-permute-start(s32[8,2048]{1,0:T(8,128)} %bitcast.144), channel_id=1, source_target_pairs={{0,1},{1,0},{2,3},{3,2},{4,5},{5,4},{6,7},{7,6}} | collective-permute-start | bytes 196616 | tf_op jit(solution)/shard_map/ppermute | solution.py:510
  8.8 30.7 %collective-permute-start.1 = (s32[8,2048]{1,0:T(8,128)}, s32[8,2048]{1,0:T(8,128)}, u32[]{:S(2)}, u32[]{:S(2)}) collective-permute-start(s32[8,2048]{1,0:T(8,128)} %bitcast.145), channel_id=1, source_target_pairs={{0,2},{1,3},{2,0},{3,1},{4,6},{5,7},{6,4},{7,5}} | collective-permute-start | bytes 196616 | tf_op jit(solution)/shard_map/ppermute | solution.py:510
  11.3 28.2 %collective-permute-start.2 = (s32[8,2048]{1,0:T(8,128)}, s32[8,2048]{1,0:T(8,128)}, u32[]{:S(2)}, u32[]{:S(2)}) collective-permute-start(s32[8,2048]{1,0:T(8,128)} %bitcast.146), channel_id=1, source_target_pairs={{0,3},{1,2},{2,1},{3,0},{4,7},{5,6},{6,5},{7,4}} | collective-permute-start | bytes 196616 | tf_op jit(solution)/shard_map/ppermute | solution.py:510
  39.5 21.3 %copy-start.44 = (s32[16]{0:T(128)}, s32[16]{0:T(128)S(1)}, u32[]{:S(2)}) copy-start(s32[16]{0:T(128)S(1)} %iota_add_fusion) | copy-start | bytes 196
  40.5 14.7 %collective-permute-start.3 = (s32[4,8,2048]{2,1,0:T(8,128)S(1)}, s32[4,8,2048]{2,1,0:T(8,128)S(1)}, u32[]{:S(2)}, u32[]{:S(2)}) collective-permute-start(s32[4,8,2048]{2,1,0:T(8,128)S(1)} %pad_add_fusion), channel_id=1, source_target_pairs={{0,4},{4,0},{1,5},{5,1},{2,6},{6,2},{3,7},{7,3}} | collective-permute-start | bytes 786440 | tf_op jit(solution)/shard_map/ppermute | solution.py:515
  117.7 19.4 %copy-start.45 = (s32[16]{0:T(128)S(1)}, s32[16]{0:T(128)}, u32[]{:S(2)}) copy-start(s32[16]{0:T(128)} %copy-done.44) | copy-start | bytes 196
  117.7 812.5 %reduce-scatter.2.cloned.1.call-start = ((), (), s32[]{:S(2)}) async-start(), calls=%async_computation.4 | async-start | bytes 41943040 | tf_op jit(solution)/shard_map/reduce_scatter | solution.py:564
  117.8 41.5 %collective-permute-start.7 = (bf16[2048,1024]{1,0:T(8,128)(2,1)}, bf16[2048,1024]{1,0:T(8,128)(2,1)}, u32[]{:S(2)}, u32[]{:S(2)}) collective-permute-start(bf16[2048,1024]{1,0:T(8,128)(2,1)} %bitcast.128), channel_id=1, source_target_pairs={{0,1},{1,0},{2,3},{3,2},{4,5},{5,4},{6,7},{7,6}} | collective-permute-start | bytes 12582920 | tf_op jit(solution)/shard_map/ppermute | solution.py:510
  117.8 41.5 %collective-permute-start.6 = (bf16[2048,1024]{1,0:T(8,128)(2,1)}, bf16[2048,1024]{1,0:T(8,128)(2,1)}, u32[]{:S(2)}, u32[]{:S(2)}) collective-permute-start(bf16[2048,1024]{1,0:T(8,128)(2,1)} %fusion.10.x_ref), channel_id=1, source_target_pairs={{0,1},{1,0},{2,3},{3,2},{4,5},{5,4},{6,7},{7,6}} | collective-permute-start | bytes 12582920 | tf_op jit(solution)/shard_map/ppermute | solution.py:510
  126.3 7.2 collective-permute-start.8
  127.3 6.3 collective-permute-start.5
  129.2 7.2 collective-permute-start.4
  565.4 11.5 copy-start.17
  565.4 11.5 copy-start.46
  568.7 8.2 collective-permute-start.9
  579.2 345.2 %all-to-all-start = ((f32[4,8,16,256]{3,2,1,0:T(8,128)}), f32[4,8,16,256]{3,2,1,0:T(8,128)}, u32[]{:S(2)}, u32[]{:S(2)}) async-start(f32[4,8,16,256]{3,2,1,0:T(8,128)} %get-tuple-element.78), calls=%async_computation.1 | async-start | bytes 1048576 | tf_op jit(solution)/shard_map/all_to_all | solution.py:565
  583.4 795.5 %all-reduce.3.cloned.1.call-start = ((), (), s32[]{:S(2)}) async-start(), calls=%async_computation.5 | async-start | bytes 34144256 | tf_op jit(solution)/shard_map/psum | solution.py:577
  815.9 110.1 %copy-start.10 = (f32[2048,64]{0,1:T(8,128)S(1)}, f32[2048,64]{0,1:T(8,128)}, u32[]{:S(2)}) copy-start(f32[2048,64]{0,1:T(8,128)} %copy-done.9) | copy-start | bytes 1572868
  815.9 110.1 %copy-start.3 = (f32[2048,64]{0,1:T(8,128)S(1)}, f32[2048,64]{0,1:T(8,128)}, u32[]{:S(2)}) copy-start(f32[2048,64]{0,1:T(8,128)} %copy-done.2) | copy-start | bytes 1572868
  815.9 110.1 %copy-start.8 = (f32[2048,64]{0,1:T(8,128)S(1)}, f32[2048,64]{0,1:T(8,128)}, u32[]{:S(2)}) copy-start(f32[2048,64]{0,1:T(8,128)} %copy-done.7) | copy-start | bytes 1572868
  815.9 110.1 %copy-start.23 = (f32[2048]{0:T(1024)S(1)}, f32[2048]{0:T(1024)}, u32[]{:S(2)}) copy-start(f32[2048]{0:T(1024)} %copy-done.22) | copy-start | bytes 24580
  816.0 110.1 %copy-start.31 = (f32[2048]{0:T(1024)S(1)}, f32[2048]{0:T(1024)}, u32[]{:S(2)}) copy-start(f32[2048]{0:T(1024)} %copy-done.30) | copy-start | bytes 24580
  816.0 110.1 %copy-start.33 = (f32[2048]{0:T(1024)S(1)}, f32[2048]{0:T(1024)}, u32[]{:S(2)}) copy-start(f32[2048]{0:T(1024)} %copy-done.32) | copy-start | bytes 24580
  1007.9 24.6 %copy-start.49 = (bf16[2048,1024]{1,0:T(8,128)(2,1)S(1)}, bf16[2048,1024]{1,0:T(8,128)(2,1)}, u32[]{:S(2)}) copy-start(bf16[2048,1024]{1,0:T(8,128)(2,1)} %get-tuple-element.79) | copy-start | bytes 12582916
  1051.0 108.4 %copy-start.5 = (bf16[2,1024,1024]{2,1,0:T(8,128)(2,1)S(1)}, bf16[2,1024,1024]{2,1,0:T(8,128)(2,1)}, u32[]{:S(2)}) copy-start(bf16[2,1024,1024]{2,1,0:T(8,128)(2,1)} %param.11) | copy-start | bytes 12582916
  1051.0 108.4 %copy-start.39 = (f32[1,8,2,128]{3,1,2,0:T(8,128)S(1)}, f32[1,8,2,128]{3,1,2,0:T(8,128)}, u32[]{:S(2)}) copy-start(f32[1,8,2,128]{3,1,2,0:T(8,128)} %copy.132) | copy-start | bytes 24580
  1051.0 108.4 %copy-start.40 = (f32[2048]{0:T(1024)S(1)}, f32[2048]{0:T(1024)}, u32[]{:S(2)}) copy-start(f32[2048]{0:T(1024)} %multiply_multiply_fusion) | copy-start | bytes 24580
  1051.0 108.4 %copy-start.41 = (f32[2048]{0:T(1024)S(1)}, f32[2048]{0:T(1024)}, u32[]{:S(2)}) copy-start(f32[2048]{0:T(1024)} %broadcast_multiply_fusion) | copy-start | bytes 24580
  1051.0 108.4 %copy-start.42 = (f32[1024]{0:T(1024)S(1)}, f32[1024]{0:T(1024)}, u32[]{:S(2)}) copy-start(f32[1024]{0:T(1024)} %convert_element_type.73) | copy-start | bytes 12292
  1382.0 11.1 copy-start.12
  (33 other events, 151.3 us)
Sparse Core Ops, SparseCore 0:
  9.8 164.8 all-gather.4
  176.5 155.1 all-gather.2
  565.6 230.4 reduce-scatter.1
  1167.6 211.2 all-reduce.2

commit v4 on v3

--- a/solution.py
+++ b/solution.py
@@ -84,21 +84,23 @@
     )(x_rows, gain_vec.astype(jnp.float32)[None, :], w_qkv, cos_t, sin_t)
 
 
-def attend_kernel(q_ref, k_ref, v_ref, ctx_ref, *, block):
-    seq_len = q_ref.shape[0]
+def attend_kernel(q_all, k_all, v_all, ctx_all, *, block):
+    seq_len = q_all.shape[0]
     diag = lax.broadcasted_iota(jnp.int32, (block, block), 0) >= lax.broadcasted_iota(jnp.int32, (block, block), 1)
-    for start in range(0, seq_len, block):
-        stop = start + block
-        scores = dot_nt(q_ref[start:stop, :], k_ref[:stop, :]) * HEAD_DIM ** -0.5
-        last = jnp.where(diag, scores[:, start:], -1e30)
-        scores = last if start == 0 else jnp.concatenate([scores[:, :start], last], axis=1)
-        raised = jnp.exp(scores - jnp.max(scores, axis=1, keepdims=True))
-        probs = (raised * (1.0 / jnp.sum(raised, axis=1, keepdims=True))).astype(jnp.bfloat16)
-        ctx_ref[start:stop, :] = dot_nn(probs, v_ref[:stop, :]).astype(jnp.bfloat16)
-
-
-def head_spec(seq_len, offset):
-    return pl.BlockSpec((seq_len, HEAD_DIM), lambda s, h: (s, h + offset))
+    for first in range(0, q_all.shape[1], HEAD_DIM):
+        q_ref, k_ref, v_ref, ctx_ref = (ref.at[:, first:first + HEAD_DIM] for ref in (q_all, k_all, v_all, ctx_all))
+        for start in range(0, seq_len, block):
+            stop = start + block
+            scores = dot_nt(q_ref[start:stop, :], k_ref[:stop, :]) * HEAD_DIM ** -0.5
+            last = jnp.where(diag, scores[:, start:], -1e30)
+            scores = last if start == 0 else jnp.concatenate([scores[:, :start], last], axis=1)
+            raised = jnp.exp(scores - jnp.max(scores, axis=1, keepdims=True))
+            probs = (raised * (1.0 / jnp.sum(raised, axis=1, keepdims=True))).astype(jnp.bfloat16)
+            ctx_ref[start:stop, :] = dot_nn(probs, v_ref[:stop, :]).astype(jnp.bfloat16)
+
+
+def head_spec(seq_len, offset, heads=1):
+    return pl.BlockSpec((seq_len, heads * HEAD_DIM), lambda s, h: (s, h + offset // heads))
 
 
 def attend(qkv_rot, num_seqs):
@@ -107,9 +109,9 @@
     return pl.pallas_call(
         functools.partial(attend_kernel, block=min(256, seq_len)),
         out_shape=jax.ShapeDtypeStruct((num_tokens, width), jnp.bfloat16),
-        grid=(num_seqs, heads),
-        in_specs=[head_spec(seq_len, 0), head_spec(seq_len, heads), head_spec(seq_len, 2 * heads)],
-        out_specs=head_spec(seq_len, 0),
+        grid=(num_seqs, heads // 2),
+        in_specs=[head_spec(seq_len, 0, 2), head_spec(seq_len, heads, 2), head_spec(seq_len, 2 * heads, 2)],
+        out_specs=head_spec(seq_len, 0, 2),
         compiler_params=pltpu.CompilerParams(vmem_limit_bytes=VMEM_MAX, dimension_semantics=('arbitrary', 'arbitrary')),
         cost_estimate=pl.CostEstimate(flops=4 * num_tokens * seq_len * width, bytes_accessed=8 * num_tokens * width, transcendentals=num_tokens * seq_len * heads),
         name='attend',
@@ -195,6 +197,39 @@
     )(qkv_rot, qkv_rot, qkv_rot, d_context, cos_t, sin_t)
 
 
+def input_grad_kernel(dqkv_ref, w_ref, x_ref, gain_ref, dh_ref, dx_ref, dgain_ref):
+    d_out = dot_nt(dqkv_ref[...], w_ref[...])
+    x_f32 = x_ref[...].astype(jnp.float32)
+    inv_rms = lax.rsqrt(jnp.mean(x_f32 * x_f32, axis=-1, keepdims=True) + EPS)
+    part = jnp.sum(d_out * x_f32 * inv_rms, axis=0, keepdims=True)
+
+    @pl.when(pl.program_id(0) == 0)
+    def _():
+        dgain_ref[...] = jnp.zeros_like(dgain_ref)
+
+    dgain_ref[...] += part
+    d_scaled = d_out * gain_ref[...]
+    d_x = inv_rms * d_scaled - x_f32 * (inv_rms * inv_rms * inv_rms) * jnp.mean(d_scaled * x_f32, axis=-1, keepdims=True)
+    dx_ref[...] = (dh_ref[...].astype(jnp.float32) + d_x).astype(jnp.bfloat16)
+
+
+def input_grad(d_qkv, w_qkv, x_rows, gain_vec, d_h):
+    num_tokens, width = x_rows.shape
+    tile = min(512, num_tokens)
+    row_spec = pl.BlockSpec((tile, width), lambda r: (r, 0))
+    gain_spec = pl.BlockSpec((1, width), lambda r: (0, 0))
+    return pl.pallas_call(
+        input_grad_kernel,
+        out_shape=[jax.ShapeDtypeStruct((num_tokens, width), jnp.bfloat16), jax.ShapeDtypeStruct((1, width), jnp.float32)],
+        grid=(num_tokens // tile,),
+        in_specs=[pl.BlockSpec((tile, 3 * width), lambda r: (r, 0)), pl.BlockSpec((width, 3 * width), lambda r: (0, 0)), row_spec, gain_spec, row_spec],
+        out_specs=[row_spec, gain_spec],
+        compiler_params=pltpu.CompilerParams(vmem_limit_bytes=VMEM_MAX, dimension_semantics=('arbitrary',)),
+        cost_estimate=pl.CostEstimate(flops=6 * num_tokens * width * width, bytes_accessed=2 * width * (6 * num_tokens + 3 * width), transcendentals=num_tokens),
+        name='input_grad',
+    )(d_qkv, w_qkv, x_rows, gain_vec.astype(jnp.float32)[None, :], d_h)
+
+
 def choice_mask(idx_rows, num_experts):
     return (idx_rows[:, :, None] == jnp.arange(num_experts, dtype=jnp.int32)[None, None, :])
 
@@ -229,9 +264,10 @@
     end = jnp.minimum((before + totals).astype(jnp.int32), capacity)
     win_start = jnp.minimum(begin // ALIGN * ALIGN, capacity - WIN)
     win_count = jnp.maximum((end - win_start + WIN - 1) // WIN, 1)
+    filled = jnp.max(end, axis=2)
     most_group = jnp.max(win_count.reshape(num_dev, local_experts // GROUP, GROUP * blocks), axis=2)
     most_block = jnp.max(win_count, axis=1)
-    return jnp.transpose(slot_of, (0, 2, 1, 3)), win_start.reshape(-1), win_count.reshape(-1), most_group.reshape(-1), most_block.reshape(-1)
+    return jnp.transpose(slot_of, (0, 2, 1, 3)), begin.reshape(-1), win_count.reshape(-1), most_group.reshape(-1), most_block.reshape(-1), filled.reshape(-1)
 
 
 def expand_routes(idx_t, values_t, first_expert, local_experts):
@@ -241,16 +277,26 @@
     return jnp.transpose(dense.reshape(num_dev, local_experts, num_tokens // TOK_BLOCK, TOK_BLOCK), (0, 2, 1, 3))
 
 
-def gather_kernel(base_ref, start_ref, count_ref, most_ref, x_ref, dy_ref, slot_ref, gate_ref, *rest, blocks, capacity, group, scaled, dev_from):
+def window_start(begin, capacity):
+    return jnp.minimum(lax.div(begin, ALIGN) * ALIGN, capacity - WIN)
+
+
+def gather_kernel(base_ref, begin_ref, count_ref, most_ref, fill_ref, x_ref, dy_ref, slot_ref, gate_ref, *rest, blocks, capacity, group, scaled, dev_from):
     s_ref, dyr_ref = rest[-2:] if scaled else rest[-3:-1]
     g_ref = None if scaled else rest[-1]
     dev, part = pl.program_id(0) + dev_from, pl.program_id(1)
     experts = group * pl.num_programs(1)
-    s_ref[...] = jnp.zeros_like(s_ref)
-    dyr_ref[...] = jnp.zeros_like(dyr_ref)
+    overflow = most_ref[dev * pl.num_programs(1) + part] > 1
+
+    @pl.when(overflow)
+    def _():
+        s_ref[...] = jnp.zeros_like(s_ref)
+        dyr_ref[...] = jnp.zeros_like(dyr_ref)
+
     if g_ref is not None:
         g_ref[...] = jnp.zeros_like(g_ref)
     row_iota = lax.broadcasted_iota(jnp.int32, (WIN, TOK_BLOCK), 0)
+    line_iota = lax.broadcasted_iota(jnp.int32, (WIN, x_ref.shape[1]), 0)
 
     def at(i, blk):
         return (dev * experts + part * group + i) * blocks + blk
@@ -264,32 +310,47 @@
         gate_col = jnp.sum(jnp.where(hit, gate_row, 0.0), axis=1, keepdims=True)
         return jnp.where(hit, 1.0, 0.0).astype(jnp.bfloat16), gate_col
 
-    def deposit(i, first, s_rows, dy_rows, gate_col):
+    def deposit(i, first, s_rows, dy_rows, gate_col, begin=None):
         rows = pl.ds(pl.multiple_of(first, ALIGN), WIN)
-        s_ref[i, 0, rows, :] += s_rows.astype(jnp.bfloat16)
-        if scaled:
-            dyr_ref[i, 0, rows, :] += (dy_rows * gate_col).astype(jnp.bfloat16)
+        s_rows = s_rows.astype(jnp.bfloat16)
+        dy_rows = (dy_rows * gate_col if scaled else dy_rows).astype(jnp.bfloat16)
+        if begin is None:
+            s_ref[i, 0, rows, :] += s_rows
+            dyr_ref[i, 0, rows, :] += dy_rows
         else:
-            dyr_ref[i, 0, rows, :] += dy_rows.astype(jnp.bfloat16)
+            earlier = line_iota < begin - first
+            s_ref[i, 0, rows, :] = jnp.where(earlier, s_ref[i, 0, rows, :], s_rows)
+            dyr_ref[i, 0, rows, :] = jnp.where(earlier, dyr_ref[i, 0, rows, :], dy_rows)
+        if not scaled:
             g_ref[i, 0, rows, :] += gate_col
 
     for blk in range(blocks):
         tokens = slice(blk * TOK_BLOCK, (blk + 1) * TOK_BLOCK)
-        firsts = [start_ref[at(i, blk)] for i in range(group)]
+        begins = [begin_ref[at(i, blk)] for i in range(group)]
+        firsts = [window_start(begin, capacity) for begin in begins]
         parts = [window(i, blk, firsts[i]) for i in range(group)]
         pick = jnp.concatenate([p[0] for p in parts], axis=0)
         s_all = jnp.dot(pick, x_ref[tokens, :], preferred_element_type=jnp.float32)
         dy_all = jnp.dot(pick, dy_ref[tokens, :], preferred_element_type=jnp.float32)
         for i in range(group):
             rows = slice(i * WIN, (i + 1) * WIN)
-            deposit(i, firsts[i], s_all[rows], dy_all[rows], parts[i][1])
-
-    @pl.when(most_ref[dev * pl.num_programs(1) + part] > 1)
+            deposit(i, firsts[i], s_all[rows], dy_all[rows], parts[i][1], begins[i])
+
+    for i in range(group):
+        def blank(step, carry):
+            rows = pl.ds(pl.multiple_of(step * ALIGN, ALIGN), ALIGN)
+            s_ref[i, 0, rows, :] = jnp.zeros((ALIGN, s_ref.shape[-1]), jnp.bfloat16)
+            dyr_ref[i, 0, rows, :] = jnp.zeros((ALIGN, s_ref.shape[-1]), jnp.bfloat16)
+            return carry
+
+        lax.fori_loop(lax.div(fill_ref[dev * experts + part * group + i] + ALIGN - 1, ALIGN), capacity // ALIGN, blank, 0)
+
+    @pl.when(overflow)
     def _():
         for i in range(group):
             def per_block(blk, carry):
                 def extra(w, inner):
-                    floor = start_ref[at(i, blk)] + w * WIN
+                    floor = window_start(begin_ref[at(i, blk)], capacity) + w * WIN
                     first = jnp.minimum(floor, capacity - WIN)
                     pick, gate_col = window(i, blk, first, floor)
                     tokens = pl.ds(pl.multiple_of(blk * TOK_BLOCK, TOK_BLOCK), TOK_BLOCK)
@@ -304,7 +365,7 @@
 
 
 def gather_slots(base_dev, routes, dev_from, num_dev, gate_of, x_table, dy_table, filled, own_dev, capacity, scaled, from_all):
-    slot_of, win_start, win_count, most, _ = routes
+    slot_of, begin, win_count, most, _, fill = routes
     total_dev, blocks, experts, _ = slot_of.shape
     width = x_table.shape[1]
     num_tokens = blocks * TOK_BLOCK
@@ -334,17 +395,17 @@
         functools.partial(gather_kernel, blocks=blocks, capacity=capacity, group=group, scaled=scaled, dev_from=dev_from),
         out_shape=out_shape,
         grid_spec=pltpu.PrefetchScalarGridSpec(
-            num_scalar_prefetch=4, grid=(num_dev, experts // group),
+            num_scalar_prefetch=5, grid=(num_dev, experts // group),
             in_specs=[pl.BlockSpec((num_tokens, width), table_map), pl.BlockSpec((num_tokens, width), table_map),
                       pl.BlockSpec(route_block, slot_map), pl.BlockSpec(route_block, gate_map)]
                      + [pl.BlockSpec(memory_space=pl.ANY)] * len(held),
             out_specs=out_specs),
-        input_output_aliases={8 + i: i for i in range(len(held))},
+        input_output_aliases={9 + i: i for i in range(len(held))},
         compiler_params=pltpu.CompilerParams(vmem_limit_bytes=VMEM_MAX, dimension_semantics=('arbitrary', 'arbitrary')),
         cost_estimate=pl.CostEstimate(flops=4 * num_dev * blocks * experts * WIN * TOK_BLOCK * width,
                                       bytes_accessed=4 * num_dev * (num_tokens + experts * capacity) * width, transcendentals=0),
         name='gather_slots',
-    )(base_dev, win_start, win_count, most, x_table, dy_table, slot_of, gate_of, *held)
+    )(base_dev, begin, win_count, most, fill, x_table, dy_table, slot_of, gate_of, *held)
 
 
 def expert_kernel(*refs, own, chunk, held):
@@ -415,7 +476,29 @@
     )(*args)
 
 
-def combine_kernel(home_ref, start_ref, count_ref, most_ref, ds_ref, dg_ref, slot_ref, *rest, experts, blocks, capacity, dev_from):
+def weight_grad_kernel(*refs, count):
+    left_ref, rights, outs = refs[0], refs[1:1 + count], refs[1 + count:]
+    for right_ref, out_ref in zip(rights, outs):
+        out_ref[0] = lax.dot_general(left_ref[0], right_ref[0], (((0,), (0,)), ((), ())), preferred_element_type=jnp.float32)
+
+
+def weight_grads(left, *rights):
+    experts, rows, width = left.shape
+    count = len(rights)
+    row_spec = pl.BlockSpec((1, rows, width), lambda e: (e, 0, 0))
+    out_spec = pl.BlockSpec((1, width, width), lambda e: (e, 0, 0))
+    return pl.pallas_call(
+        functools.partial(weight_grad_kernel, count=count),
+        out_shape=[jax.ShapeDtypeStruct((experts, width, width), jnp.float32)] * count,
+        grid=(experts,), in_specs=[row_spec] * (1 + count), out_specs=[out_spec] * count,
+        compiler_params=pltpu.CompilerParams(vmem_limit_bytes=VMEM_MAX, dimension_semantics=('arbitrary',)),
+        cost_estimate=pl.CostEstimate(flops=2 * count * experts * rows * width * width,
+                                      bytes_accessed=experts * width * (2 * (1 + count) * rows + 4 * count * width), transcendentals=0),
+        name='weight_grads',
+    )(left, *rights)
+
+
+def combine_kernel(home_ref, begin_ref, count_ref, most_ref, ds_ref, dg_ref, slot_ref, *rest, experts, blocks, capacity, dev_from):
     out_ref, dgt_ref = rest[-2:]
     dev, blk = pl.program_id(0) + dev_from, pl.program_id(1)
     row_iota = lax.broadcasted_iota(jnp.int32, (WIN, TOK_BLOCK), 0)
@@ -432,7 +515,7 @@
     def spread(pick, rows):
         return lax.dot_general(pick, rows, (((0,), (0,)), ((), ())), preferred_element_type=jnp.float32)
 
-    parts = [window(e, start_ref[(dev * experts + e) * blocks + blk]) for e in range(experts)]
+    parts = [window(e, window_start(begin_ref[(dev * experts + e) * blocks + blk], capacity)) for e in range(experts)]
     out_ref[...] = spread(jnp.concatenate([p[0] for p in parts], axis=0), jnp.concatenate([p[1] for p in parts], axis=0))
     for e in range(experts):
         dgt_ref[0, 0, e:e + 1, :] = parts[e][2]
@@ -443,7 +526,7 @@
             at = (dev * experts + e) * blocks + blk
 
             def extra(w, carry):
-                floor = start_ref[at] + w * WIN
+                floor = window_start(begin_ref[at], capacity) + w * WIN
                 pick, rows, gate_row = window(e, jnp.minimum(floor, capacity - WIN), floor)
                 out_ref[...] += spread(pick, rows)
                 dgt_ref[0, 0, e:e + 1, :] += gate_row
@@ -453,7 +536,7 @@
 
 
 def combine_slots(home, routes, dev_from, num_dev, total_dev, d_slots, d_gate_slots, filled):
-    slot_of, win_start, win_count, _, most = routes
+    slot_of, begin, win_count, _, most, _ = routes
     experts, _, capacity, width = d_slots.shape
     blocks = slot_of.shape[1]
     num_tokens = blocks * TOK_BLOCK
@@ -479,7 +562,7 @@
         cost_estimate=pl.CostEstimate(flops=2 * num_dev * blocks * experts * WIN * TOK_BLOCK * width,
                                       bytes_accessed=2 * num_dev * (2 * num_tokens + experts * capacity) * width, transcendentals=0),
         name='combine_slots',
-    )(home, win_start, win_count, most, d_slots, d_gate_slots, slot_of, *held)
+    )(home, begin, win_count, most, d_slots, d_gate_slots, slot_of, *held)
 
 
 def dense_backward(saved_state, x_rows, dy_rows, d_logits, d_normed2_moe, norm1_gain, norm2_gain, w_qkv, w_attn_out, w_router):
@@ -492,10 +575,8 @@
     d_context = jnp.einsum('te,de->td', d_h, w_attn_out, preferred_element_type=jnp.float32).astype(jnp.bfloat16)
     d_qkv = attend_back(qkv_rot, d_context, cos_t, sin_t, num_seqs)
     d_w_qkv = jnp.einsum('td,te->de', normed1, d_qkv, preferred_element_type=jnp.float32)
-    d_normed1 = jnp.einsum('te,de->td', d_qkv, w_qkv, preferred_element_type=jnp.float32)
-    d_x_part, d_norm1_gain = rms_norm_bwd(x_rows, norm1_gain, d_normed1)
-    d_x = (d_h.astype(jnp.float32) + d_x_part).astype(jnp.bfloat16)
-    small = jnp.concatenate([d_w_router, d_norm1_gain[:, None], d_norm2_gain[:, None]], axis=1)
+    d_x, d_norm1_gain = input_grad(d_qkv, w_qkv, x_rows, norm1_gain, d_h)
+    small = jnp.concatenate([d_w_router, d_norm1_gain.T, d_norm2_gain[:, None]], axis=1)
     return d_x, d_qkv, (d_w_qkv, d_w_attn_out, small)
 
 
@@ -507,13 +588,10 @@
     exp_spec = P('ep', None, None)
 
     def swap(value, distance):
-        return lax.ppermute(value, 'ep', [(r, r ^ distance) for r in range(ep_size)])
+        return lax.ppermute(value, ('dp', 'ep'), [(r, r ^ distance) for r in range(num_dev)])
 
     def spread_routes(value):
-        near = jnp.stack([value, swap(value, 1)])
-        row = [near, jnp.stack([swap(value, 2), swap(value, 3)])]
-        far = lax.ppermute(jnp.concatenate(row, axis=0), 'dp', [(r, r ^ 1) for r in range(dp_size)])
-        return row + [far]
+        return [value] + [swap(value, distance) for distance in range(1, num_dev)]
 
     def local_step(x_tokens, dy_tokens, route_idx, norm1_gain, norm2_gain, w_qkv, w_attn_out, w_router, w_gate, w_up, w_down):
         num_seqs, seq_len, model_width = x_tokens.shape
@@ -532,7 +610,7 @@
         dy_all = lax.all_gather(dy_rows, ('dp', 'ep'), axis=0, tiled=True)
         idx_parts = spread_routes(idx_rows.T)
         dy_pair = swap(dy_rows, 1)
-        routes = slot_positions(jnp.concatenate(idx_parts, axis=0), first_expert, local_experts, capacity)
+        routes = slot_positions(jnp.stack(idx_parts), first_expert, local_experts, capacity)
 
         cos_t, sin_t = rope_tables(seq_len)
         normed1, qkv_rot = qkv_project(x_rows, norm1_gain, w_qkv, cos_t, sin_t)
@@ -546,7 +624,9 @@
         gates = probs_all * hits / picked_sum
         gate_t = jnp.sum(jnp.where(choice_mask(idx_rows, num_experts), gates[:, None, :], 0.0), axis=2).T
         x_all = lax.all_gather(normed2, ('dp', 'ep'), axis=0, tiled=True)
-        gate_near, gate_x, gate_far = (expand_routes(i, g, first_expert, local_experts) for i, g in zip(idx_parts, spread_routes(gate_t)))
+        gate_parts = spread_routes(gate_t)
+        gate_near, gate_x, gate_far = (expand_routes(jnp.stack(idx_parts[lo:hi]), jnp.stack(gate_parts[lo:hi]), first_expert, local_experts)
+                                       for lo, hi in ((0, 2), (2, ep_size), (ep_size, num_dev)))
 
         gather = functools.partial(gather_slots, me[None], routes, own_dev=ep_size, capacity=capacity)
         rows_of = lambda a: a.reshape(local_experts, -1, a.shape[-1])
@@ -567,17 +647,16 @@
         d_out, _ = lax.optimization_barrier((d_out, d_tok))
         s_arr, dy_arr = gather(4, 4, gate_far, x_all, dy_all, (s_arr, slots_of(d_out, num_dev)), scaled=True, from_all=True)
         s_all, d_out = rows_of(s_arr), rows_of(dy_arr)
-        hidden, dag, dau = expert_pass(False, tile, 2, 2, s_all, d_out, None, *weights, (hidden, dag, dau))
-        mm = functools.partial(jnp.einsum, preferred_element_type=jnp.float32)
-        d_w_down = mm('ecf,ecd->efd', hidden, d_out)
+        hidden, dag, dau = expert_pass(False, 2 * tile, 1, 1, s_all, d_out, None, *weights, (hidden, dag, dau))
+        hidden, d_normed2_moe = lax.optimization_barrier((hidden, d_normed2_moe))
+        d_w_down, = weight_grads(hidden, d_out)
 
         d_logits = gate_backward(probs_all, hits, picked_sum, d_gate_dense).astype(jnp.bfloat16)
         saved_state = (normed1, qkv_rot, context, h_rows, normed2, cos_t, sin_t, num_seqs)
         d_x, d_qkv, dense_grads = dense_backward(saved_state, x_rows, dy_rows, d_logits, d_normed2_moe, norm1_gain, norm2_gain, w_qkv, w_attn_out, w_router)
         d_w_qkv, d_w_attn_out, small = lax.psum(dense_grads, ('dp', 'ep'))
         s_all, dag, dau, _ = lax.optimization_barrier((s_all, dag, dau, d_qkv))
-        d_w_gate = mm('ecd,ecf->edf', s_all, dag)
-        d_w_up = mm('ecd,ecf->edf', s_all, dau)
+        d_w_gate, d_w_up = weight_grads(s_all, dag, dau)
         return (d_x.reshape(x_tokens.shape), small[:, num_experts], small[:, num_experts + 1], d_w_qkv, d_w_attn_out, small[:, :num_experts],
                 d_w_gate, d_w_up, d_w_down)
 

time: 1410 us -> 1250 us (0.89)
  matrix products: 406 us -> 56.8 us
  Pallas kernels: 772 us -> 1070 us
  waiting for transfers between devices: 123 us -> 10.1 us
    dot_general x4 -> x0, matrix products: 350 us -> none  [the longest x1 110 us: local_step(): d_w_up = mm('ecd,ecf->edf', s_all, dau)]
    pallas_call x0 -> x3, Pallas kernels: none -> 304 us  [the longest x2 281 us: weight_grads(): pl.pallas_call(functools.partial(weight_grad_kernel, count=count), out_sh...]
    psum x1, waiting for transfers between devices: 102 us -> 0.01 us  [local_step(): d_w_qkv, d_w_attn_out, small = lax.psum(dense_grads, ('dp', 'ep'))]
  transfers between devices with their start and end apart: 15 -> 21, of which waited for: 5 -> 6; matrix products, arithmetic and copies ran while one was open for 20% -> 5% of each run, Pallas kernels for 36% -> 63%
where the time goes in v4:
time: 1250 us; the launch traced here: 1240 us
  Pallas kernels  1070 us (86%)
  matrix products  56.8 us (5%)
  local copies, waits for them, and re-layouts  37.2 us (3%)
  other arithmetic  30.4 us (2%)
  starting transfers between devices  20.7 us (2%)
  between operations  14.5 us (1%)
    pallas_call x3, Pallas kernels, expert_pass(): pl.pallas_call(functools.partial(expert_kernel, own=own, chunk=min(256, w...  456 us
    pallas_call x2, Pallas kernels, weight_grads(): pl.pallas_call(functools.partial(weight_grad_kernel, count=count), out_sh...  281 us
    pallas_call x4, Pallas kernels, gather_slots(): pl.pallas_call(functools.partial(gather_kernel, blocks=blocks, capacity=c...  150 us
    pallas_call x1, Pallas kernels, attend_back(): pl.pallas_call(functools.partial(attend_back_kernel, block=min(256, seq_l...  55.2 us
    pallas_call x2, Pallas kernels, combine_slots(): pl.pallas_call(functools.partial(combine_kernel, experts=experts, blocks=...  51 us
    pallas_call x1, Pallas kernels, attend(): pl.pallas_call(functools.partial(attend_kernel, block=min(256, seq_len)),...  37.1 us
    unnamed x81, local copies, waits for them, and re-layouts  27.3 us
  transfers between devices with their start and end apart: 21, of which 6 were waited for; matrix products, arithmetic and copies ran while one was open for 5% of the time, Pallas kernels for 63%

profile of v4, /device:TPU:0, one launch (start us, length us, event | category | flops | bytes accessed | tf_op | source)
XLA Modules:
  0.0 1244.4 jit_solution(2399248596409523640)
XLA Ops:
  8.8 2.5 collective-permute-start.1
  20.2 21.3 %qkv_project.1 = (bf16[2048,1024]{1,0:T(8,128)(2,1)}, bf16[2048,3072]{1,0:T(8,128)(2,1)}) custom-call(bf16[2048,1024]{1,0:T(8,128)(2,1)} %bitcast.174, f32[1,1024]{1,0:T(1,128)} %bitcast.170, bf16[1024,3072]{1,0:T(8,128)(2,1)} %w_ref.3, f32[1024,128]{1,0:T(8,128)} %get-tuple-element.134.cos_ref, f32[1024,128]{1,0:T(8,128)} %get-tuple-element.135.sin_ref), custom_call_target="tpu_custom_call" | custom-call | flops 12884901888 | bytes 27262976 | tf_op jit(solution)/shard_map/qkv_project/pallas_call | solution.py:75
  41.5 2.5 collective-permute-start.5
  53.7 3.9 convert_reduce_fusion
  64.1 37.1 %attend.1 = bf16[2048,1024]{1,0:T(8,128)(2,1)} custom-call(bf16[2048,3072]{1,0:T(8,128)(2,1)} %get-tuple-element.59.q_all.k_all.v_all.q_ref.k_ref.v_ref, bf16[2048,3072]{1,0:T(8,128)(2,1)} %get-tuple-element.59.q_all.k_all.v_all.q_ref.k_ref.v_ref, bf16[2048,3072]{1,0:T(8,128)(2,1)} %get-tuple-element.59.q_all.k_all.v_all.q_ref.k_ref.v_ref), custom_call_target="tpu_custom_call" | custom-call | flops 8589934592 | bytes 16777216 | tf_op jit(solution)/shard_map/attend/pallas_call | solution.py:109
  101.2 9.1 fusion
  112.3 2.5 fusion.2.x_ref
  116.0 3.8 fusion.45
  126.7 4.0 collective-permute-done.15
  134.9 19.5 %gather_slots.4 = (bf16[16,8,320,1024]{3,2,1,0:T(8,128)(2,1)}, bf16[16,8,320,1024]{3,2,1,0:T(8,128)(2,1)}, f32[16,4,320,1]{3,2,1,0:T(8,128)}) custom-call(s32[1]{0:T(128)} %bitcast.18.base_ref, s32[1024]{0:T(1024)} %copy-done.22, s32[1024]{0:T(1024)} %fusion.36.count_ref, s32[32]{0:T(128)} %reshape.172.most_ref, s32[128]{0:T(128)} %reshape.174.fill_ref, ...), custom_call_target="tpu_custom_call" | custom-call | flops 8589934592 | bytes 29360128 | tf_op jit(solution)/shard_map/gather_slots/pallas_call | solution.py:394
  154.4 21.3 %gather_slots.5 = (bf16[16,8,320,1024]{3,2,1,0:T(8,128)(2,1)}, bf16[16,8,320,1024]{3,2,1,0:T(8,128)(2,1)}, f32[16,4,320,1]{3,2,1,0:T(8,128)}) custom-call(s32[1]{0:T(128)} %bitcast.18.base_ref, s32[1024]{0:T(1024)} %copy-done.22, s32[1024]{0:T(1024)} %fusion.36.count_ref, ...), custom_call_target="tpu_custom_call", output_to_operand_aliasing={{0}: (9, {}), {1}: (10, {}), {2}: (11, {})} | custom-call | flops 8589934592 | bytes 29360128 | tf_op jit(solution)/shard_map/gather_slots/pallas_call | solution.py:394
  175.7 150.5 %expert_own.2 = (bf16[16,2560,1024]{2,1,0:T(8,128)(2,1)}, bf16[16,2560,1024]{2,1,0:T(8,128)(2,1)}, bf16[16,2560,1024]{2,1,0:T(8,128)(2,1)}, bf16[16,2560,1024]{2...) custom-call(bf16[16,2560,1024]{2,1,0:T(8,128)(2,1)} %bitcast.32.refs_0_, ...), custom_call_target="tpu_custom_call", output_to_operand_aliasing={{3}: (1, {})} | custom-call | flops 128849018880 | bytes 247463936 | tf_op jit(solution)/shard_map/expert_own/pallas_call | solution.py:467
  326.2 26.0 %combine_slots.2 = (f32[8192,1024]{1,0:T(8,128)}, f32[4,8,16,256]{3,2,1,0:T(8,128)}) custom-call(s32[1]{0:T(128)} %bitcast.39.home_ref, s32[1024]{0:T(1024)} %copy-done.22, s32[1024]{0:T(1024)} %fusion.36.count_ref, s32[64]{0:T(128)} %reshape.173.most_ref, bf16[16,2,320,1024]{3,2,1,0:T(8,128)(2,1)} %bitcast.177, f32[16,2,320,1]{3,2,1,0:T(8,128)} %bitcast.178, ...), custom_call_target="tpu_custom_call" | custom-call | flops 8589934592 | bytes 37748736 | tf_op jit(solution)/shard_map/combine_slots/pallas_call | solution.py:548
  352.1 36.6 %gather_slots.6 = (bf16[16,8,320,1024]{3,2,1,0:T(8,128)(2,1)}, bf16[16,8,320,1024]{3,2,1,0:T(8,128)(2,1)}, f32[16,4,320,1]{3,2,1,0:T(8,128)}) custom-call(s32[1]{0:T(128)} %bitcast.18.base_ref, s32[1024]{0:T(1024)} %copy-done.22, s32[1024]{0:T(1024)} %fusion.36.count_ref, ...), custom_call_target="tpu_custom_call", output_to_operand_aliasing={{0}: (9, {}), {1}: (10, {}), {2}: (11, {})} | custom-call | flops 17179869184 | bytes 58720256 | tf_op jit(solution)/shard_map/gather_slots/pallas_call | solution.py:394
  388.7 147.5 %expert_own.3 = (bf16[16,2560,1024]{2,1,0:T(8,128)(2,1)}, bf16[16,2560,1024]{2,1,0:T(8,128)(2,1)}, bf16[16,2560,1024]{2,1,0:T(8,128)(2,1)}, bf16[16,2560,1024]{2...) custom-call(bf16[16,2560,1024]{2,1,0:T(8,128)(2,1)} %bitcast.36.refs, ...), custom_call_target="tpu_custom_call", output_to_operand_aliasing={{3}: (1, {}), {0}: (6, {}), {1}: (7, {}), {2}: (8, {})} | custom-call | flops 128849018880 | bytes 247463936 | tf_op jit(solution)/shard_map/expert_own/pallas_call | solution.py:467
  536.2 25.0 %combine_slots.3 = (f32[8192,1024]{1,0:T(8,128)}, f32[4,8,16,256]{3,2,1,0:T(8,128)}) custom-call(s32[1]{0:T(128)} %bitcast.39.home_ref, s32[1024]{0:T(1024)} %copy-done.22, s32[1024]{0:T(1024)} %fusion.36.count_ref, s32[64]{0:T(128)} %reshape.173.most_ref, bf16[16,2,320,1024]{3,2,1,0:T(8,128)(2,1)} %bitcast.120, ...), custom_call_target="tpu_custom_call", output_to_operand_aliasing={{0}: (7, {}), {1}: (8, {})} | custom-call | flops 8589934592 | bytes 37748736 | tf_op jit(solution)/shard_map/combine_slots/pallas_call | solution.py:548
  562.1 3.9 collective-permute-start.9
  574.8 4.2 all-to-all-start
  579.1 72.3 %gather_slots.7 = (bf16[16,8,320,1024]{3,2,1,0:T(8,128)(2,1)}, bf16[16,8,320,1024]{3,2,1,0:T(8,128)(2,1)}) custom-call(s32[1]{0:T(128)} %bitcast.18.base_ref, s32[1024]{0:T(1024)} %copy-done.22, s32[1024]{0:T(1024)} %fusion.36.count_ref, s32[32]{0:T(128)} %reshape.172.most_ref, ...), custom_call_target="tpu_custom_call", output_to_operand_aliasing={{0}: (9, {}), {1}: (10, {})} | custom-call | flops 34359738368 | bytes 117440512 | tf_op jit(solution)/shard_map/gather_slots/pallas_call | solution.py:394
  651.3 158.5 %expert_far.1 = (bf16[16,2560,1024]{2,1,0:T(8,128)(2,1)}, bf16[16,2560,1024]{2,1,0:T(8,128)(2,1)}, bf16[16,2560,1024]{2,1,0:T(8,128)(2,1)}) custom-call(bf16[16,2560,1024]{2,1,0:T(8,128)(2,1)} %bitcast.45.refs_0_, bf16[16,2560,1024]{2,1,0:T(8,128)(2,1)} %bitcast.46.refs_1_, ...), custom_call_target="tpu_custom_call", output_to_operand_aliasing={{0}: (5, {}), {1}: (6, {}), {2}: (7, {})} | custom-call | flops 128849018880 | bytes 394264576 | tf_op jit(solution)/shard_map/expert_far/pallas_call | solution.py:467
  815.3 3.7 fusion.48
  819.1 6.8 fusion.9
  826.2 3.2 fusion.6.dh_ref
  829.4 6.2 convolution_convert_fusion.dctx_ref
  835.7 6.2 fusion.47
  841.8 55.2 %attend_back.1.dqkv_ref = bf16[2048,3072]{1,0:T(8,128)(2,1)} custom-call(bf16[2048,3072]{1,0:T(8,128)(2,1)} %get-tuple-element.59.q_all.k_all.v_all.q_ref.k_ref.v_ref, bf16[2048,3072]{1,0:T(8,128)(2,1)} %get-tuple-element.59.q_all.k_all.v_all.q_ref.k_ref.v_ref, bf16[2048,3072]{1,0:T(8,128)(2,1)} %get-tuple-element.59.q_all.k_all.v_all.q_ref.k_ref.v_ref, ...), custom_call_target="tpu_custom_call" | custom-call | flops 21474836480 | bytes 29360128 | tf_op jit(solution)/shard_map/attend_back/pallas_call | solution.py:186
  897.0 22.7 %input_grad.1 = (bf16[2048,1024]{1,0:T(8,128)(2,1)}, f32[1,1024]{1,0:T(1,128)}) custom-call(bf16[2048,3072]{1,0:T(8,128)(2,1)} %attend_back.1.dqkv_ref, bf16[1024,3072]{1,0:T(8,128)(2,1)} %w_ref.3, bf16[2048,1024]{1,0:T(8,128)(2,1)} %bitcast.176, f32[1,1024]{1,0:T(1,128)} %bitcast.171, bf16[2048,1024]{1,0:T(8,128)(2,1)} %copy-done.8), custom_call_target="tpu_custom_call" | custom-call | flops 12884901888 | bytes 31457280 | tf_op jit(solution)/shard_map/input_grad/pallas_call | solution.py:221
  919.8 19.4 %fusion.46 = f32[1024,3072]{1,0:T(8,128)} fusion(bf16[2048,1024]{1,0:T(8,128)(2,1)} %get-tuple-element.98, bf16[2048,3072]{1,0:T(8,128)(2,1)} %attend_back.1.dqkv_ref), kind=kOutput, calls=%fused_computation.122 | convolution fusion | flops 12884901888 | bytes 29360128 | tf_op jit(solution)/shard_map/td,te->de/dot_general | solution.py:577
  940.0 184.2 %weight_grads.2 = (f32[16,1024,1024]{2,1,0:T(8,128)}, f32[16,1024,1024]{2,1,0:T(8,128)}) custom-call(bf16[16,2560,1024]{2,1,0:T(8,128)(2,1)} %bitcast.45.refs_0_, bf16[16,2560,1024]{2,1,0:T(8,128)(2,1)} %get-tuple-element.102.refs_1_, bf16[16,2560,1024]{2,1,0:T(8,128)(2,1)} %get-tuple-element.103.refs_2_), custom_call_target="tpu_custom_call" | custom-call | flops 171798691840 | bytes 385875968 | tf_op jit(solution)/shard_map/weight_grads/pallas_call | solution.py:490
  1124.2 97.2 %weight_grads.3 = f32[16,1024,1024]{2,1,0:T(8,128)} custom-call(bf16[16,2560,1024]{2,1,0:T(8,128)(2,1)} %get-tuple-element.106.refs_0_, bf16[16,2560,1024]{2,1,0:T(8,128)(2,1)} %bitcast.46.refs_1_), custom_call_target="tpu_custom_call" | custom-call | flops 85899345920 | bytes 234881024 | tf_op jit(solution)/shard_map/weight_grads/pallas_call | solution.py:490
  1224.5 11.1 copy.144
  1235.7 2.0 copy.145
  (172 shorter events, 59.9 us)
Async XLA Ops:
  7.2 12.4 copy-start.10
  7.2 344.9 %all-gather.5.cloned.1.call-start = ((), (), s32[]{:S(2)}) async-start(), calls=%async_computation.3 | async-start | bytes 37748736 | tf_op jit(solution)/shard_map/all_gather | solution.py:610
  7.9 344.2 %all-gather.3.cloned.1.call-start = ((), (), s32[]{:S(2)}) async-start(), calls=%async_computation.2 | async-start | bytes 37748736 | tf_op jit(solution)/shard_map/all_gather | solution.py:626
  8.0 33.5 %collective-permute-start = (s32[8,2048]{1,0:T(8,128)}, s32[8,2048]{1,0:T(8,128)}, u32[]{:S(2)}, u32[]{:S(2)}) collective-permute-start(s32[8,2048]{1,0:T(8,128)} %bitcast.136), channel_id=1, source_target_pairs={{0,1},{1,0},{2,3},{3,2},{4,5},{5,4},{6,7},{7,6}} | collective-permute-start | bytes 196616 | tf_op jit(solution)/shard_map/ppermute | solution.py:591
  8.8 36.7 %collective-permute-start.1 = (s32[8,2048]{1,0:T(8,128)}, s32[8,2048]{1,0:T(8,128)}, u32[]{:S(2)}, u32[]{:S(2)}) collective-permute-start(s32[8,2048]{1,0:T(8,128)} %bitcast.137), channel_id=1, source_target_pairs={{0,2},{1,3},{2,0},{3,1},{4,6},{5,7},{6,4},{7,5}} | collective-permute-start | bytes 196616 | tf_op jit(solution)/shard_map/ppermute | solution.py:591
  11.3 35.9 %collective-permute-start.2 = (s32[8,2048]{1,0:T(8,128)}, s32[8,2048]{1,0:T(8,128)}, u32[]{:S(2)}, u32[]{:S(2)}) collective-permute-start(s32[8,2048]{1,0:T(8,128)} %bitcast.138), channel_id=1, source_target_pairs={{0,3},{1,2},{2,1},{3,0},{4,7},{5,6},{6,5},{7,4}} | collective-permute-start | bytes 196616 | tf_op jit(solution)/shard_map/ppermute | solution.py:591
  11.4 37.3 %collective-permute-start.3 = (s32[8,2048]{1,0:T(8,128)}, s32[8,2048]{1,0:T(8,128)}, u32[]{:S(2)}, u32[]{:S(2)}) collective-permute-start(s32[8,2048]{1,0:T(8,128)} %bitcast.139), channel_id=1, source_target_pairs={{0,4},{1,5},{2,6},{3,7},{4,0},{5,1},{6,2},{7,3}} | collective-permute-start | bytes 196616 | tf_op jit(solution)/shard_map/ppermute | solution.py:591
  13.2 37.0 %collective-permute-start.4 = (s32[8,2048]{1,0:T(8,128)}, s32[8,2048]{1,0:T(8,128)}, u32[]{:S(2)}, u32[]{:S(2)}) collective-permute-start(s32[8,2048]{1,0:T(8,128)} %bitcast.140), channel_id=1, source_target_pairs={{0,5},{1,4},{2,7},{3,6},{4,1},{5,0},{6,3},{7,2}} | collective-permute-start | bytes 196616 | tf_op jit(solution)/shard_map/ppermute | solution.py:591
  41.5 16.4 %copy-start.30 = (s32[16]{0:T(128)}, s32[16]{0:T(128)S(1)}, u32[]{:S(2)}) copy-start(s32[16]{0:T(128)S(1)} %iota_add_fusion) | copy-start | bytes 196
  41.5 10.1 collective-permute-start.5
  45.5 6.9 collective-permute-start.6
  101.2 11.1 copy-start.26
  114.9 17.1 %copy-start.31 = (s32[16]{0:T(128)S(1)}, s32[16]{0:T(128)}, u32[]{:S(2)}) copy-start(s32[16]{0:T(128)} %copy-done.30) | copy-start | bytes 196
  114.9 704.2 %reduce-scatter.2.cloned.1.call-start = ((), (), s32[]{:S(2)}) async-start(), calls=%async_computation.4 | async-start | bytes 41943040 | tf_op jit(solution)/shard_map/reduce_scatter | solution.py:644
  114.9 39.4 %collective-permute-start.14 = (bf16[2048,1024]{1,0:T(8,128)(2,1)}, bf16[2048,1024]{1,0:T(8,128)(2,1)}, u32[]{:S(2)}, u32[]{:S(2)}) collective-permute-start(bf16[2048,1024]{1,0:T(8,128)(2,1)} %bitcast.122), channel_id=1, source_target_pairs={{0,1},{1,0},{2,3},{3,2},{4,5},{5,4},{6,7},{7,6}} | collective-permute-start | bytes 12582920 | tf_op jit(solution)/shard_map/ppermute | solution.py:591
  115.2 39.2 %collective-permute-start.13 = (bf16[2048,1024]{1,0:T(8,128)(2,1)}, bf16[2048,1024]{1,0:T(8,128)(2,1)}, u32[]{:S(2)}, u32[]{:S(2)}) collective-permute-start(bf16[2048,1024]{1,0:T(8,128)(2,1)} %fusion.2.x_ref), channel_id=1, source_target_pairs={{0,1},{1,0},{2,3},{3,2},{4,5},{5,4},{6,7},{7,6}} | collective-permute-start | bytes 12582920 | tf_op jit(solution)/shard_map/ppermute | solution.py:591
  122.8 7.9 collective-permute-start.15
  123.0 7.7 collective-permute-start.12
  124.4 7.6 collective-permute-start.11
  561.3 11.3 copy-start.32
  562.1 6.6 collective-permute-start.10
  562.1 6.9 collective-permute-start.9
  566.0 4.8 collective-permute-start.8
  566.0 6.5 collective-permute-start.7
  574.8 235.0 %all-to-all-start = ((f32[4,8,16,256]{3,2,1,0:T(8,128)}), f32[4,8,16,256]{3,2,1,0:T(8,128)}, u32[]{:S(2)}, u32[]{:S(2)}) async-start(f32[4,8,16,256]{3,2,1,0:T(8,128)} %get-tuple-element.95), calls=%async_computation.1 | async-start | bytes 1048576 | tf_op jit(solution)/shard_map/all_to_all | solution.py:645
  579.0 642.4 %all-reduce.3.cloned.1.call-start = ((), (), s32[]{:S(2)}) async-start(), calls=%async_computation.5 | async-start | bytes 34144256 | tf_op jit(solution)/shard_map/psum | solution.py:657
  809.8 9.2 copy-start.13
  809.8 9.2 copy-start.25
  919.7 19.4 %copy-start.9 = (f32[1024,64]{0,1:T(8,128)S(1)}, f32[1024,64]{0,1:T(8,128)}, u32[]{:S(2)}) copy-start(f32[1024,64]{0,1:T(8,128)} %fusion.48) | copy-start | bytes 786436
  919.7 19.4 %copy-start.29 = (f32[1024]{0:T(1024)S(1)}, f32[1024]{0:T(1024)}, u32[]{:S(2)}) copy-start(f32[1024]{0:T(1024)} %get-tuple-element.107) | copy-start | bytes 12292
  919.8 19.4 %copy-start.33 = (f32[1,1024]{1,0:T(1,128)S(1)}, f32[1,1024]{1,0:T(1,128)}, u32[]{:S(2)}) copy-start(f32[1,1024]{1,0:T(1,128)} %get-tuple-element.97) | copy-start | bytes 12292
  1224.5 11.1 copy-start.7
  (24 other events, 96.9 us)
Sparse Core Ops, SparseCore 0:
  9.8 162.0 all-gather.4
  173.7 155.0 all-gather.2
  561.4 229.2 reduce-scatter.1
  940.1 211.7 all-reduce.2

commit v5 on v4

--- a/solution.py
+++ b/solution.py
@@ -21,27 +21,16 @@
     return 8 * ((5 * num_tokens * top_k + 32 * num_experts - 1) // (32 * num_experts))
 
 
-def rms_norm(x_rows, gain_vec):
-    x_f32 = x_rows.astype(jnp.float32)
-    inv_rms = lax.rsqrt(jnp.mean(x_f32 * x_f32, axis=-1, keepdims=True) + EPS)
-    return (x_f32 * inv_rms * gain_vec.astype(jnp.float32)).astype(jnp.bfloat16)
-
-
-def rms_norm_bwd(x_rows, gain_vec, d_out):
-    x_f32 = x_rows.astype(jnp.float32)
-    inv_rms = lax.rsqrt(jnp.mean(x_f32 * x_f32, axis=-1, keepdims=True) + EPS)
-    d_gain = jnp.sum(d_out * x_f32 * inv_rms, axis=0)
-    d_scaled = d_out * gain_vec.astype(jnp.float32)
-    d_x = inv_rms * d_scaled - x_f32 * inv_rms ** 3 * jnp.mean(d_scaled * x_f32, axis=-1, keepdims=True)
-    return d_x, d_gain
-
-
 def dot_nn(left, right):
     return jnp.dot(left, right, preferred_element_type=jnp.float32)
 
 
 def dot_nt(left, right):
     return lax.dot_general(left, right, (((1,), (1,)), ((), ())), preferred_element_type=jnp.float32)
+
+
+def dot_tn(left, right):
+    return lax.dot_general(left, right, (((0,), (0,)), ((), ())), preferred_element_type=jnp.float32)
 
 
 def rope_tables(seq_len):
@@ -52,43 +41,52 @@
     return jnp.concatenate([cos_b, cos_b], axis=1), jnp.concatenate([-sin_b, sin_b], axis=1)
 
 
-def qkv_kernel(x_ref, gain_ref, w_ref, cos_ref, sin_ref, normed_ref, qkv_ref, *, rotated, chunk):
+def unit_rms(rows_f32):
+    return lax.rsqrt(jnp.mean(rows_f32 * rows_f32, axis=-1, keepdims=True) + EPS)
+
+
+def join_heads(ref):
+    return jnp.concatenate([ref[h] for h in range(ref.shape[0])], axis=1)
+
+
+def qkv_kernel(x_ref, gain_ref, w_ref, cos_ref, sin_ref, normed_t_ref, qkv_ref, *, rotated, chunk):
     x_f32 = x_ref[...].astype(jnp.float32)
-    inv_rms = lax.rsqrt(jnp.mean(x_f32 * x_f32, axis=-1, keepdims=True) + EPS)
-    normed_ref[...] = (x_f32 * inv_rms * gain_ref[...]).astype(jnp.bfloat16)
+    normed = (x_f32 * unit_rms(x_f32) * gain_ref[...]).astype(jnp.bfloat16)
+    normed_t_ref[...] = jnp.transpose(normed)
     for c in range(0, w_ref.shape[1], chunk):
-        acc = dot_nn(normed_ref[...], w_ref[:, c:c + chunk])
+        acc = dot_nn(normed, w_ref[:, c:c + chunk])
         for h in range(0, chunk, HEAD_DIM):
             head = acc[:, h:h + HEAD_DIM]
             if c + h < rotated:
                 head = head * cos_ref[...] + pltpu.roll(head, HEAD_DIM // 2, 1) * sin_ref[...]
-            qkv_ref[:, c + h:c + h + HEAD_DIM] = head.astype(jnp.bfloat16)
-
-
-def qkv_project(x_rows, gain_vec, w_qkv, cos_t, sin_t):
+            qkv_ref[(c + h) // HEAD_DIM] = head.astype(jnp.bfloat16)
+
+
+def qkv_project(x_rows, gain_row, w_qkv, cos_t, sin_t):
     num_tokens, width = x_rows.shape
     seq_len = cos_t.shape[0]
     tile = min(512, seq_len)
     per_seq = seq_len // tile
+    heads = 3 * width // HEAD_DIM
     row_spec = pl.BlockSpec((tile, width), lambda r: (r, 0))
     table_spec = pl.BlockSpec((tile, HEAD_DIM), lambda r: (lax.rem(r, per_seq), 0))
     return pl.pallas_call(
         functools.partial(qkv_kernel, rotated=2 * width, chunk=256),
-        out_shape=[jax.ShapeDtypeStruct((num_tokens, width), jnp.bfloat16), jax.ShapeDtypeStruct((num_tokens, 3 * width), jnp.bfloat16)],
+        out_shape=[jax.ShapeDtypeStruct((width, num_tokens), jnp.bfloat16), jax.ShapeDtypeStruct((heads, num_tokens, HEAD_DIM), jnp.bfloat16)],
         grid=(num_tokens // tile,),
         in_specs=[row_spec, pl.BlockSpec((1, width), lambda r: (0, 0)), pl.BlockSpec((width, 3 * width), lambda r: (0, 0)), table_spec, table_spec],
-        out_specs=[row_spec, pl.BlockSpec((tile, 3 * width), lambda r: (r, 0))],
+        out_specs=[pl.BlockSpec((width, tile), lambda r: (0, r)), pl.BlockSpec((heads, tile, HEAD_DIM), lambda r: (0, r, 0))],
         compiler_params=pltpu.CompilerParams(vmem_limit_bytes=VMEM_MAX, dimension_semantics=('arbitrary',)),
         cost_estimate=pl.CostEstimate(flops=6 * num_tokens * width * width, bytes_accessed=2 * width * (5 * num_tokens + 3 * width), transcendentals=num_tokens),
         name='qkv_project',
-    )(x_rows, gain_vec.astype(jnp.float32)[None, :], w_qkv, cos_t, sin_t)
+    )(x_rows, gain_row, w_qkv, cos_t, sin_t)
 
 
 def attend_kernel(q_all, k_all, v_all, ctx_all, *, block):
-    seq_len = q_all.shape[0]
+    count, seq_len, _ = q_all.shape
     diag = lax.broadcasted_iota(jnp.int32, (block, block), 0) >= lax.broadcasted_iota(jnp.int32, (block, block), 1)
-    for first in range(0, q_all.shape[1], HEAD_DIM):
-        q_ref, k_ref, v_ref, ctx_ref = (ref.at[:, first:first + HEAD_DIM] for ref in (q_all, k_all, v_all, ctx_all))
+    for head in range(count):
+        q_ref, k_ref, v_ref, ctx_ref = (ref.at[head] for ref in (q_all, k_all, v_all, ctx_all))
         for start in range(0, seq_len, block):
             stop = start + block
             scores = dot_nt(q_ref[start:stop, :], k_ref[:stop, :]) * HEAD_DIM ** -0.5
@@ -100,15 +98,15 @@
 
 
 def head_spec(seq_len, offset, heads=1):
-    return pl.BlockSpec((seq_len, heads * HEAD_DIM), lambda s, h: (s, h + offset // heads))
+    return pl.BlockSpec((heads, seq_len, HEAD_DIM), lambda s, h: (h + offset // heads, s, 0))
 
 
 def attend(qkv_rot, num_seqs):
-    num_tokens, width = qkv_rot.shape[0], qkv_rot.shape[1] // 3
-    seq_len, heads = num_tokens // num_seqs, width // HEAD_DIM
+    heads, num_tokens = qkv_rot.shape[0] // 3, qkv_rot.shape[1]
+    seq_len, width = num_tokens // num_seqs, heads * HEAD_DIM
     return pl.pallas_call(
         functools.partial(attend_kernel, block=min(256, seq_len)),
-        out_shape=jax.ShapeDtypeStruct((num_tokens, width), jnp.bfloat16),
+        out_shape=jax.ShapeDtypeStruct((heads, num_tokens, HEAD_DIM), jnp.bfloat16),
         grid=(num_seqs, heads // 2),
         in_specs=[head_spec(seq_len, 0, 2), head_spec(seq_len, heads, 2), head_spec(seq_len, 2 * heads, 2)],
         out_specs=head_spec(seq_len, 0, 2),
@@ -118,40 +116,25 @@
     )(qkv_rot, qkv_rot, qkv_rot)
 
 
-def attend_back_kernel(q_ref, k_ref, v_ref, dctx_ref, cos_ref, sin_ref, out_ref, stage, d_key, d_val, sems, *, block, heads):
-    seq, head = pl.program_id(0), pl.program_id(1)
-    step = seq * heads + head
-    slot = lax.rem(step, 2)
-    seq_len = q_ref.shape[0]
+def attend_back_kernel(q_ref, k_ref, v_ref, dctx_ref, cos_ref, sin_ref, out_ref, d_key, d_val, *, block):
+    seq_len = q_ref.shape[1]
     scale = HEAD_DIM ** -0.5
     causal = lax.broadcasted_iota(jnp.int32, (block, block), 0) <= lax.broadcasted_iota(jnp.int32, (block, block), 1)
 
-    def copies(at_step, at_slot):
-        at_seq, at_head = at_step // heads, lax.rem(at_step, heads)
-        rows = pl.ds(pl.multiple_of(at_seq * seq_len, seq_len), seq_len)
-        return [pltpu.make_async_copy(stage.at[at_slot, i],
-                                      out_ref.at[rows, pl.ds(pl.multiple_of((at_head + i * heads) * HEAD_DIM, HEAD_DIM), HEAD_DIM)],
-                                      sems.at[at_slot, i]) for i in range(3)]
-
-    @pl.when(step >= 2)
-    def _():
-        for copy in copies(step - 2, slot):
-            copy.wait()
-
-    def unrotate(grad):
+    def unrotate(grad, cos, sin):
         grad = grad.astype(jnp.bfloat16).astype(jnp.float32)
-        return lambda cos, sin: (grad * cos + pltpu.roll(grad * sin, HEAD_DIM // 2, 1)).astype(jnp.bfloat16)
-
-    key_t = jnp.transpose(k_ref[...])
+        return (grad * cos + pltpu.roll(grad * sin, HEAD_DIM // 2, 1)).astype(jnp.bfloat16)
+
+    key_t = jnp.transpose(k_ref[0])
     for start in range(0, seq_len, block):
         stop = start + block
-        query, d_ctx = q_ref[start:stop, :], dctx_ref[start:stop, :]
-        scores = dot_nt(k_ref[:stop, :], query) * scale
+        query, d_ctx = q_ref[0, start:stop, :], dctx_ref[0, start:stop, :]
+        scores = dot_nt(k_ref[0, :stop, :], query) * scale
         last = jnp.where(causal, scores[start:, :], -1e30)
         scores = last if start == 0 else jnp.concatenate([scores[:start, :], last], axis=0)
         raised = jnp.exp(scores - jnp.max(scores, axis=0, keepdims=True))
         probs = raised * (1.0 / jnp.sum(raised, axis=0, keepdims=True))
-        d_probs = dot_nt(v_ref[:stop, :], d_ctx).astype(jnp.bfloat16).astype(jnp.float32)
+        d_probs = dot_nt(v_ref[0, :stop, :], d_ctx).astype(jnp.bfloat16).astype(jnp.float32)
         mean_d = jnp.sum(d_probs * probs, axis=0, keepdims=True)
         d_scores = (probs * (d_probs - mean_d) * scale).astype(jnp.bfloat16)
         d_v = dot_nn(probs.astype(jnp.bfloat16), d_ctx)
@@ -165,42 +148,158 @@
             d_val[start:stop, :] = d_v[start:]
             d_key[start:stop, :] = d_k[start:]
         d_q = jnp.transpose(dot_nn(key_t[:, :stop], d_scores))
-        stage[slot, 0, start:stop, :] = unrotate(d_q)(cos_ref[start:stop, :], sin_ref[start:stop, :])
-    stage[slot, 1] = unrotate(d_key[...])(cos_ref[...], sin_ref[...])
-    stage[slot, 2] = d_val[...].astype(jnp.bfloat16)
-    for copy in copies(step, slot):
-        copy.start()
-
-    @pl.when(step == pl.num_programs(0) * heads - 1)
-    def _():
-        for copy in copies(step - 1, 1 - slot):
-            copy.wait()
-        for copy in copies(step, slot):
-            copy.wait()
+        out_ref[0, 0, start:stop, :] = unrotate(d_q, cos_ref[start:stop, :], sin_ref[start:stop, :])
+    out_ref[1, 0] = unrotate(d_key[...], cos_ref[...], sin_ref[...])
+    out_ref[2, 0] = d_val[...].astype(jnp.bfloat16)
 
 
 def attend_back(qkv_rot, d_context, cos_t, sin_t, num_seqs):
-    num_tokens, width = d_context.shape
-    seq_len, heads = num_tokens // num_seqs, width // HEAD_DIM
+    heads, num_tokens, _ = d_context.shape
+    seq_len, width = num_tokens // num_seqs, heads * HEAD_DIM
     table_spec = pl.BlockSpec((seq_len, HEAD_DIM), lambda s, h: (0, 0))
     return pl.pallas_call(
-        functools.partial(attend_back_kernel, block=min(256, seq_len), heads=heads),
-        out_shape=jax.ShapeDtypeStruct((num_tokens, 3 * width), jnp.bfloat16),
+        functools.partial(attend_back_kernel, block=min(256, seq_len)),
+        out_shape=jax.ShapeDtypeStruct((3, heads, num_tokens, HEAD_DIM), jnp.bfloat16),
         grid=(num_seqs, heads),
         in_specs=[head_spec(seq_len, 0), head_spec(seq_len, heads), head_spec(seq_len, 2 * heads), head_spec(seq_len, 0), table_spec, table_spec],
-        out_specs=pl.BlockSpec(memory_space=pl.ANY),
-        scratch_shapes=[pltpu.VMEM((2, 3, seq_len, HEAD_DIM), jnp.bfloat16), pltpu.VMEM((seq_len, HEAD_DIM), jnp.float32),
-                        pltpu.VMEM((seq_len, HEAD_DIM), jnp.float32), pltpu.SemaphoreType.DMA((2, 3))],
+        out_specs=pl.BlockSpec((3, 1, seq_len, HEAD_DIM), lambda s, h: (0, h, s, 0)),
+        scratch_shapes=[pltpu.VMEM((seq_len, HEAD_DIM), jnp.float32), pltpu.VMEM((seq_len, HEAD_DIM), jnp.float32)],
         compiler_params=pltpu.CompilerParams(vmem_limit_bytes=VMEM_MAX, dimension_semantics=('arbitrary', 'arbitrary')),
         cost_estimate=pl.CostEstimate(flops=10 * num_tokens * seq_len * width, bytes_accessed=14 * num_tokens * width, transcendentals=num_tokens * seq_len * heads),
         name='attend_back',
-    )(qkv_rot, qkv_rot, qkv_rot, d_context, cos_t, sin_t)
+    )(qkv_rot, qkv_rot, qkv_rot, d_context, cos_t, sin_t).reshape(3 * heads, num_tokens, HEAD_DIM)
+
+
+def choice_hits(idx_ref, shape):
+    lanes = lax.broadcasted_iota(jnp.int32, shape, 1)
+    hits = jnp.zeros(shape, jnp.float32)
+    for k in range(idx_ref.shape[1]):
+        hits += jnp.where(idx_ref[:, k:k + 1] == lanes, 1.0, 0.0)
+    return hits
+
+
+def router_kernel(ctx_ref, w_ref, x_ref, gain_ref, router_ref, idx_ref, h_ref, normed_ref, probs_ref, gate_ref, *, ranks, local_experts):
+    hidden = (x_ref[...].astype(jnp.float32) + dot_nn(join_heads(ctx_ref), w_ref[...])).astype(jnp.bfloat16)
+    h_ref[...] = hidden
+    h_f32 = hidden.astype(jnp.float32)
+    normed = (h_f32 * unit_rms(h_f32) * gain_ref[...]).astype(jnp.bfloat16)
+    normed_ref[...] = normed
+    logits = dot_nn(normed, router_ref[...])
+    lanes = lax.broadcasted_iota(jnp.int32, logits.shape, 1)
+    logits = jnp.where(lanes < ranks * local_experts, logits, -jnp.inf)
+    raised = jnp.exp(logits - jnp.max(logits, axis=1, keepdims=True))
+    probs = raised / jnp.sum(raised, axis=1, keepdims=True)
+    probs_ref[...] = probs
+    picked = probs * choice_hits(idx_ref, probs.shape)
+    gates = picked / jnp.sum(picked, axis=1, keepdims=True)
+    for blk in range(gates.shape[0] // TOK_BLOCK):
+        gate_t = jnp.transpose(gates[blk * TOK_BLOCK:(blk + 1) * TOK_BLOCK, :])
+        for rank in range(ranks):
+            gate_ref[rank, blk] = gate_t[rank * local_experts:(rank + 1) * local_experts, :]
+
+
+def route_tokens(context, w_attn_out, x_rows, gain_row, router_pad, idx_rows, ranks, local_experts):
+    heads, num_tokens, _ = context.shape
+    width, lanes = x_rows.shape[1], router_pad.shape[1]
+    tile = min(512, num_tokens)
+    row_spec = pl.BlockSpec((tile, width), lambda r: (r, 0))
+    whole = lambda shape: pl.BlockSpec(shape, lambda r: (0,) * len(shape))
+    return pl.pallas_call(
+        functools.partial(router_kernel, ranks=ranks, local_experts=local_experts),
+        out_shape=[jax.ShapeDtypeStruct((num_tokens, width), jnp.bfloat16), jax.ShapeDtypeStruct((num_tokens, width), jnp.bfloat16),
+                   jax.ShapeDtypeStruct((num_tokens, lanes), jnp.float32),
+                   jax.ShapeDtypeStruct((ranks, num_tokens // TOK_BLOCK, local_experts, TOK_BLOCK), jnp.float32)],
+        grid=(num_tokens // tile,),
+        in_specs=[pl.BlockSpec((heads, tile, HEAD_DIM), lambda r: (0, r, 0)), whole((width, width)), row_spec, whole((1, width)), whole((width, lanes)),
+                  pl.BlockSpec((tile, idx_rows.shape[1]), lambda r: (r, 0))],
+        out_specs=[row_spec, row_spec, pl.BlockSpec((tile, lanes), lambda r: (r, 0)),
+                   pl.BlockSpec((ranks, tile // TOK_BLOCK, local_experts, TOK_BLOCK), lambda r: (0, r, 0, 0))],
+        compiler_params=pltpu.CompilerParams(vmem_limit_bytes=VMEM_MAX, dimension_semantics=('arbitrary',)),
+        cost_estimate=pl.CostEstimate(flops=2 * num_tokens * width * (width + lanes), bytes_accessed=2 * width * (4 * num_tokens + width), transcendentals=num_tokens * lanes),
+        name='route_tokens',
+    )(context, w_attn_out, x_rows, gain_row, router_pad, idx_rows)
+
+
+def attn_out_grad_kernel(moe_ref, probs_ref, idx_ref, dgate_ref, h_ref, normed_ref, ctx_ref, dy_ref, gain_ref, router_ref, w_ref,
+                         dh_ref, dctx_ref, drouter_ref, dgain_ref, dw_ref, *, ranks, local_experts):
+    @pl.when(pl.program_id(0) == 0)
+    def _():
+        drouter_ref[...] = jnp.zeros_like(drouter_ref)
+        dgain_ref[...] = jnp.zeros_like(dgain_ref)
+        dw_ref[...] = jnp.zeros_like(dw_ref)
+
+    probs = probs_ref[...]
+    hits = choice_hits(idx_ref, probs.shape)
+    picked_sum = jnp.sum(probs * hits, axis=1, keepdims=True)
+    gates = probs * hits / picked_sum
+    blank = jnp.zeros((probs.shape[1] - ranks * local_experts, TOK_BLOCK), jnp.float32)
+    d_gates = jnp.concatenate([jnp.transpose(jnp.concatenate([dgate_ref[rank, blk] for rank in range(ranks)] + [blank], axis=0))
+                               for blk in range(dgate_ref.shape[1])], axis=0)
+    d_probs = hits * (d_gates - jnp.sum(d_gates * gates, axis=1, keepdims=True)) / picked_sum
+    d_logits = (probs * (d_probs - jnp.sum(d_probs * probs, axis=1, keepdims=True))).astype(jnp.bfloat16)
+    drouter_ref[...] += dot_tn(normed_ref[...], d_logits)
+    d_normed = moe_ref[...] + dot_nt(d_logits, router_ref[...])
+    h_f32 = h_ref[...].astype(jnp.float32)
+    inv_rms = unit_rms(h_f32)
+    dgain_ref[...] += jnp.sum(d_normed * h_f32 * inv_rms, axis=0, keepdims=True)
+    d_scaled = d_normed * gain_ref[...]
+    d_part = inv_rms * d_scaled - h_f32 * (inv_rms * inv_rms * inv_rms) * jnp.mean(d_scaled * h_f32, axis=-1, keepdims=True)
+    d_hidden = (dy_ref[...].astype(jnp.float32) + d_part).astype(jnp.bfloat16)
+    dh_ref[...] = d_hidden
+    d_ctx = dot_nt(d_hidden, w_ref[...]).astype(jnp.bfloat16)
+    for head in range(dctx_ref.shape[0]):
+        dctx_ref[head] = d_ctx[:, head * HEAD_DIM:(head + 1) * HEAD_DIM]
+    dw_ref[...] += dot_tn(join_heads(ctx_ref), d_hidden)
+
+
+def attn_out_grad(d_normed_moe, probs, idx_rows, d_gate_blk, h_rows, normed, context, dy_rows, gain_row, router_pad, w_attn_out):
+    heads, num_tokens, _ = context.shape
+    width, lanes = h_rows.shape[1], router_pad.shape[1]
+    ranks, _, local_experts, _ = d_gate_blk.shape
+    tile = min(512, num_tokens)
+    row_spec = pl.BlockSpec((tile, width), lambda r: (r, 0))
+    head_rows = pl.BlockSpec((heads, tile, HEAD_DIM), lambda r: (0, r, 0))
+    whole = lambda shape: pl.BlockSpec(shape, lambda r: (0,) * len(shape))
+    return pl.pallas_call(
+        functools.partial(attn_out_grad_kernel, ranks=ranks, local_experts=local_experts),
+        out_shape=[jax.ShapeDtypeStruct((num_tokens, width), jnp.bfloat16), jax.ShapeDtypeStruct(context.shape, jnp.bfloat16),
+                   jax.ShapeDtypeStruct((width, lanes), jnp.float32), jax.ShapeDtypeStruct((1, width), jnp.float32),
+                   jax.ShapeDtypeStruct((width, width), jnp.float32)],
+        grid=(num_tokens // tile,),
+        in_specs=[row_spec, pl.BlockSpec((tile, lanes), lambda r: (r, 0)), pl.BlockSpec((tile, idx_rows.shape[1]), lambda r: (r, 0)),
+                  pl.BlockSpec((ranks, tile // TOK_BLOCK, local_experts, TOK_BLOCK), lambda r: (0, r, 0, 0)), row_spec, row_spec, head_rows, row_spec,
+                  whole((1, width)), whole((width, lanes)), whole((width, width))],
+        out_specs=[row_spec, head_rows, whole((width, lanes)), whole((1, width)), whole((width, width))],
+        compiler_params=pltpu.CompilerParams(vmem_limit_bytes=VMEM_MAX, dimension_semantics=('arbitrary',)),
+        cost_estimate=pl.CostEstimate(flops=4 * num_tokens * width * (width + lanes), bytes_accessed=2 * width * (8 * num_tokens + 3 * width), transcendentals=num_tokens),
+        name='attn_out_grad',
+    )(d_normed_moe, probs, idx_rows, d_gate_blk, h_rows, normed, context, dy_rows, gain_row, router_pad, w_attn_out)
+
+
+def qkv_grad_kernel(normed_t_ref, dqkv_ref, dw_ref):
+    dw_ref[...] = dot_nn(normed_t_ref[...], join_heads(dqkv_ref))
+
+
+def qkv_grad(normed_t, d_qkv):
+    width, num_tokens = normed_t.shape
+    heads = d_qkv.shape[0]
+    group = 2 if heads % 4 else 4
+    return pl.pallas_call(
+        qkv_grad_kernel,
+        out_shape=jax.ShapeDtypeStruct((width, heads * HEAD_DIM), jnp.float32),
+        grid=(heads // group,),
+        in_specs=[pl.BlockSpec((width, num_tokens), lambda c: (0, 0)), pl.BlockSpec((group, num_tokens, HEAD_DIM), lambda c: (c, 0, 0))],
+        out_specs=pl.BlockSpec((width, group * HEAD_DIM), lambda c: (0, c)),
+        compiler_params=pltpu.CompilerParams(vmem_limit_bytes=VMEM_MAX, dimension_semantics=('arbitrary',)),
+        cost_estimate=pl.CostEstimate(flops=6 * num_tokens * width * width, bytes_accessed=2 * width * (4 * num_tokens + 6 * width), transcendentals=0),
+        name='qkv_grad',
+    )(normed_t, d_qkv)
 
 
 def input_grad_kernel(dqkv_ref, w_ref, x_ref, gain_ref, dh_ref, dx_ref, dgain_ref):
-    d_out = dot_nt(dqkv_ref[...], w_ref[...])
+    d_out = dot_nt(join_heads(dqkv_ref), w_ref[...])
     x_f32 = x_ref[...].astype(jnp.float32)
-    inv_rms = lax.rsqrt(jnp.mean(x_f32 * x_f32, axis=-1, keepdims=True) + EPS)
+    inv_rms = unit_rms(x_f32)
     part = jnp.sum(d_out * x_f32 * inv_rms, axis=0, keepdims=True)
 
     @pl.when(pl.program_id(0) == 0)
@@ -213,7 +312,7 @@
     dx_ref[...] = (dh_ref[...].astype(jnp.float32) + d_x).astype(jnp.bfloat16)
 
 
-def input_grad(d_qkv, w_qkv, x_rows, gain_vec, d_h):
+def input_grad(d_qkv, w_qkv, x_rows, gain_row, d_h):
     num_tokens, width = x_rows.shape
     tile = min(512, num_tokens)
     row_spec = pl.BlockSpec((tile, width), lambda r: (r, 0))
@@ -222,29 +321,12 @@
         input_grad_kernel,
         out_shape=[jax.ShapeDtypeStruct((num_tokens, width), jnp.bfloat16), jax.ShapeDtypeStruct((1, width), jnp.float32)],
         grid=(num_tokens // tile,),
-        in_specs=[pl.BlockSpec((tile, 3 * width), lambda r: (r, 0)), pl.BlockSpec((width, 3 * width), lambda r: (0, 0)), row_spec, gain_spec, row_spec],
+        in_specs=[pl.BlockSpec((d_qkv.shape[0], tile, HEAD_DIM), lambda r: (0, r, 0)), pl.BlockSpec((width, 3 * width), lambda r: (0, 0)), row_spec, gain_spec, row_spec],
         out_specs=[row_spec, gain_spec],
         compiler_params=pltpu.CompilerParams(vmem_limit_bytes=VMEM_MAX, dimension_semantics=('arbitrary',)),
         cost_estimate=pl.CostEstimate(flops=6 * num_tokens * width * width, bytes_accessed=2 * width * (6 * num_tokens + 3 * width), transcendentals=num_tokens),
         name='input_grad',
-    )(d_qkv, w_qkv, x_rows, gain_vec.astype(jnp.float32)[None, :], d_h)
-
-
-def choice_mask(idx_rows, num_experts):
-    return (idx_rows[:, :, None] == jnp.arange(num_experts, dtype=jnp.int32)[None, None, :])
-
-
-def gate_forward(logits, idx_rows, num_experts):
-    probs_all = jax.nn.softmax(logits, axis=-1)
-    hits = jnp.sum(choice_mask(idx_rows, num_experts).astype(jnp.float32), axis=1)
-    picked_sum = jnp.sum(probs_all * hits, axis=1, keepdims=True)
-    return probs_all, hits, picked_sum
-
-
-def gate_backward(probs_all, hits, picked_sum, d_gate_dense):
-    gates = probs_all * hits / picked_sum
-    d_probs = hits * (d_gate_dense - jnp.sum(d_gate_dense * gates, axis=1, keepdims=True)) / picked_sum
-    return probs_all * (d_probs - jnp.sum(d_probs * probs_all, axis=1, keepdims=True))
+    )(d_qkv, w_qkv, x_rows, gain_row, d_h)
 
 
 def slot_positions(idx_t, first_expert, local_experts, capacity):
@@ -270,13 +352,6 @@
     return jnp.transpose(slot_of, (0, 2, 1, 3)), begin.reshape(-1), win_count.reshape(-1), most_group.reshape(-1), most_block.reshape(-1), filled.reshape(-1)
 
 
-def expand_routes(idx_t, values_t, first_expert, local_experts):
-    num_dev, _, num_tokens = idx_t.shape
-    experts = first_expert + jnp.arange(local_experts, dtype=jnp.int32)
-    dense = jnp.sum(jnp.where(idx_t[:, None, :, :] == experts[None, :, None, None], values_t[:, None, :, :], 0.0), axis=2)
-    return jnp.transpose(dense.reshape(num_dev, local_experts, num_tokens // TOK_BLOCK, TOK_BLOCK), (0, 2, 1, 3))
-
-
 def window_start(begin, capacity):
     return jnp.minimum(lax.div(begin, ALIGN) * ALIGN, capacity - WIN)
 
@@ -295,6 +370,9 @@
 
     if g_ref is not None:
         g_ref[...] = jnp.zeros_like(g_ref)
+    cleared = max(capacity - 128, 0) // ALIGN * ALIGN
+    for ref in (s_ref, dyr_ref):
+        ref[:, 0, cleared:, :] = jnp.zeros((group, capacity - cleared, ref.shape[-1]), jnp.bfloat16)
     row_iota = lax.broadcasted_iota(jnp.int32, (WIN, TOK_BLOCK), 0)
     line_iota = lax.broadcasted_iota(jnp.int32, (WIN, x_ref.shape[1]), 0)
 
@@ -343,7 +421,7 @@
             dyr_ref[i, 0, rows, :] = jnp.zeros((ALIGN, s_ref.shape[-1]), jnp.bfloat16)
             return carry
 
-        lax.fori_loop(lax.div(fill_ref[dev * experts + part * group + i] + ALIGN - 1, ALIGN), capacity // ALIGN, blank, 0)
+        lax.fori_loop(lax.div(fill_ref[dev * experts + part * group + i] + ALIGN - 1, ALIGN), cleared // ALIGN, blank, 0)
 
     @pl.when(overflow)
     def _():
@@ -426,7 +504,7 @@
         silu = act_gate * sig
         hid_ref[0, :, cols] = (silu * act_up).astype(jnp.bfloat16)
         dau_ref[0, :, cols] = (d_hidden * silu).astype(jnp.bfloat16)
-        dag_ref[0, :, cols] = (d_hidden * act_up * (sig * (1.0 + act_gate * (1.0 - sig)))).astype(jnp.bfloat16)
+        dag_ref[0, :, cols] = (d_hidden * act_up * (sig + silu * (1.0 - sig))).astype(jnp.bfloat16)
     if own:
         d_gate = None
         for c in range(0, width, chunk):
@@ -479,7 +557,7 @@
 def weight_grad_kernel(*refs, count):
     left_ref, rights, outs = refs[0], refs[1:1 + count], refs[1 + count:]
     for right_ref, out_ref in zip(rights, outs):
-        out_ref[0] = lax.dot_general(left_ref[0], right_ref[0], (((0,), (0,)), ((), ())), preferred_element_type=jnp.float32)
+        out_ref[0] = dot_tn(left_ref[0], right_ref[0])
 
 
 def weight_grads(left, *rights):
@@ -498,13 +576,13 @@
     )(left, *rights)
 
 
-def combine_kernel(home_ref, begin_ref, count_ref, most_ref, ds_ref, dg_ref, slot_ref, *rest, experts, blocks, capacity, dev_from):
+def combine_kernel(home_ref, begin_ref, count_ref, most_ref, ds_ref, dg_ref, slot_ref, *rest, experts, blocks, capacity, dev_from, pairs):
     out_ref, dgt_ref = rest[-2:]
-    dev, blk = pl.program_id(0) + dev_from, pl.program_id(1)
+    dev = pl.program_id(0) + dev_from
     row_iota = lax.broadcasted_iota(jnp.int32, (WIN, TOK_BLOCK), 0)
 
-    def window(e, first, floor=None):
-        slot_row = slot_ref[0, 0, e:e + 1, :]
+    def window(e, sub, first, floor=None):
+        slot_row = slot_ref[0, sub, e:e + 1, :]
         hit = slot_row == row_iota + first
         if floor is not None:
             hit = hit & (slot_row >= floor)
@@ -512,27 +590,36 @@
         gate_row = jnp.sum(jnp.where(hit, dg_ref[e, 0, rows, :], 0.0), axis=0, keepdims=True)
         return jnp.where(hit, 1.0, 0.0).astype(jnp.bfloat16), ds_ref[e, 0, rows, :], gate_row
 
-    def spread(pick, rows):
-        return lax.dot_general(pick, rows, (((0,), (0,)), ((), ())), preferred_element_type=jnp.float32)
-
-    parts = [window(e, window_start(begin_ref[(dev * experts + e) * blocks + blk], capacity)) for e in range(experts)]
-    out_ref[...] = spread(jnp.concatenate([p[0] for p in parts], axis=0), jnp.concatenate([p[1] for p in parts], axis=0))
-    for e in range(experts):
-        dgt_ref[0, 0, e:e + 1, :] = parts[e][2]
-
-    @pl.when(most_ref[dev * blocks + blk] > 1)
-    def _():
+    for sub in range(pairs):
+        blk = pl.program_id(1) * pairs + sub
+        tokens = slice(sub * TOK_BLOCK, (sub + 1) * TOK_BLOCK)
+        parts = [window(e, sub, window_start(begin_ref[(dev * experts + e) * blocks + blk], capacity)) for e in range(experts)]
+        out_ref[tokens, :] = dot_tn(jnp.concatenate([p[0] for p in parts], axis=0), jnp.concatenate([p[1] for p in parts], axis=0))
         for e in range(experts):
-            at = (dev * experts + e) * blocks + blk
-
-            def extra(w, carry):
-                floor = window_start(begin_ref[at], capacity) + w * WIN
-                pick, rows, gate_row = window(e, jnp.minimum(floor, capacity - WIN), floor)
-                out_ref[...] += spread(pick, rows)
-                dgt_ref[0, 0, e:e + 1, :] += gate_row
-                return carry
-
-            lax.fori_loop(1, count_ref[at], extra, 0)
+            dgt_ref[0, sub, e:e + 1, :] = parts[e][2]
+
+    for sub in range(pairs):
+        blk = pl.program_id(1) * pairs + sub
+        tokens = slice(sub * TOK_BLOCK, (sub + 1) * TOK_BLOCK)
+
+        @pl.when(most_ref[dev * blocks + blk] > 1)
+        def _():
+            def per_expert(e, outer):
+                at = (dev * experts + e) * blocks + blk
+
+                def extra(w, carry):
+                    floor = window_start(begin_ref[at], capacity) + w * WIN
+                    first = jnp.minimum(floor, capacity - WIN)
+                    rows = pl.ds(pl.multiple_of(first, ALIGN), WIN)
+                    slot_row = slot_ref[0, sub, pl.ds(e, 1), :]
+                    hit = (slot_row == row_iota + first) & (slot_row >= floor)
+                    out_ref[tokens, :] += dot_tn(jnp.where(hit, 1.0, 0.0).astype(jnp.bfloat16), ds_ref[e, 0, rows, :])
+                    dgt_ref[0, sub, pl.ds(e, 1), :] += jnp.sum(jnp.where(hit, dg_ref[e, 0, rows, :], 0.0), axis=0, keepdims=True)
+                    return carry
+
+                return lax.fori_loop(1, count_ref[at], extra, outer)
+
+            lax.fori_loop(0, experts, per_expert, 0)
 
 
 def combine_slots(home, routes, dev_from, num_dev, total_dev, d_slots, d_gate_slots, filled):
@@ -540,44 +627,30 @@
     experts, _, capacity, width = d_slots.shape
     blocks = slot_of.shape[1]
     num_tokens = blocks * TOK_BLOCK
+    pairs = 2 if blocks % 2 == 0 else 1
 
     def home_of(d, home_ref):
         return lax.bitwise_xor(d + dev_from, home_ref[0])
 
     held = () if filled is None else tuple(filled)
     return pl.pallas_call(
-        functools.partial(combine_kernel, experts=experts, blocks=blocks, capacity=capacity, dev_from=dev_from),
+        functools.partial(combine_kernel, experts=experts, blocks=blocks, capacity=capacity, dev_from=dev_from, pairs=pairs),
         out_shape=[jax.ShapeDtypeStruct((total_dev * num_tokens, width), jnp.float32),
                    jax.ShapeDtypeStruct((total_dev, blocks, experts, TOK_BLOCK), jnp.float32)],
         grid_spec=pltpu.PrefetchScalarGridSpec(
-            num_scalar_prefetch=4, grid=(num_dev, blocks),
+            num_scalar_prefetch=4, grid=(num_dev, blocks // pairs),
             in_specs=[pl.BlockSpec((experts, 1, capacity, width), lambda d, b, *_: (0, d, 0, 0)),
                       pl.BlockSpec((experts, 1, capacity, 1), lambda d, b, *_: (0, d, 0, 0)),
-                      pl.BlockSpec((1, 1, experts, TOK_BLOCK), lambda d, b, *_: (d + dev_from, b, 0, 0))]
+                      pl.BlockSpec((1, pairs, experts, TOK_BLOCK), lambda d, b, *_: (d + dev_from, b, 0, 0))]
                      + [pl.BlockSpec(memory_space=pl.ANY)] * len(held),
-            out_specs=[pl.BlockSpec((TOK_BLOCK, width), lambda d, b, home_ref, *_: (home_of(d, home_ref) * blocks + b, 0)),
-                       pl.BlockSpec((1, 1, experts, TOK_BLOCK), lambda d, b, home_ref, *_: (home_of(d, home_ref), b, 0, 0))]),
+            out_specs=[pl.BlockSpec((pairs * TOK_BLOCK, width), lambda d, b, home_ref, *_: (home_of(d, home_ref) * (blocks // pairs) + b, 0)),
+                       pl.BlockSpec((1, pairs, experts, TOK_BLOCK), lambda d, b, home_ref, *_: (home_of(d, home_ref), b, 0, 0))]),
         input_output_aliases={7 + i: i for i in range(len(held))},
         compiler_params=pltpu.CompilerParams(vmem_limit_bytes=VMEM_MAX, dimension_semantics=('arbitrary', 'arbitrary')),
         cost_estimate=pl.CostEstimate(flops=2 * num_dev * blocks * experts * WIN * TOK_BLOCK * width,
                                       bytes_accessed=2 * num_dev * (2 * num_tokens + experts * capacity) * width, transcendentals=0),
         name='combine_slots',
     )(home, begin, win_count, most, d_slots, d_gate_slots, slot_of, *held)
-
-
-def dense_backward(saved_state, x_rows, dy_rows, d_logits, d_normed2_moe, norm1_gain, norm2_gain, w_qkv, w_attn_out, w_router):
-    normed1, qkv_rot, context, h_rows, normed2, cos_t, sin_t, num_seqs = saved_state
-    d_w_router = jnp.einsum('td,te->de', normed2, d_logits, preferred_element_type=jnp.float32)
-    d_normed2 = d_normed2_moe + jnp.einsum('te,de->td', d_logits, w_router, preferred_element_type=jnp.float32)
-    d_h_part, d_norm2_gain = rms_norm_bwd(h_rows, norm2_gain, d_normed2)
-    d_h = (dy_rows.astype(jnp.float32) + d_h_part).astype(jnp.bfloat16)
-    d_w_attn_out = jnp.einsum('td,te->de', context, d_h, preferred_element_type=jnp.float32)
-    d_context = jnp.einsum('te,de->td', d_h, w_attn_out, preferred_element_type=jnp.float32).astype(jnp.bfloat16)
-    d_qkv = attend_back(qkv_rot, d_context, cos_t, sin_t, num_seqs)
-    d_w_qkv = jnp.einsum('td,te->de', normed1, d_qkv, preferred_element_type=jnp.float32)
-    d_x, d_norm1_gain = input_grad(d_qkv, w_qkv, x_rows, norm1_gain, d_h)
-    small = jnp.concatenate([d_w_router, d_norm1_gain.T, d_norm2_gain[:, None]], axis=1)
-    return d_x, d_qkv, (d_w_qkv, d_w_attn_out, small)
 
 
 def solution(mesh):
@@ -613,20 +686,17 @@
         routes = slot_positions(jnp.stack(idx_parts), first_expert, local_experts, capacity)
 
         cos_t, sin_t = rope_tables(seq_len)
-        normed1, qkv_rot = qkv_project(x_rows, norm1_gain, w_qkv, cos_t, sin_t)
+        gain1, gain2 = norm1_gain.astype(jnp.float32)[None, :], norm2_gain.astype(jnp.float32)[None, :]
+        router_pad = jnp.pad(w_router, ((0, 0), (0, -num_experts % 128)))
+        normed1_t, qkv_rot = qkv_project(x_rows, gain1, w_qkv, cos_t, sin_t)
         qkv_rot, routes = lax.optimization_barrier((qkv_rot, routes))
         context = attend(qkv_rot, num_seqs)
-        h_rows = (x_rows.astype(jnp.float32) + jnp.dot(context, w_attn_out, preferred_element_type=jnp.float32)).astype(jnp.bfloat16)
-        normed2 = rms_norm(h_rows, norm2_gain)
+        h_rows, normed2, probs, gate_blk = route_tokens(context, w_attn_out, x_rows, gain2, router_pad, idx_rows, ep_size, local_experts)
         x_pair = swap(normed2, 1)
-        logits = jnp.dot(normed2, w_router, preferred_element_type=jnp.float32)
-        probs_all, hits, picked_sum = gate_forward(logits, idx_rows, num_experts)
-        gates = probs_all * hits / picked_sum
-        gate_t = jnp.sum(jnp.where(choice_mask(idx_rows, num_experts), gates[:, None, :], 0.0), axis=2).T
         x_all = lax.all_gather(normed2, ('dp', 'ep'), axis=0, tiled=True)
-        gate_parts = spread_routes(gate_t)
-        gate_near, gate_x, gate_far = (expand_routes(jnp.stack(idx_parts[lo:hi]), jnp.stack(gate_parts[lo:hi]), first_expert, local_experts)
-                                       for lo, hi in ((0, 2), (2, ep_size), (ep_size, num_dev)))
+        gate_for = [lax.dynamic_index_in_dim(gate_blk, jnp.bitwise_xor(ep_rank, d), axis=0, keepdims=False) for d in range(ep_size)]
+        gate_parts = [gate_for[0]] + [swap(gate_for[d % ep_size], d) for d in range(1, num_dev)]
+        gate_near, gate_x, gate_far = (jnp.stack(gate_parts[lo:hi]) for lo, hi in ((0, 2), (2, ep_size), (ep_size, num_dev)))
 
         gather = functools.partial(gather_slots, me[None], routes, own_dev=ep_size, capacity=capacity)
         rows_of = lambda a: a.reshape(local_experts, -1, a.shape[-1])
@@ -643,7 +713,6 @@
         d_tok, d_gate_t = combine(2, 2, d_slots=slots_of(ds_x, 2), d_gate_slots=slots_of(dg_x, 2), filled=combined)
         d_normed2_moe = lax.psum_scatter(d_tok, 'ep', scatter_dimension=0, tiled=True)
         d_gate_blk = lax.all_to_all(d_gate_t, 'ep', 0, 0, tiled=True)
-        d_gate_dense = jnp.transpose(d_gate_blk, (1, 3, 0, 2)).reshape(num_tokens, num_experts)
         d_out, _ = lax.optimization_barrier((d_out, d_tok))
         s_arr, dy_arr = gather(4, 4, gate_far, x_all, dy_all, (s_arr, slots_of(d_out, num_dev)), scaled=True, from_all=True)
         s_all, d_out = rows_of(s_arr), rows_of(dy_arr)
@@ -651,9 +720,13 @@
         hidden, d_normed2_moe = lax.optimization_barrier((hidden, d_normed2_moe))
         d_w_down, = weight_grads(hidden, d_out)
 
-        d_logits = gate_backward(probs_all, hits, picked_sum, d_gate_dense).astype(jnp.bfloat16)
-        saved_state = (normed1, qkv_rot, context, h_rows, normed2, cos_t, sin_t, num_seqs)
-        d_x, d_qkv, dense_grads = dense_backward(saved_state, x_rows, dy_rows, d_logits, d_normed2_moe, norm1_gain, norm2_gain, w_qkv, w_attn_out, w_router)
+        d_h, d_context, d_w_router, d_norm2_gain, d_w_attn_out = attn_out_grad(d_normed2_moe, probs, idx_rows, d_gate_blk, h_rows, normed2, context,
+                                                                               dy_rows, gain2, router_pad, w_attn_out)
+        d_qkv = attend_back(qkv_rot, d_context, cos_t, sin_t, num_seqs)
+        d_x, d_norm1_gain = input_grad(d_qkv, w_qkv, x_rows, gain1, d_h)
+        d_w_qkv = qkv_grad(normed1_t, d_qkv)
+        small = jnp.concatenate([d_w_router[:, :num_experts], d_norm1_gain.T, d_norm2_gain.T], axis=1)
+        dense_grads = (d_w_qkv, d_w_attn_out, small)
         d_w_qkv, d_w_attn_out, small = lax.psum(dense_grads, ('dp', 'ep'))
         s_all, dag, dau, _ = lax.optimization_barrier((s_all, dag, dau, d_qkv))
         d_w_gate, d_w_up = weight_grads(s_all, dag, dau)

time: 1250 us -> 1230 us (0.984)
  matrix products: 56.8 us -> 1.47 us
  Pallas kernels: 1070 us -> 1120 us
  other arithmetic: 30.4 us -> 17.6 us
    pallas_call x0 -> x3, Pallas kernels: none -> 59.4 us  [the longest x1 26.4 us: attn_out_grad(): pl.pallas_call(functools.partial(attn_out_grad_kernel, ranks=ranks, local...]
    dot_general x7 -> x0, matrix products: 55.3 us -> none  [the longest x1 19.4 us: dense_backward(): jnp.einsum('td,te->de', normed1, d_qkv, preferred_element_type=jnp.float32)]
    unnamed x81 -> x21, local copies, waits for them, and re-layouts: 27.3 us -> 26.4 us
  transfers between devices with their start and end apart: 21 -> 21, of which waited for: 6 -> 4; matrix products, arithmetic and copies ran while one was open for 5% -> 3% of each run, Pallas kernels for 63% -> 65%
where the time goes in v5:
time: 1230 us
  Pallas kernels  1120 us (91%)
  local copies, waits for them, and re-layouts  39.1 us (3%)
  starting transfers between devices  21.1 us (2%)
  other arithmetic  17.6 us (1%)
  between operations  14.2 us (1%)
    pallas_call x3, Pallas kernels, expert_pass(): pl.pallas_call(functools.partial(expert_kernel, own=own, chunk=min(256, w...  451 us
    pallas_call x2, Pallas kernels, weight_grads(): pl.pallas_call(functools.partial(weight_grad_kernel, count=count), out_sh...  282 us
    pallas_call x4, Pallas kernels, gather_slots(): pl.pallas_call(functools.partial(gather_kernel, blocks=blocks, capacity=c...  150 us
    pallas_call x1, Pallas kernels, attend_back(): pl.pallas_call(functools.partial(attend_back_kernel, block=min(256, seq_l...  54.8 us
    pallas_call x2, Pallas kernels, combine_slots(): pl.pallas_call(functools.partial(combine_kernel, experts=experts, blocks=...  48.7 us
    pallas_call x1, Pallas kernels, attend(): pl.pallas_call(functools.partial(attend_kernel, block=min(256, seq_len)),...  36.8 us
    pallas_call x1, Pallas kernels, attn_out_grad(): pl.pallas_call(functools.partial(attn_out_grad_kernel, ranks=ranks, local...  26.4 us
    unnamed x21, local copies, waits for them, and re-layouts  26.4 us
  transfers between devices with their start and end apart: 21, of which 4 were waited for; matrix products, arithmetic and copies ran while one was open for 3% of the time, Pallas kernels for 65%

profile of v5, /device:TPU:0, one launch (start us, length us, event | category | flops | bytes accessed | tf_op | source)
XLA Modules:
  0.0 1229.1 jit_solution(13586628054619599197)
XLA Ops:
  10.9 2.5 collective-permute-start.1
  20.7 2.0 fusion.8
  24.6 20.3 %qkv_project.1 = (bf16[1024,2048]{1,0:T(8,128)(2,1)}, bf16[24,2048,128]{2,1,0:T(8,128)(2,1)}) custom-call(bf16[2048,1024]{1,0:T(8,128)(2,1)} %bitcast.112, f32[1,1024]{1,0:T(1,128)} %bitcast.108, bf16[1024,3072]{1,0:T(8,128)(2,1)} %w_ref.7, f32[1024,128]{1,0:T(8,128)} %get-tuple-element.188.cos_ref, f32[1024,128]{1,0:T(8,128)} %get-tuple-element.189.sin_ref), custom_call_target="tpu_custom_call" | custom-call | flops 12884901888 | bytes 27262976 | tf_op jit(solution)/shard_map/qkv_project/pallas_call | solution.py:73
  44.9 2.7 collective-permute-start.5
  56.6 3.9 convert_reduce_fusion
  66.9 36.8 %attend.1.ctx_ref = bf16[8,2048,128]{2,1,0:T(8,128)(2,1)} custom-call(bf16[24,2048,128]{2,1,0:T(8,128)(2,1)} %get-tuple-element.68.q_all.k_all.v_all.q_ref.k_ref.v_ref, bf16[24,2048,128]{2,1,0:T(8,128)(2,1)} %get-tuple-element.68.q_all.k_all.v_all.q_ref.k_ref.v_ref, bf16[24,2048,128]{2,1,0:T(8,128)(2,1)} %get-tuple-element.68.q_all.k_all.v_all.q_ref.k_ref.v_ref), custom_call_target="tpu_custom_call" | custom-call | flops 8589934592 | bytes 16777216 | tf_op jit(solution)/shard_map/attend/pallas_call | solution.py:107
  103.7 14.6 %route_tokens.1 = (bf16[2048,1024]{1,0:T(8,128)(2,1)}, bf16[2048,1024]{1,0:T(8,128)(2,1)}, f32[2048,128]{1,0:T(8,128)}, f32[4,8,16,256]{3,2,1,0:T(8,128)}) custom-call(bf16[8,2048,128]{2,1,0:T(8,128)(2,1)} %attend.1.ctx_ref, bf16[1024,1024]{1,0:T(8,128)(2,1)} %w_ref.6, bf16[2048,1024]{1,0:T(8,128)(2,1)} %bitcast.113, f32[1,1024]{1,0:T(1,128)} %bitcast.110, ...), custom_call_target="tpu_custom_call" | custom-call | flops 4831838208 | bytes 18874368 | tf_op jit(solution)/shard_map/route_tokens/pallas_call | solution.py:207
  118.9 2.0 constant_dynamic-slice_fusion
  122.8 19.5 %gather_slots.4 = (bf16[16,8,320,1024]{3,2,1,0:T(8,128)(2,1)}, bf16[16,8,320,1024]{3,2,1,0:T(8,128)(2,1)}, f32[16,4,320,1]{3,2,1,0:T(8,128)}) custom-call(s32[1]{0:T(128)} %bitcast.17.base_ref, s32[1024]{0:T(1024)} %copy-done.2, s32[1024]{0:T(1024)} %fusion.24.count_ref, s32[32]{0:T(128)} %reshape.131.most_ref, s32[128]{0:T(128)} %reshape.133.fill_ref, ...), custom_call_target="tpu_custom_call" | custom-call | flops 8589934592 | bytes 29360128 | tf_op jit(solution)/shard_map/gather_slots/pallas_call | solution.py:472
  144.0 21.6 %gather_slots.5 = (bf16[16,8,320,1024]{3,2,1,0:T(8,128)(2,1)}, bf16[16,8,320,1024]{3,2,1,0:T(8,128)(2,1)}, f32[16,4,320,1]{3,2,1,0:T(8,128)}) custom-call(s32[1]{0:T(128)} %bitcast.17.base_ref, s32[1024]{0:T(1024)} %copy-done.2, s32[1024]{0:T(1024)} %fusion.24.count_ref, ...), custom_call_target="tpu_custom_call", output_to_operand_aliasing={{0}: (9, {}), {1}: (10, {}), {2}: (11, {})} | custom-call | flops 8589934592 | bytes 29360128 | tf_op jit(solution)/shard_map/gather_slots/pallas_call | solution.py:472
  165.6 148.9 %expert_own.2 = (bf16[16,2560,1024]{2,1,0:T(8,128)(2,1)}, bf16[16,2560,1024]{2,1,0:T(8,128)(2,1)}, bf16[16,2560,1024]{2,1,0:T(8,128)(2,1)}, bf16[16,2560,1024]{2...) custom-call(bf16[16,2560,1024]{2,1,0:T(8,128)(2,1)} %bitcast.31.refs_0_, ...), custom_call_target="tpu_custom_call", output_to_operand_aliasing={{3}: (1, {})} | custom-call | flops 128849018880 | bytes 247463936 | tf_op jit(solution)/shard_map/expert_own/pallas_call | solution.py:545
  314.5 25.1 %combine_slots.2 = (f32[8192,1024]{1,0:T(8,128)}, f32[4,8,16,256]{3,2,1,0:T(8,128)}) custom-call(s32[1]{0:T(128)} %bitcast.38.home_ref, s32[1024]{0:T(1024)} %copy-done.2, s32[1024]{0:T(1024)} %fusion.24.count_ref, s32[64]{0:T(128)} %reshape.132.most_ref, bf16[16,2,320,1024]{3,2,1,0:T(8,128)(2,1)} %bitcast.115, f32[16,2,320,1]{3,2,1,0:T(8,128)} %bitcast.118, ...), custom_call_target="tpu_custom_call" | custom-call | flops 8589934592 | bytes 37748736 | tf_op jit(solution)/shard_map/combine_slots/pallas_call | solution.py:636
  339.6 36.9 %gather_slots.6 = (bf16[16,8,320,1024]{3,2,1,0:T(8,128)(2,1)}, bf16[16,8,320,1024]{3,2,1,0:T(8,128)(2,1)}, f32[16,4,320,1]{3,2,1,0:T(8,128)}) custom-call(s32[1]{0:T(128)} %bitcast.17.base_ref, s32[1024]{0:T(1024)} %copy-done.2, s32[1024]{0:T(1024)} %fusion.24.count_ref, ...), custom_call_target="tpu_custom_call", output_to_operand_aliasing={{0}: (9, {}), {1}: (10, {}), {2}: (11, {})} | custom-call | flops 17179869184 | bytes 58720256 | tf_op jit(solution)/shard_map/gather_slots/pallas_call | solution.py:472
  376.5 147.3 %expert_own.3 = (bf16[16,2560,1024]{2,1,0:T(8,128)(2,1)}, bf16[16,2560,1024]{2,1,0:T(8,128)(2,1)}, bf16[16,2560,1024]{2,1,0:T(8,128)(2,1)}, bf16[16,2560,1024]{2...) custom-call(bf16[16,2560,1024]{2,1,0:T(8,128)(2,1)} %bitcast.35.refs, ...), custom_call_target="tpu_custom_call", output_to_operand_aliasing={{3}: (1, {}), {0}: (6, {}), {1}: (7, {}), {2}: (8, {})} | custom-call | flops 128849018880 | bytes 247463936 | tf_op jit(solution)/shard_map/expert_own/pallas_call | solution.py:545
  523.8 23.6 %combine_slots.3 = (f32[8192,1024]{1,0:T(8,128)}, f32[4,8,16,256]{3,2,1,0:T(8,128)}) custom-call(s32[1]{0:T(128)} %bitcast.38.home_ref, s32[1024]{0:T(1024)} %copy-done.2, s32[1024]{0:T(1024)} %fusion.24.count_ref, s32[64]{0:T(128)} %reshape.132.most_ref, bf16[16,2,320,1024]{3,2,1,0:T(8,128)(2,1)} %bitcast.84, ...), custom_call_target="tpu_custom_call", output_to_operand_aliasing={{0}: (7, {}), {1}: (8, {})} | custom-call | flops 8589934592 | bytes 37748736 | tf_op jit(solution)/shard_map/combine_slots/pallas_call | solution.py:636
  547.4 4.7 collective-permute-start.9
  553.9 3.6 collective-permute-done.9
  557.5 3.4 collective-permute-done.8
  560.9 2.8 collective-permute-done.7
  564.5 4.2 all-to-all-start
  568.8 72.0 %gather_slots.7 = (bf16[16,8,320,1024]{3,2,1,0:T(8,128)(2,1)}, bf16[16,8,320,1024]{3,2,1,0:T(8,128)(2,1)}) custom-call(s32[1]{0:T(128)} %bitcast.17.base_ref, s32[1024]{0:T(1024)} %copy-done.2, s32[1024]{0:T(1024)} %fusion.24.count_ref, s32[32]{0:T(128)} %reshape.131.most_ref, s32[128]{0:T(128)} %reshape.133.fill_ref, ...), custom_call_target="tpu_custom_call", output_to_operand_aliasing={{0}: (9, {}), {1}: (10, {})} | custom-call | flops 34359738368 | bytes 117440512 | tf_op jit(solution)/shard_map/gather_slots/pallas_call | solution.py:472
  640.8 154.6 %expert_far.1 = (bf16[16,2560,1024]{2,1,0:T(8,128)(2,1)}, bf16[16,2560,1024]{2,1,0:T(8,128)(2,1)}, bf16[16,2560,1024]{2,1,0:T(8,128)(2,1)}) custom-call(bf16[16,2560,1024]{2,1,0:T(8,128)(2,1)} %bitcast.44.refs_0_, bf16[16,2560,1024]{2,1,0:T(8,128)(2,1)} %bitcast.45.refs_1_, ...), custom_call_target="tpu_custom_call", output_to_operand_aliasing={{0}: (5, {}), {1}: (6, {}), {2}: (7, {})} | custom-call | flops 128849018880 | bytes 394264576 | tf_op jit(solution)/shard_map/expert_far/pallas_call | solution.py:545
  795.4 26.4 %attn_out_grad.1 = (bf16[2048,1024]{1,0:T(8,128)(2,1)}, bf16[8,2048,128]{2,1,0:T(8,128)(2,1)}, f32[1024,128]{1,0:T(8,128)}, f32[1,1024]{1,0:T(1,128)}, f32[1024,1024]{1,0:T(8,128)}) custom-call(f32[2048,1024]{1,0:T(8,128)} %reduce-scatter.2.cloned.1.call-done.moe_ref, f32[2048,128]{1,0:T(8,128)} %get-tuple-element.106.probs_ref, s32[2048,8]{1,0:T(8,128)} %bitcast.88, ...), custom_call_target="tpu_custom_call" | custom-call | flops 9663676416 | bytes 39845888 | tf_op jit(solution)/shard_map/attn_out_grad/pallas_call | solution.py:263
  821.8 54.8 %attend_back.1 = bf16[3,8,2048,128]{3,2,1,0:T(8,128)(2,1)} custom-call(bf16[24,2048,128]{2,1,0:T(8,128)(2,1)} %get-tuple-element.68.q_all.k_all.v_all.q_ref.k_ref.v_ref, bf16[24,2048,128]{2,1,0:T(8,128)(2,1)} %get-tuple-element.68.q_all.k_all.v_all.q_ref.k_ref.v_ref, bf16[24,2048,128]{2,1,0:T(8,128)(2,1)} %get-tuple-element.68.q_all.k_all.v_all.q_ref.k_ref.v_ref, ...), custom_call_target="tpu_custom_call" | custom-call | flops 21474836480 | bytes 29360128 | tf_op jit(solution)/shard_map/attend_back/pallas_call | solution.py:160
  878.3 22.3 %input_grad.1 = (bf16[2048,1024]{1,0:T(8,128)(2,1)}, f32[1,1024]{1,0:T(1,128)}) custom-call(bf16[24,2048,128]{2,1,0:T(8,128)(2,1)} %bitcast.116, bf16[1024,3072]{1,0:T(8,128)(2,1)} %w_ref.7, bf16[2048,1024]{1,0:T(8,128)(2,1)} %bitcast.114, f32[1,1024]{1,0:T(1,128)} %bitcast.109, bf16[2048,1024]{1,0:T(8,128)(2,1)} %get-tuple-element.110.dh_ref), custom_call_target="tpu_custom_call" | custom-call | flops 12884901888 | bytes 31457280 | tf_op jit(solution)/shard_map/input_grad/pallas_call | solution.py:320
  902.4 18.4 %qkv_grad.1 = f32[1024,3072]{1,0:T(8,128)} custom-call(bf16[1024,2048]{1,0:T(8,128)(2,1)} %get-tuple-element.115.normed_t_ref, bf16[24,2048,128]{2,1,0:T(8,128)(2,1)} %bitcast.117), custom_call_target="tpu_custom_call" | custom-call | flops 12884901888 | bytes 29360128 | tf_op jit(solution)/shard_map/qkv_grad/pallas_call | solution.py:287
  920.7 2.5 pad_maximum_fusion.3
  923.3 184.7 %weight_grads.2 = (f32[16,1024,1024]{2,1,0:T(8,128)}, f32[16,1024,1024]{2,1,0:T(8,128)}) custom-call(bf16[16,2560,1024]{2,1,0:T(8,128)(2,1)} %bitcast.44.refs_0_, bf16[16,2560,1024]{2,1,0:T(8,128)(2,1)} %get-tuple-element.120.refs_1_, bf16[16,2560,1024]{2,1,0:T(8,128)(2,1)} %get-tuple-element.121.refs_2_), custom_call_target="tpu_custom_call" | custom-call | flops 171798691840 | bytes 385875968 | tf_op jit(solution)/shard_map/weight_grads/pallas_call | solution.py:568
  1107.9 96.9 %weight_grads.3 = f32[16,1024,1024]{2,1,0:T(8,128)} custom-call(bf16[16,2560,1024]{2,1,0:T(8,128)(2,1)} %get-tuple-element.124.refs_0_, bf16[16,2560,1024]{2,1,0:T(8,128)(2,1)} %bitcast.45.refs_1_), custom_call_target="tpu_custom_call" | custom-call | flops 85899345920 | bytes 234881024 | tf_op jit(solution)/shard_map/weight_grads/pallas_call | solution.py:568
  1204.8 2.4 slice_reduce_fusion
  1209.2 11.1 copy.152
  1220.3 2.0 copy.153
  (90 shorter events, 40.5 us)
Async XLA Ops:
  7.2 332.4 %all-gather.5.cloned.1.call-start = ((), (), s32[]{:S(2)}) async-start(), calls=%async_computation.3 | async-start | bytes 37748736 | tf_op jit(solution)/shard_map/all_gather | solution.py:683
  7.9 331.7 %all-gather.3.cloned.1.call-start = ((), (), s32[]{:S(2)}) async-start(), calls=%async_computation.2 | async-start | bytes 37748736 | tf_op jit(solution)/shard_map/all_gather | solution.py:696
  9.1 7.5 copy-start
  10.1 34.7 %collective-permute-start = (s32[8,2048]{1,0:T(8,128)}, s32[8,2048]{1,0:T(8,128)}, u32[]{:S(2)}, u32[]{:S(2)}) collective-permute-start(s32[8,2048]{1,0:T(8,128)} %copy.93), channel_id=1, source_target_pairs={{0,1},{1,0},{2,3},{3,2},{4,5},{5,4},{6,7},{7,6}} | collective-permute-start | bytes 196616 | tf_op jit(solution)/shard_map/ppermute | solution.py:664
  10.9 38.1 %collective-permute-start.1 = (s32[8,2048]{1,0:T(8,128)}, s32[8,2048]{1,0:T(8,128)}, u32[]{:S(2)}, u32[]{:S(2)}) collective-permute-start(s32[8,2048]{1,0:T(8,128)} %copy.93), channel_id=1, source_target_pairs={{0,2},{1,3},{2,0},{3,1},{4,6},{5,7},{6,4},{7,5}} | collective-permute-start | bytes 196616 | tf_op jit(solution)/shard_map/ppermute | solution.py:664
  13.4 37.1 %collective-permute-start.2 = (s32[8,2048]{1,0:T(8,128)}, s32[8,2048]{1,0:T(8,128)}, u32[]{:S(2)}, u32[]{:S(2)}) collective-permute-start(s32[8,2048]{1,0:T(8,128)} %copy.93), channel_id=1, source_target_pairs={{0,3},{1,2},{2,1},{3,0},{4,7},{5,6},{6,5},{7,4}} | collective-permute-start | bytes 196616 | tf_op jit(solution)/shard_map/ppermute | solution.py:664
  13.5 38.4 %collective-permute-start.3 = (s32[8,2048]{1,0:T(8,128)}, s32[8,2048]{1,0:T(8,128)}, u32[]{:S(2)}, u32[]{:S(2)}) collective-permute-start(s32[8,2048]{1,0:T(8,128)} %copy.93), channel_id=1, source_target_pairs={{0,4},{1,5},{2,6},{3,7},{4,0},{5,1},{6,2},{7,3}} | collective-permute-start | bytes 196616 | tf_op jit(solution)/shard_map/ppermute | solution.py:664
  15.3 38.1 %collective-permute-start.4 = (s32[8,2048]{1,0:T(8,128)}, s32[8,2048]{1,0:T(8,128)}, u32[]{:S(2)}, u32[]{:S(2)}) collective-permute-start(s32[8,2048]{1,0:T(8,128)} %copy.93), channel_id=1, source_target_pairs={{0,5},{1,4},{2,7},{3,6},{4,1},{5,0},{6,3},{7,2}} | collective-permute-start | bytes 196616 | tf_op jit(solution)/shard_map/ppermute | solution.py:664
  44.9 10.1 collective-permute-start.5
  49.0 7.0 collective-permute-start.6
  62.5 4.4 copy-start.2
  118.3 677.0 %reduce-scatter.2.cloned.1.call-start = ((), (), s32[]{:S(2)}) async-start(), calls=%async_computation.4 | async-start | bytes 41943040 | tf_op jit(solution)/shard_map/reduce_scatter | solution.py:714
  118.4 25.6 %collective-permute-start.14 = (bf16[2048,1024]{1,0:T(8,128)(2,1)}, bf16[2048,1024]{1,0:T(8,128)(2,1)}, u32[]{:S(2)}, u32[]{:S(2)}) collective-permute-start(bf16[2048,1024]{1,0:T(8,128)(2,1)} %bitcast.94), channel_id=1, source_target_pairs={{0,1},{1,0},{2,3},{3,2},{4,5},{5,4},{6,7},{7,6}} | collective-permute-start | bytes 12582920 | tf_op jit(solution)/shard_map/ppermute | solution.py:664
  118.5 25.5 %collective-permute-start.13 = (bf16[2048,1024]{1,0:T(8,128)(2,1)}, bf16[2048,1024]{1,0:T(8,128)(2,1)}, u32[]{:S(2)}, u32[]{:S(2)}) collective-permute-start(bf16[2048,1024]{1,0:T(8,128)(2,1)} %get-tuple-element.73.x_ref.normed_ref), channel_id=1, source_target_pairs={{0,1},{1,0},{2,3},{3,2},{4,5},{5,4},{6,7},{7,6}} | collective-permute-start | bytes 12582920 | tf_op jit(solution)/shard_map/ppermute | solution.py:664
  120.9 21.4 %collective-permute-start.12 = (f32[8,16,256]{2,1,0:T(8,128)}, f32[8,16,256]{2,1,0:T(8,128)}, u32[]{:S(2)}, u32[]{:S(2)}) collective-permute-start(f32[8,16,256]{2,1,0:T(8,128)} %get-tuple-element.180), channel_id=1, source_target_pairs={{0,3},{1,2},{2,1},{3,0},{4,7},{5,6},{6,5},{7,4}} | collective-permute-start | bytes 393224 | tf_op jit(solution)/shard_map/ppermute | solution.py:664
  122.2 20.1 %collective-permute-start.11 = (f32[8,16,256]{2,1,0:T(8,128)}, f32[8,16,256]{2,1,0:T(8,128)}, u32[]{:S(2)}, u32[]{:S(2)}) collective-permute-start(f32[8,16,256]{2,1,0:T(8,128)} %get-tuple-element.181), channel_id=1, source_target_pairs={{0,2},{1,3},{2,0},{3,1},{4,6},{5,7},{6,4},{7,5}} | collective-permute-start | bytes 393224 | tf_op jit(solution)/shard_map/ppermute | solution.py:664
  122.6 21.4 %collective-permute-start.15 = (f32[8,16,256]{2,1,0:T(8,128)}, f32[8,16,256]{2,1,0:T(8,128)}, u32[]{:S(2)}, u32[]{:S(2)}) collective-permute-start(f32[8,16,256]{2,1,0:T(8,128)} %get-tuple-element.182), channel_id=1, source_target_pairs={{0,1},{1,0},{2,3},{3,2},{4,5},{5,4},{6,7},{7,6}} | collective-permute-start | bytes 393224 | tf_op jit(solution)/shard_map/ppermute | solution.py:664
  547.4 4.8 copy-start.3
  547.4 6.5 collective-permute-start.10
  547.4 10.1 collective-permute-start.9
  552.1 8.7 collective-permute-start.8
  552.2 11.5 collective-permute-start.7
  564.5 230.9 %all-to-all-start = ((f32[4,8,16,256]{3,2,1,0:T(8,128)}), f32[4,8,16,256]{3,2,1,0:T(8,128)}, u32[]{:S(2)}, u32[]{:S(2)}) async-start(f32[4,8,16,256]{3,2,1,0:T(8,128)} %get-tuple-element.107), calls=%async_computation.1 | async-start | bytes 1048576 | tf_op jit(solution)/shard_map/all_to_all | solution.py:715
  568.8 636.0 %all-reduce.4.cloned.1.call-start = ((), (), s32[]{:S(2)}) async-start(), calls=%async_computation.5 | async-start | bytes 34603008 | tf_op jit(solution)/shard_map/psum | solution.py:730
  1209.2 11.1 copy-start.1
Sparse Core Ops, SparseCore 0:
  9.8 164.8 all-gather.4
  176.5 155.0 all-gather.2
  547.5 229.9 reduce-scatter.1
  923.4 213.0 all-reduce.3
